TPU v7x, 128 devices: a whole 4x4x4 slice. The times are simulated.
128 devices in a mesh: gx: 4 (over y_hi, core), gy: 4 (over x), gz: 8 (over y_lo, z).
Axes of the slice: x: 4, y: 4 (y_hi: 2, y_lo: 2; y = y_hi * 2 + y_lo), z: 4, core: 2. Of those that a mesh axis runs over, the one named last changes fastest.
Arguments:
- features: float32 [64, 64, 256, 128], P('gx', 'gy', 'gz'), may hold values from -6 to 6
- scales: float32 [64, 64, 256], P('gx', 'gy', 'gz'), may hold values from 0.2 to 0.4
- thetas: float32 [2, 4, 128], replicated, may hold values from -1 to 1
- weights: float32 [2, 128, 128], replicated, may hold values from -0.5 to 0.5
Outputs:
- hidden: float32 [64, 64, 256, 128], P('gx', 'gy', 'gz')
All inputs are finite; a program needn't handle non-finite values.
Results may differ from a plain program's by a relative error of at most 0.00011.
Values sent between devices are 32-bit elements; how exact they have to be, the bound alone decides.
No kernel may reach another device: no remote copies, remote signals or barrier semaphores. Data moves between devices by JAX's collectives and lax.ppermute only.
A program may use at most 64 MiB of HBM per device.

v0:
```python
import functools

import jax
import jax.numpy as jnp
from jax import lax
from jax.experimental import pallas as pl
from jax.experimental.pallas import tpu as pltpu
from jax.sharding import PartitionSpec as P


AXES = ("gx", "gy", "gz")
NX, NY, NZ, C = 16, 16, 32, 128
PLANE = NY * NZ
ROWS = NX * PLANE
FACE = {"gx": PLANE, "gy": NX * NZ, "gz": NX * NY}
LINE = {"gy": NZ, "gz": NY}
CROSS = ("gx", 1)
LOCALS = (("gy", 0), ("gy", 1), ("gz", 1), ("gz", 0), ("gx", 0))
SCALES = 16

F32 = jnp.float32
VM = pl.BlockSpec(memory_space=pltpu.VMEM)
HBM = pl.BlockSpec(memory_space=pltpu.HBM)
MIB = 1024 * 1024


def arr(rows, cols=C, dtype=F32):
    return jax.ShapeDtypeStruct((rows, cols), dtype)


def locals_out(lines):
    return [arr(FACE[a] + lines * LINE.get(a, 0)) for a, _ in LOCALS]


def swap(x, axis, kind):
    n = lax.axis_size(axis)
    pairs = []
    for i in range(kind, n + kind, 2):
        a, b = i % n, (i + 1) % n
        pairs += [(a, b), (b, a)]
    return lax.ppermute(x, axis, pairs)


def exchange(sends, cross=None, late=None):
    first = [] if cross is None else [swap(cross, *CROSS)]
    got = [swap(s, a, k) for s, (a, k) in zip(sends, LOCALS)]
    last = [] if late is None else [swap(late, *CROSS)]
    return first, got, last


def side(axis, kind):
    odd = lax.rem(lax.axis_index(axis), 2)
    return odd if kind else 1 - odd


def face_slices(axis, kind):
    up = side(axis, kind)
    if axis == "gx":
        base = up * ((NX - 1) * PLANE)
        return lambda i: (pl.ds(pl.multiple_of(base + i * NZ, NZ), NZ), pl.ds(pl.multiple_of(i * NZ, NZ), NZ))
    if axis == "gy":
        base = up * ((NY - 1) * NZ)
        return lambda i: (pl.ds(pl.multiple_of(base + i * PLANE, NZ), NZ), pl.ds(pl.multiple_of(i * NZ, NZ), NZ))
    base = up * (NZ - 1)
    return lambda i: (pl.ds(base + i * PLANE, NY, stride=NZ), pl.ds(pl.multiple_of(i * NY, NY), NY))


def plane_line(axis, kind):
    up = side(axis, kind)
    if axis == "gy":
        return pl.ds(pl.multiple_of(up * ((NY - 1) * NZ), NZ), NZ)
    return pl.ds(up * (NZ - 1), NY, stride=NZ)


def line_rows(axis, i):
    return pl.ds(FACE[axis] + i * LINE[axis], LINE[axis])


def cross_base(depth):
    up = side(*CROSS)
    return pl.multiple_of(up * ((NX - depth) * PLANE) + (1 - up) * ((depth - 1) * PLANE), PLANE)


def loop(n, body, unroll=4):
    def step(i, c):
        body(i)
        return c

    lax.fori_loop(0, n, step, 0, unroll=unroll)


def copy_plane(src, base, dst):
    def body(i):
        at = pl.multiple_of(i * 64, 64)
        dst[pl.ds(at, 64), :] = src[pl.ds(pl.multiple_of(base + at, 64), 64), :]

    loop(PLANE // 64, body)


def emit_face(w, axis, kind, send):
    at = face_slices(axis, kind)

    def body(i):
        src, dst = at(i)
        send[dst, :] = w[src, :]

    loop(NX, body)


def emit_locals(w, sends, ghosts=()):
    for (axis, kind), send in zip(LOCALS, sends):
        emit_face(w, axis, kind, send)
        if axis != "gx":
            for i, g in enumerate(ghosts):
                send[line_rows(axis, i), :] = g[plane_line(axis, kind), :]


def fix_faces(half, w, a2, halos, cross):
    for (axis, kind), halo in list(zip(LOCALS, halos))[::-1] + [(CROSS, cross)]:
        at = face_slices(axis, kind)

        def body(i, at=at, halo=halo):
            dst, src = at(i)
            r = a2[dst, :] * halo[src, :]
            w[dst, :] = w[dst, :] + (0.5 * r if half else r)

        loop(NX, body)


def fix_lines(half, g, a2, halos, i):
    for (axis, kind), halo in zip(LOCALS, halos):
        if axis == "gx":
            continue
        at = plane_line(axis, kind)
        r = a2[at, :] * halo[line_rows(axis, i), :]
        g[at, :] = g[at, :] + (0.5 * r if half else r)


def yz_sums(w, base, emit):
    sub = lax.broadcasted_iota(jnp.int32, (8, C), 0)
    top, bottom = sub == 0, sub == 7
    nv = NZ // 8

    def at(y):
        return [w[pl.ds(pl.multiple_of(base + y * NZ + 8 * k, 8), 8), :] for k in range(nv)]

    below, here = None, at(0)
    for y in range(NY):
        above = at(y + 1) if y + 1 < NY else None
        dn = [pltpu.roll(v, 1, 0) for v in here]
        up = [pltpu.roll(v, 7, 0) for v in here]
        for k in range(nv):
            n = jnp.where(top, dn[k - 1] if k else 0.0, dn[k]) + jnp.where(
                bottom, up[k + 1] if k + 1 < nv else 0.0, up[k]
            )
            for other in (below, above):
                if other is not None:
                    n = n + other[k]
            emit(y * NZ + 8 * k, n)
        below, here = here, above


def rows8(base, r):
    return pl.ds(pl.multiple_of(base + r, 8), 8)


def local_pass(half, w, a2, prior, out):
    def plane(base, lo, hi):
        def emit(r, n):
            if lo:
                n = n + w[rows8(base, r - PLANE), :]
            if hi:
                n = n + w[rows8(base, r + PLANE), :]
            v = a2[rows8(base, r), :] * n
            out[rows8(base, r), :] = 0.5 * v if half else v - prior[rows8(base, r), :]

        yz_sums(w, base, emit)

    plane(0, False, True)
    lax.fori_loop(1, NX - 1, lambda i, c: (plane(pl.multiple_of(i * PLANE, PLANE), True, True), c)[1], 0)
    plane((NX - 1) * PLANE, True, False)


def ghost_pass(half, g, inner, inner_base, a2, prior, out):
    def emit(r, n):
        v = a2[rows8(0, r), :] * (n + inner[rows8(inner_base, r), :])
        out[rows8(0, r), :] = 0.5 * v if half else v - prior[rows8(0, r), :]

    yz_sums(g, 0, emit)


def ghost_add(half, g, a2, outer, out):
    def body(i):
        rows = pl.ds(pl.multiple_of(i * 64, 64), 64)
        r = a2[rows, :] * outer[rows, :]
        out[rows, :] = g[rows, :] + (0.5 * r if half else r)

    loop(PLANE // 64, body)


def spread(tile, emit):
    st = jnp.transpose(tile, (1, 0))
    for j in range(NY):
        emit(j, jnp.broadcast_to(st[:NZ, j : j + 1], (NZ, C)))


def start_kernel(feat, scales, w0, sb, d1, d2, d3, *rest):
    sends, (buf, sems) = rest[:5], rest[5:]

    def copy(i):
        rows = pl.ds(pl.multiple_of(i * PLANE, PLANE), PLANE)
        return pltpu.make_async_copy(feat.at[rows, :], buf.at[rows, :], sems.at[i])

    for i in range(NX):
        copy(i).start()
    for i in range(NX):
        copy(i).wait()

        def emit(j, b, i=i):
            rows = pl.ds(i * PLANE + j * NZ, NZ)
            sb[rows, :] = b
            w0[rows, :] = b * buf[rows, :]

        spread(scales[i], emit)
    up = side(*CROSS)
    for depth, d in ((1, d1), (2, d2), (3, d3)):
        copy_plane(w0, cross_base(depth), d)
        if depth < 3:
            d[PLANE:, :] = jnp.zeros((SCALES, C), F32)
            d[PLANE:, :NZ] = scales[up * (NX - depth) + (1 - up) * (depth - 1)]
    emit_locals(w0, sends)


def aux_kernel(sb, weights, a2, rs, w4):
    def body(i):
        rows = pl.ds(pl.multiple_of(i * 64, 64), 64)
        s = sb[rows, :]
        a2[rows, :] = -2.0 * (s * s)
        rs[rows, :] = 1.0 / s

    loop(ROWS // 64, body, 2)
    for layer in range(2):
        w = weights[layer]
        hi = w.astype(jnp.bfloat16)
        lo = (w - hi.astype(F32)).astype(jnp.bfloat16)
        both = jnp.concatenate([hi, lo], axis=1)
        w4[layer, :C, :] = both
        w4[layer, C:, :] = both


def ghost_aux_kernel(d, a2g):
    def emit(j, b):
        a2g[pl.ds(j * NZ, NZ), :] = -2.0 * (b * b)

    spread(d[PLANE:, :], emit)


def local1_kernel(w0, a2, w1):
    local_pass(True, w0, a2, None, w1)


def local2_kernel(w1, a2, w0, d1, a2g1, w2, p1):
    local_pass(False, w1, a2, w0, w2)
    ghost_pass(True, d1, w0, cross_base(1), a2g1, None, p1)


def local3_kernel(w2, a2, w1, d1, d2, w1g1, a2g1, a2g2, w3, p2, q1):
    local_pass(False, w2, a2, w1, w3)
    ghost_pass(True, d2, d1, 0, a2g2, None, p2)
    ghost_pass(False, w1g1, w1, cross_base(1), a2g1, d1, q1)


def fix1_kernel(w_in, a2, d1, *rest):
    halos, w, sends = rest[:5], rest[5], rest[6:]
    fix_faces(True, w, a2, halos, d1)
    emit_locals(w, sends, (d1,))


def fix2_kernel(w_in, a2, d2, p1, a2g1, *rest):
    halos, w, w1g1, sends = rest[:5], rest[5], rest[6], rest[7:]
    ghost_add(True, p1, a2g1, d2, w1g1)
    fix_lines(True, w1g1, a2g1, halos, 0)
    fix_faces(False, w, a2, halos, w1g1)
    emit_locals(w, sends, (w1g1, d2))


def fix3(w, a2, d3, p2, q1, a2g1, a2g2, halos, g2, g1):
    ghost_add(True, p2, a2g2, d3, g2)
    fix_lines(True, g2, a2g2, halos, 1)
    ghost_add(False, q1, a2g1, g2, g1)
    fix_lines(False, g1, a2g1, halos, 0)
    fix_faces(False, w, a2, halos, g1)


def mixed(layer, ws, rs, thetas, w4, rows):
    t = None
    for k, w in enumerate(ws):
        term = thetas[layer, k : k + 1, :] * w[rows, :]
        t = term if t is None else t + term
    hi = t.astype(jnp.bfloat16)
    lo = (t - hi.astype(F32)).astype(jnp.bfloat16)
    both = jnp.dot(jnp.concatenate([hi, lo], axis=1), w4[layer], preferred_element_type=F32)
    v = (both[:, :C] + both[:, C:]) * rs[rows, :]
    return v / (1.0 + jnp.exp(-v))


def face_mix_kernel(layer, w3_in, a2, d3, p2, q1, a2g1, a2g2, w0, w1, w2, sb, rs, thetas, w4, *rest):
    halos, w3, d1, sends, (g2, g1, ft) = rest[:5], rest[5], rest[6], rest[7:12], rest[12:]
    fix3(w3, a2, d3, p2, q1, a2g1, a2g2, halos, g2, g1)
    ws = (w0, w1, w2, w3)
    for (axis, kind), send in [(CROSS, d1)] + list(zip(LOCALS, sends)):
        at = face_slices(axis, kind)
        size = FACE[axis]
        if axis == "gx":
            base = side(axis, kind) * ((NX - 1) * PLANE)

            def body(i, base=base, send=send):
                rows = pl.ds(pl.multiple_of(base + i * 256, 256), 256)
                send[pl.ds(pl.multiple_of(i * 256, 256), 256), :] = sb[rows, :] * mixed(
                    layer, ws, rs, thetas, w4, rows
                )

            loop(size // 256, body, True)
            continue

        def gather(i, at=at):
            src, dst = at(i)
            for k, w in enumerate(ws + (rs, sb)):
                ft[k, dst, :] = w[src, :]

        loop(NX, gather)

        def body(i, send=send):
            rows = pl.ds(pl.multiple_of(i * 256, 256), 256)
            send[rows, :] = ft[5, rows, :] * mixed(
                layer, tuple(ft.at[k] for k in range(4)), ft.at[4], thetas, w4, rows
            )

        loop(size // 256, body, True)


def mix_kernel(layer, w0, w1, w2, w3, sb, rs, thetas, w4, out, d2, d3):
    def body(i):
        rows = pl.ds(pl.multiple_of(i * 256, 256), 256)
        out[rows, :] = sb[rows, :] * mixed(layer, (w0, w1, w2, w3), rs, thetas, w4, rows)

    loop(ROWS // 256, body, 2)
    copy_plane(out, cross_base(2), d2)
    copy_plane(out, cross_base(3), d3)


def last_kernel(layer, w3_in, a2, d3, p2, q1, a2g1, a2g2, w0, w1, w2, rs, thetas, w4, *rest):
    halos, (w3, out), (g2, g1, buf, sems) = rest[:5], rest[5:7], rest[7:]
    fix3(w3, a2, d3, p2, q1, a2g1, a2g2, halos, g2, g1)

    def copy(i):
        rows = pl.ds(pl.multiple_of(i * PLANE, PLANE), PLANE)
        return pltpu.make_async_copy(buf.at[rows, :], out.at[rows, :], sems.at[i])

    def body(i):
        for h in range(2):
            rows = pl.ds(pl.multiple_of(i * PLANE + h * 256, 256), 256)
            buf[rows, :] = mixed(layer, (w0, w1, w2, w3), rs, thetas, w4, rows)
        copy(i).start()

    loop(NX, body, 1)
    loop(NX, lambda i: copy(i).wait(), 1)


def call(kernel, out_shape, args, in_hbm=(), out_hbm=(), scratch=(), aliases=None, mib=1):
    return pl.pallas_call(
        kernel,
        out_shape=out_shape,
        in_specs=[HBM if i in in_hbm else VM for i in range(len(args))],
        out_specs=[HBM if i in out_hbm else VM for i in range(len(out_shape))],
        scratch_shapes=list(scratch),
        input_output_aliases=aliases or {},
        compiler_params=pltpu.CompilerParams(vmem_limit_bytes=mib * MIB),
    )(*args)


def per_device(features, scales, thetas, weights):
    shape = features.shape
    feat = pltpu.with_memory_space_constraint(features.reshape(ROWS, C), pltpu.HBM)
    block, plane = arr(ROWS), arr(PLANE)
    dma = [pltpu.VMEM((ROWS, C), F32), pltpu.SemaphoreType.DMA((NX,))]
    ghosts = [pltpu.VMEM((PLANE, C), F32)] * 2
    w0, sb, s1, s2, s3, *sends = call(
        start_kernel,
        [block, block, arr(PLANE + SCALES), arr(PLANE + SCALES), plane] + locals_out(0),
        (feat, scales),
        in_hbm=(0,),
        scratch=dma,
        mib=6,
    )
    for layer in range(2):
        last = layer == 1
        if last:
            w0, s2, s3 = call(
                functools.partial(mix_kernel, 0), [block, plane, plane], (w0, w1, w2, w3, sb, rs, thetas, w4)
            )
        (d1,), halos, (d2,) = exchange(sends, cross=s1, late=s2)
        if not last:
            a2, rs, w4 = call(
                aux_kernel, [block, block, jax.ShapeDtypeStruct((2, 2 * C, 2 * C), jnp.bfloat16)], (sb, weights)
            )
        (w1,) = call(local1_kernel, [block], (w0, a2))
        w1, *sends = call(fix1_kernel, [block] + locals_out(1), (w1, a2, d1, *halos), aliases={0: 0})
        _, halos, (d3,) = exchange(sends, late=s3)
        if not last:
            (a2g1,) = call(ghost_aux_kernel, [plane], (d1,))
        w2, p1 = call(local2_kernel, [block, plane], (w1, a2, w0, d1, a2g1))
        w2, w1g1, *sends = call(
            fix2_kernel, [block, plane] + locals_out(2), (w2, a2, d2, p1, a2g1, *halos), aliases={0: 0}
        )
        _, halos, _ = exchange(sends)
        if not last:
            (a2g2,) = call(ghost_aux_kernel, [plane], (d2,))
        w3, p2, q1 = call(local3_kernel, [block, plane, plane], (w2, a2, w1, d1, d2, w1g1, a2g1, a2g2))
        tail = (w3, a2, d3, p2, q1, a2g1, a2g2, w0, w1, w2)
        if not last:
            w3, s1, *sends = call(
                functools.partial(face_mix_kernel, layer),
                [block, plane] + locals_out(0),
                (*tail, sb, rs, thetas, w4, *halos),
                scratch=ghosts + [pltpu.VMEM((6, PLANE, C), F32)],
                mib=6,
                aliases={0: 0},
            )
        else:
            _, out = call(
                functools.partial(last_kernel, layer),
                [block, block],
                (*tail, rs, thetas, w4, *halos),
                out_hbm=(1,),
                scratch=ghosts + dma,
                mib=8,
                aliases={0: 0},
            )
    return out.reshape(shape)


def solution(mesh):
    return jax.shard_map(
        per_device,
        mesh=mesh,
        in_specs=(P(*AXES, None), P(*AXES), P(), P()),
        out_specs=P(*AXES, None),
        check_vma=False,
    )
```

profile of v0, /device:TPU:1, one launch (start us, length us, event | category | flops | bytes accessed | tf_op | source)
XLA Modules:
  0.0 108.9 jit_solution(760657699136532761)
XLA Ops:
  0.0 0.9 copy-done.3
  0.9 5.5 %shard_map.46 = (f32[8192,128]{1,0:T(8,128)S(1)}, f32[8192,128]{1,0:T(8,128)S(1)}, f32[528,128]{1,0:T(8,128)S(1)}, f32[528,128]{1,0:T(8,128)S(1)}, f32[512,128]{...) custom-call(f32[8192,128]{1,0:T(8,128)} %bitcast.2, ...), custom_call_target="tpu_custom_call" | custom-call | tf_op jit(solution)/shard_map/pallas_call | solution.py:371
  6.5 5.7 %collective-permute-start.3 = (f32[256,128]{1,0:T(8,128)S(1)}, f32[256,128]{1,0:T(8,128)S(1)}, u32[]{:S(2)}, u32[]{:S(2)}) collective-permute-start(f32[256,128]{1,0:T(8,128)S(1)} %get-tuple-element.71), channel_id=1, source_target_pairs={{1,2},{2,1},{3,4},{4,3},{5,6},{6,5},{7,0},{0,7},{9,10},{10,9},{11,... | collective-permute-start | bytes 393224 | tf_op jit(solution)/shard_map/ppermute | solution.py:41
  12.1 3.5 %collective-permute-start = (f32[528,128]{1,0:T(8,128)S(1)}, f32[528,128]{1,0:T(8,128)S(1)}, u32[]{:S(2)}, u32[]{:S(2)}) collective-permute-start(f32[528,128]{1,0:T(8,128)S(1)} %get-tuple-element.68), channel_id=1, source_target_pairs={{32,64},{64,32},{96,0},{0,96},{33,65},{65,33},{97,1},{1,97},{34,66... | collective-permute-start | bytes 811016 | tf_op jit(solution)/shard_map/ppermute | solution.py:41
  15.6 1.2 %collective-permute-start.1 = (f32[512,128]{1,0:T(8,128)S(1)}, f32[512,128]{1,0:T(8,128)S(1)}, u32[]{:S(2)}, u32[]{:S(2)}) collective-permute-start(f32[512,128]{1,0:T(8,128)S(1)} %get-tuple-element.69), channel_id=1, source_target_pairs={{0,8},{8,0},{16,24},{24,16},{1,9},{9,1},{17,25},{25,17},{2,10},{10... | collective-permute-start | bytes 786440 | tf_op jit(solution)/shard_map/ppermute | solution.py:41
  16.8 1.8 %collective-permute-start.2 = (f32[512,128]{1,0:T(8,128)S(1)}, f32[512,128]{1,0:T(8,128)S(1)}, u32[]{:S(2)}, u32[]{:S(2)}) collective-permute-start(f32[512,128]{1,0:T(8,128)S(1)} %get-tuple-element.70), channel_id=1, source_target_pairs={{8,16},{16,8},{24,0},{0,24},{9,17},{17,9},{25,1},{1,25},{10,18},{1... | collective-permute-start | bytes 786440 | tf_op jit(solution)/shard_map/ppermute | solution.py:41
  18.7 2.4 %collective-permute-done.4.rest_3_ = f32[256,128]{1,0:T(8,128)S(1)} collective-permute-done((f32[256,128]{1,0:T(8,128)S(1)}, f32[256,128]{1,0:T(8,128)S(1)}, u32[]{:S(2)}, u32[]{:S(2)}) %collective-permute-start.4) | collective-permute-done | bytes 131104 | tf_op jit(solution)/shard_map/ppermute | solution.py:41
  21.1 0.6 collective-permute-start.6
  21.7 1.0 shard_map.47
  22.8 1.5 %shard_map.48.w_in = f32[8192,128]{1,0:T(8,128)S(1)} custom-call(f32[8192,128]{1,0:T(8,128)S(1)} %get-tuple-element.65.w0, f32[8192,128]{1,0:T(8,128)S(1)} %get-tuple-element.67.a2), custom_call_target="tpu_custom_call" | custom-call | tf_op jit(solution)/shard_map/pallas_call | solution.py:371
  24.3 1.7 %collective-permute-done.2.rest_1_ = f32[512,128]{1,0:T(8,128)S(1)} collective-permute-done((f32[512,128]{1,0:T(8,128)S(1)}, f32[512,128]{1,0:T(8,128)S(1)}, u32[]{:S(2)}, u32[]{:S(2)}) %collective-permute-start.2) | collective-permute-done | bytes 262176 | tf_op jit(solution)/shard_map/ppermute | solution.py:41
  26.1 1.3 %shard_map.49 = (f32[8192,128]{1,0:T(8,128)S(1)}, f32[544,128]{1,0:T(8,128)S(1)}, f32[544,128]{1,0:T(8,128)S(1)}, f32[272,128]{1,0:T(8,128)S(1)}, f32[272,128]{1,0:T(8,128)S(1)}, /*index=5*/f32[512,128]{1,0:T(8,128)S(1)}) custom-call(f32[8192,128]{1,0:T(8,128)S(1)} %shard_map.48.w_in, ...), custom_call_target="tpu_custom_call", output_to_operand_aliasing={{0}: (0, {})} | custom-call | tf_op jit(solution)/shard_map/pallas_call | solution.py:371
  27.4 1.9 %collective-permute-start.8 = (f32[544,128]{1,0:T(8,128)S(1)}, f32[544,128]{1,0:T(8,128)S(1)}, u32[]{:S(2)}, u32[]{:S(2)}) collective-permute-start(f32[544,128]{1,0:T(8,128)S(1)} %get-tuple-element.79), channel_id=1, source_target_pairs={{8,16},{16,8},{24,0},{0,24},{9,17},{17,9},{25,1},{1,25},{10,18},{1... | collective-permute-start | bytes 835592 | tf_op jit(solution)/shard_map/ppermute | solution.py:41
  29.3 1.0 collective-permute-start.11
  30.3 1.0 collective-permute-start.9
  31.8 5.9 %collective-permute-done.9.rest_2_ = f32[272,128]{1,0:T(8,128)S(1)} collective-permute-done((f32[272,128]{1,0:T(8,128)S(1)}, f32[272,128]{1,0:T(8,128)S(1)}, u32[]{:S(2)}, u32[]{:S(2)}) %collective-permute-start.9) | collective-permute-done | bytes 139296 | tf_op jit(solution)/shard_map/ppermute | solution.py:41
  37.6 2.5 %collective-permute-start.12 = (f32[512,128]{1,0:T(8,128)S(1)}, f32[512,128]{1,0:T(8,128)S(1)}, u32[]{:S(2)}, u32[]{:S(2)}) collective-permute-start(f32[512,128]{1,0:T(8,128)S(1)} %get-tuple-element.86), channel_id=1, source_target_pairs={{32,64},{64,32},{96,0},{0,96},{33,65},{65,33},{97,1},{1,97},{34,66... | collective-permute-start | bytes 786440 | tf_op jit(solution)/shard_map/ppermute | solution.py:41
  40.4 1.6 %shard_map.51 = (f32[8192,128]{1,0:T(8,128)S(1)}, f32[512,128]{1,0:T(8,128)S(1)}) custom-call(f32[8192,128]{1,0:T(8,128)S(1)} %get-tuple-element.74.w1, f32[8192,128]{1,0:T(8,128)S(1)} %get-tuple-element.67.a2, f32[8192,128]{1,0:T(8,128)S(1)} %get-tuple-element.65.w0, f32[528,128]{1,0:T(8,128)S(1)} %collective-permute-done.d1.d, f32[512,128]{1,0:T(8,128)S(1)} %shard_map.50.a2g1), custom_call_target="tpu_custom_call" | custom-call | tf_op jit(solution)/shard_map/pallas_call | solution.py:371
  42.0 1.4 %shard_map.52 = (f32[8192,128]{1,0:T(8,128)S(1)}, f32[512,128]{1,0:T(8,128)S(1)}, f32[576,128]{1,0:T(8,128)S(1)}, f32[576,128]{1,0:T(8,128)S(1)}, f32[288,128]{1...) custom-call(f32[8192,128]{1,0:T(8,128)S(1)} %get-tuple-element.75.w_in, ...), custom_call_target="tpu_custom_call", output_to_operand_aliasing={{0}: (0, {})} | custom-call | tf_op jit(solution)/shard_map/pallas_call | solution.py:371
  43.8 0.6 collective-permute-start.14
  44.5 3.4 %collective-permute-done.12.d3 = f32[512,128]{1,0:T(8,128)S(1)} collective-permute-done((f32[512,128]{1,0:T(8,128)S(1)}, f32[512,128]{1,0:T(8,128)S(1)}, u32[]{:S(2)}, u32[]{:S(2)}) %collective-permute-start.12) | collective-permute-done | bytes 262176 | tf_op jit(solution)/shard_map/ppermute | solution.py:41
  48.1 1.7 %shard_map.54 = (f32[8192,128]{1,0:T(8,128)S(1)}, f32[512,128]{1,0:T(8,128)S(1)}, f32[512,128]{1,0:T(8,128)S(1)}) custom-call(f32[8192,128]{1,0:T(8,128)S(1)} %get-tuple-element.83.w2, f32[8192,128]{1,0:T(8,128)S(1)} %get-tuple-element.67.a2, f32[8192,128]{1,0:T(8,128)S(1)} %get-tuple-element.74.w1, f32[528,128]{1,0:T(8,128)S(1)} %collective-permute-done.d1.d, ...), custom_call_target="tpu_custom_call" | custom-call | tf_op jit(solution)/shard_map/pallas_call | solution.py:371
  49.8 1.6 %collective-permute-done.15.rest_2_ = f32[288,128]{1,0:T(8,128)S(1)} collective-permute-done((f32[288,128]{1,0:T(8,128)S(1)}, f32[288,128]{1,0:T(8,128)S(1)}, u32[]{:S(2)}, u32[]{:S(2)}) %collective-permute-start.15) | collective-permute-done | bytes 147488 | tf_op jit(solution)/shard_map/ppermute | solution.py:41
  51.5 1.2 %collective-permute-done.16.rest_3_ = f32[288,128]{1,0:T(8,128)S(1)} collective-permute-done((f32[288,128]{1,0:T(8,128)S(1)}, f32[288,128]{1,0:T(8,128)S(1)}, u32[]{:S(2)}, u32[]{:S(2)}) %collective-permute-start.16) | collective-permute-done | bytes 147488 | tf_op jit(solution)/shard_map/ppermute | solution.py:41
  52.7 1.0 collective-permute-done.14.rest_1_
  53.7 4.3 %shard_map.55 = (f32[8192,128]{1,0:T(8,128)S(1)}, f32[512,128]{1,0:T(8,128)S(1)}, f32[512,128]{1,0:T(8,128)S(1)}, f32[512,128]{1,0:T(8,128)S(1)}, f32[256,128]{1...) custom-call(f32[8192,128]{1,0:T(8,128)S(1)} %get-tuple-element.85.w3_in, ...), custom_call_target="tpu_custom_call", output_to_operand_aliasing={{0}: (0, {})} | custom-call | tf_op jit(solution)/shard_map/pallas_call | solution.py:371
  58.3 3.7 %collective-permute-start.18 = (f32[512,128]{1,0:T(8,128)S(1)}, f32[512,128]{1,0:T(8,128)S(1)}, u32[]{:S(2)}, u32[]{:S(2)}) collective-permute-start(f32[512,128]{1,0:T(8,128)S(1)} %get-tuple-element.98), channel_id=1, source_target_pairs={{32,64},{64,32},{96,0},{0,96},{33,65},{65,33},{97,1},{1,97},{34,66... | collective-permute-start | bytes 786440 | tf_op jit(solution)/shard_map/ppermute | solution.py:41
  62.0 1.3 %collective-permute-start.20 = (f32[512,128]{1,0:T(8,128)S(1)}, f32[512,128]{1,0:T(8,128)S(1)}, u32[]{:S(2)}, u32[]{:S(2)}) collective-permute-start(f32[512,128]{1,0:T(8,128)S(1)} %get-tuple-element.100), channel_id=1, source_target_pairs={{8,16},{16,8},{24,0},{0,24},{9,17},{17,9},{25,1},{1,25},{10,18},{1... | collective-permute-start | bytes 786440 | tf_op jit(solution)/shard_map/ppermute | solution.py:41
  63.3 1.3 %collective-permute-done.21.rest_2_ = f32[256,128]{1,0:T(8,128)S(1)} collective-permute-done((f32[256,128]{1,0:T(8,128)S(1)}, f32[256,128]{1,0:T(8,128)S(1)}, u32[]{:S(2)}, u32[]{:S(2)}) %collective-permute-start.21) | collective-permute-done | bytes 131104 | tf_op jit(solution)/shard_map/ppermute | solution.py:41
  64.6 2.2 %copy-done.1 = f32[8192,128]{1,0:T(8,128)S(1)} copy-done((f32[8192,128]{1,0:T(8,128)S(1)}, f32[8192,128]{1,0:T(8,128)}, u32[]{:S(2)}) %copy-start.1) | copy-done | bytes 4194328
  66.8 4.4 %shard_map.56 = (f32[8192,128]{1,0:T(8,128)S(1)}, f32[512,128]{1,0:T(8,128)S(1)}, f32[512,128]{1,0:T(8,128)S(1)}) custom-call(f32[8192,128]{1,0:T(8,128)S(1)} %get-tuple-element.65.w0, f32[8192,128]{1,0:T(8,128)S(1)} %get-tuple-element.74.w1, f32[8192,128]{1,0:T(8,128)S(1)} %get-tuple-element.83.w2, f32[8192,128]{1,0:T(8,128)S(1)} %get-tuple-element.96.w3, ...), custom_call_target="tpu_custom_call" | custom-call | tf_op jit(solution)/shard_map/pallas_call | solution.py:371
  71.2 3.8 %collective-permute-start.24 = (f32[512,128]{1,0:T(8,128)S(1)}, f32[512,128]{1,0:T(8,128)S(1)}, u32[]{:S(2)}, u32[]{:S(2)}) collective-permute-start(f32[512,128]{1,0:T(8,128)S(1)} %get-tuple-element.106), channel_id=1, source_target_pairs={{32,64},{64,32},{96,0},{0,96},{33,65},{65,33},{97,1},{1,97},{34,66... | collective-permute-start | bytes 786440 | tf_op jit(solution)/shard_map/ppermute | solution.py:41
  75.0 1.5 %shard_map.57.w_in = f32[8192,128]{1,0:T(8,128)S(1)} custom-call(f32[8192,128]{1,0:T(8,128)S(1)} %get-tuple-element.97.w0, f32[8192,128]{1,0:T(8,128)S(1)} %get-tuple-element.67.a2), custom_call_target="tpu_custom_call" | custom-call | tf_op jit(solution)/shard_map/pallas_call | solution.py:371
  76.5 1.3 %shard_map.58 = (f32[8192,128]{1,0:T(8,128)S(1)}, f32[544,128]{1,0:T(8,128)S(1)}, f32[544,128]{1,0:T(8,128)S(1)}, f32[272,128]{1,0:T(8,128)S(1)}, f32[272,128]{1,0:T(8,128)S(1)}, /*index=5*/f32[512,128]{1,0:T(8,128)S(1)}) custom-call(f32[8192,128]{1,0:T(8,128)S(1)} %shard_map.57.w_in, ...), custom_call_target="tpu_custom_call", output_to_operand_aliasing={{0}: (0, {})} | custom-call | tf_op jit(solution)/shard_map/pallas_call | solution.py:371
  77.9 1.1 %collective-permute-start.26 = (f32[544,128]{1,0:T(8,128)S(1)}, f32[544,128]{1,0:T(8,128)S(1)}, u32[]{:S(2)}, u32[]{:S(2)}) collective-permute-start(f32[544,128]{1,0:T(8,128)S(1)} %get-tuple-element.109), channel_id=1, source_target_pairs={{8,16},{16,8},{24,0},{0,24},{9,17},{17,9},{25,1},{1,25},{10,18},{1... | collective-permute-start | bytes 835592 | tf_op jit(solution)/shard_map/ppermute | solution.py:41
  79.3 0.6 collective-permute-start.27
  79.8 1.3 %collective-permute-done.24.d2 = f32[512,128]{1,0:T(8,128)S(1)} collective-permute-done((f32[512,128]{1,0:T(8,128)S(1)}, f32[512,128]{1,0:T(8,128)S(1)}, u32[]{:S(2)}, u32[]{:S(2)}) %collective-permute-start.24) | collective-permute-done | bytes 262176 | tf_op jit(solution)/shard_map/ppermute | solution.py:41
  81.1 1.7 %collective-permute-start.28 = (f32[272,128]{1,0:T(8,128)S(1)}, f32[272,128]{1,0:T(8,128)S(1)}, u32[]{:S(2)}, u32[]{:S(2)}) collective-permute-start(f32[272,128]{1,0:T(8,128)S(1)} %get-tuple-element.111), channel_id=1, source_target_pairs={{0,1},{1,0},{2,3},{3,2},{4,5},{5,4},{6,7},{7,6},{8,9},{9,8},{10,11... | collective-permute-start | bytes 417800 | tf_op jit(solution)/shard_map/ppermute | solution.py:41
  82.9 3.5 %collective-permute-done.27.rest_2_ = f32[272,128]{1,0:T(8,128)S(1)} collective-permute-done((f32[272,128]{1,0:T(8,128)S(1)}, f32[272,128]{1,0:T(8,128)S(1)}, u32[]{:S(2)}, u32[]{:S(2)}) %collective-permute-start.27) | collective-permute-done | bytes 139296 | tf_op jit(solution)/shard_map/ppermute | solution.py:41
  86.3 3.3 %collective-permute-start.30 = (f32[512,128]{1,0:T(8,128)S(1)}, f32[512,128]{1,0:T(8,128)S(1)}, u32[]{:S(2)}, u32[]{:S(2)}) collective-permute-start(f32[512,128]{1,0:T(8,128)S(1)} %get-tuple-element.116), channel_id=1, source_target_pairs={{32,64},{64,32},{96,0},{0,96},{33,65},{65,33},{97,1},{1,97},{34,66... | collective-permute-start | bytes 786440 | tf_op jit(solution)/shard_map/ppermute | solution.py:41
  89.6 1.6 %shard_map.59 = (f32[8192,128]{1,0:T(8,128)S(1)}, f32[512,128]{1,0:T(8,128)S(1)}) custom-call(f32[8192,128]{1,0:T(8,128)S(1)} %get-tuple-element.104.w1, f32[8192,128]{1,0:T(8,128)S(1)} %get-tuple-element.67.a2, f32[8192,128]{1,0:T(8,128)S(1)} %get-tuple-element.97.w0, f32[512,128]{1,0:T(8,128)S(1)} %collective-permute-done.18.d1, f32[512,128]{1,0:T(8,128)S(1)} %shard_map.50.a2g1), custom_call_target="tpu_custom_call" | custom-call | tf_op jit(solution)/shard_map/pallas_call | solution.py:371
  91.3 1.4 %shard_map.60 = (f32[8192,128]{1,0:T(8,128)S(1)}, f32[512,128]{1,0:T(8,128)S(1)}, f32[576,128]{1,0:T(8,128)S(1)}, f32[576,128]{1,0:T(8,128)S(1)}, f32[288,128]{1...) custom-call(f32[8192,128]{1,0:T(8,128)S(1)} %get-tuple-element.105.w_in, ...), custom_call_target="tpu_custom_call", output_to_operand_aliasing={{0}: (0, {})} | custom-call | tf_op jit(solution)/shard_map/pallas_call | solution.py:371
  92.8 1.8 %collective-permute-start.32 = (f32[576,128]{1,0:T(8,128)S(1)}, f32[576,128]{1,0:T(8,128)S(1)}, u32[]{:S(2)}, u32[]{:S(2)}) collective-permute-start(f32[576,128]{1,0:T(8,128)S(1)} %get-tuple-element.120), channel_id=1, source_target_pairs={{8,16},{16,8},{24,0},{0,24},{9,17},{17,9},{25,1},{1,25},{10,18},{1... | collective-permute-start | bytes 884744 | tf_op jit(solution)/shard_map/ppermute | solution.py:41
  94.6 1.8 %collective-permute-done.30.d3 = f32[512,128]{1,0:T(8,128)S(1)} collective-permute-done((f32[512,128]{1,0:T(8,128)S(1)}, f32[512,128]{1,0:T(8,128)S(1)}, u32[]{:S(2)}, u32[]{:S(2)}) %collective-permute-start.30) | collective-permute-done | bytes 262176 | tf_op jit(solution)/shard_map/ppermute | solution.py:41
  96.4 2.1 %shard_map.61 = (f32[8192,128]{1,0:T(8,128)S(1)}, f32[512,128]{1,0:T(8,128)S(1)}, f32[512,128]{1,0:T(8,128)S(1)}) custom-call(f32[8192,128]{1,0:T(8,128)S(1)} %get-tuple-element.113.w2, f32[8192,128]{1,0:T(8,128)S(1)} %get-tuple-element.67.a2, f32[8192,128]{1,0:T(8,128)S(1)} %get-tuple-element.104.w1, f32[512,128]{1,0:T(8,128)S(1)} %collective-permute-done.18.d1, ...), custom_call_target="tpu_custom_call" | custom-call | tf_op jit(solution)/shard_map/pallas_call | solution.py:371
  98.5 3.1 %collective-permute-done.33.rest_2_ = f32[288,128]{1,0:T(8,128)S(1)} collective-permute-done((f32[288,128]{1,0:T(8,128)S(1)}, f32[288,128]{1,0:T(8,128)S(1)}, u32[]{:S(2)}, u32[]{:S(2)}) %collective-permute-start.33) | collective-permute-done | bytes 147488 | tf_op jit(solution)/shard_map/ppermute | solution.py:41
  101.6 1.0 collective-permute-done.32.rest_1_
  102.5 6.2 %shard_map.62 = (f32[8192,128]{1,0:T(8,128)S(1)}, f32[8192,128]{1,0:T(8,128)}) custom-call(f32[8192,128]{1,0:T(8,128)S(1)} %get-tuple-element.115.w3_in, f32[8192,128]{1,0:T(8,128)S(1)} %get-tuple-element.67.a2, f32[512,128]{1,0:T(8,128)S(1)} %collective-permute-done.30.d3, f32[512,128]{1,0:T(8,128)S(1)} %get-tuple-element.117.p2, ...), custom_call_target="tpu_custom_call", output_to_operand_aliasing={{0}: (0, {})} | custom-call | tf_op jit(solution)/shard_map/pallas_call | solution.py:371
  (53 shorter events, 2.4 us)
Async XLA Ops:
  0.0 0.9 copy-start.3
  0.9 20.8 %copy-start.4 = (f32[2,128,128]{2,1,0:T(8,128)S(1)}, f32[2,128,128]{2,1,0:T(8,128)}, u32[]{:S(2)}) copy-start(f32[2,128,128]{2,1,0:T(8,128)} %weights.1) | copy-start | bytes 393220
  6.5 12.2 %collective-permute-start.3 = (f32[256,128]{1,0:T(8,128)S(1)}, f32[256,128]{1,0:T(8,128)S(1)}, u32[]{:S(2)}, u32[]{:S(2)}) collective-permute-start(f32[256,128]{1,0:T(8,128)S(1)} %get-tuple-element.71), channel_id=1, source_target_pairs={{1,2},{2,1},{3,4},{4,3},{5,6},{6,5},{7,0},{0,7},{9,10},{10,9},{11,... | collective-permute-start | bytes 393224 | tf_op jit(solution)/shard_map/ppermute | solution.py:41
  12.1 13.9 %collective-permute-start = (f32[528,128]{1,0:T(8,128)S(1)}, f32[528,128]{1,0:T(8,128)S(1)}, u32[]{:S(2)}, u32[]{:S(2)}) collective-permute-start(f32[528,128]{1,0:T(8,128)S(1)} %get-tuple-element.68), channel_id=1, source_target_pairs={{32,64},{64,32},{96,0},{0,96},{33,65},{65,33},{97,1},{1,97},{34,66... | collective-permute-start | bytes 811016 | tf_op jit(solution)/shard_map/ppermute | solution.py:41
  15.6 5.5 %collective-permute-start.4 = (f32[256,128]{1,0:T(8,128)S(1)}, f32[256,128]{1,0:T(8,128)S(1)}, u32[]{:S(2)}, u32[]{:S(2)}) collective-permute-start(f32[256,128]{1,0:T(8,128)S(1)} %get-tuple-element.72), channel_id=1, source_target_pairs={{0,1},{1,0},{2,3},{3,2},{4,5},{5,4},{6,7},{7,6},{8,9},{9,8},{10,11... | collective-permute-start | bytes 393224 | tf_op jit(solution)/shard_map/ppermute | solution.py:41
  15.6 8.7 %collective-permute-start.1 = (f32[512,128]{1,0:T(8,128)S(1)}, f32[512,128]{1,0:T(8,128)S(1)}, u32[]{:S(2)}, u32[]{:S(2)}) collective-permute-start(f32[512,128]{1,0:T(8,128)S(1)} %get-tuple-element.69), channel_id=1, source_target_pairs={{0,8},{8,0},{16,24},{24,16},{1,9},{9,1},{17,25},{25,17},{2,10},{10... | collective-permute-start | bytes 786440 | tf_op jit(solution)/shard_map/ppermute | solution.py:41
  16.8 9.2 %collective-permute-start.2 = (f32[512,128]{1,0:T(8,128)S(1)}, f32[512,128]{1,0:T(8,128)S(1)}, u32[]{:S(2)}, u32[]{:S(2)}) collective-permute-start(f32[512,128]{1,0:T(8,128)S(1)} %get-tuple-element.70), channel_id=1, source_target_pairs={{8,16},{16,8},{24,0},{0,24},{9,17},{17,9},{25,1},{1,25},{10,18},{1... | collective-permute-start | bytes 786440 | tf_op jit(solution)/shard_map/ppermute | solution.py:41
  18.6 7.4 %collective-permute-start.5 = (f32[512,128]{1,0:T(8,128)S(1)}, f32[512,128]{1,0:T(8,128)S(1)}, u32[]{:S(2)}, u32[]{:S(2)}) collective-permute-start(f32[512,128]{1,0:T(8,128)S(1)} %get-tuple-element.73), channel_id=1, source_target_pairs={{0,32},{32,0},{64,96},{96,64},{1,33},{33,1},{65,97},{97,65},{2,34}... | collective-permute-start | bytes 786440 | tf_op jit(solution)/shard_map/ppermute | solution.py:41
  21.1 10.2 %collective-permute-start.6 = (f32[528,128]{1,0:T(8,128)S(1)}, f32[528,128]{1,0:T(8,128)S(1)}, u32[]{:S(2)}, u32[]{:S(2)}) collective-permute-start(f32[528,128]{1,0:T(8,128)S(1)} %get-tuple-element.76), channel_id=1, source_target_pairs={{32,64},{64,32},{96,0},{0,96},{33,65},{65,33},{97,1},{1,97},{34,66... | collective-permute-start | bytes 811016 | tf_op jit(solution)/shard_map/ppermute | solution.py:41
  22.8 30.9 %copy-start = (f32[8192,128]{1,0:T(8,128)}, f32[8192,128]{1,0:T(8,128)S(1)}, u32[]{:S(2)}) copy-start(f32[8192,128]{1,0:T(8,128)S(1)} %get-tuple-element.89.rs) | copy-start | bytes 12582916
  27.3 14.7 %collective-permute-start.7 = (f32[544,128]{1,0:T(8,128)S(1)}, f32[544,128]{1,0:T(8,128)S(1)}, u32[]{:S(2)}, u32[]{:S(2)}) collective-permute-start(f32[544,128]{1,0:T(8,128)S(1)} %get-tuple-element.78), channel_id=1, source_target_pairs={{0,8},{8,0},{16,24},{24,16},{1,9},{9,1},{17,25},{25,17},{2,10},{10... | collective-permute-start | bytes 835592 | tf_op jit(solution)/shard_map/ppermute | solution.py:41
  27.4 14.6 %collective-permute-start.8 = (f32[544,128]{1,0:T(8,128)S(1)}, f32[544,128]{1,0:T(8,128)S(1)}, u32[]{:S(2)}, u32[]{:S(2)}) collective-permute-start(f32[544,128]{1,0:T(8,128)S(1)} %get-tuple-element.79), channel_id=1, source_target_pairs={{8,16},{16,8},{24,0},{0,24},{9,17},{17,9},{25,1},{1,25},{10,18},{1... | collective-permute-start | bytes 835592 | tf_op jit(solution)/shard_map/ppermute | solution.py:41
  29.3 12.7 %collective-permute-start.11 = (f32[512,128]{1,0:T(8,128)S(1)}, f32[512,128]{1,0:T(8,128)S(1)}, u32[]{:S(2)}, u32[]{:S(2)}) collective-permute-start(f32[512,128]{1,0:T(8,128)S(1)} %get-tuple-element.82), channel_id=1, source_target_pairs={{0,32},{32,0},{64,96},{96,64},{1,33},{33,1},{65,97},{97,65},{2,34}... | collective-permute-start | bytes 786440 | tf_op jit(solution)/shard_map/ppermute | solution.py:41
  30.3 7.3 %collective-permute-start.9 = (f32[272,128]{1,0:T(8,128)S(1)}, f32[272,128]{1,0:T(8,128)S(1)}, u32[]{:S(2)}, u32[]{:S(2)}) collective-permute-start(f32[272,128]{1,0:T(8,128)S(1)} %get-tuple-element.80), channel_id=1, source_target_pairs={{1,2},{2,1},{3,4},{4,3},{5,6},{6,5},{7,0},{0,7},{9,10},{10,9},{11,... | collective-permute-start | bytes 417800 | tf_op jit(solution)/shard_map/ppermute | solution.py:41
  31.3 10.7 %collective-permute-start.10 = (f32[272,128]{1,0:T(8,128)S(1)}, f32[272,128]{1,0:T(8,128)S(1)}, u32[]{:S(2)}, u32[]{:S(2)}) collective-permute-start(f32[272,128]{1,0:T(8,128)S(1)} %get-tuple-element.81), channel_id=1, source_target_pairs={{0,1},{1,0},{2,3},{3,2},{4,5},{5,4},{6,7},{7,6},{8,9},{9,8},{10,11... | collective-permute-start | bytes 417800 | tf_op jit(solution)/shard_map/ppermute | solution.py:41
  37.6 10.2 %collective-permute-start.12 = (f32[512,128]{1,0:T(8,128)S(1)}, f32[512,128]{1,0:T(8,128)S(1)}, u32[]{:S(2)}, u32[]{:S(2)}) collective-permute-start(f32[512,128]{1,0:T(8,128)S(1)} %get-tuple-element.86), channel_id=1, source_target_pairs={{32,64},{64,32},{96,0},{0,96},{33,65},{65,33},{97,1},{1,97},{34,66... | collective-permute-start | bytes 786440 | tf_op jit(solution)/shard_map/ppermute | solution.py:41
  43.4 9.3 %collective-permute-start.13 = (f32[576,128]{1,0:T(8,128)S(1)}, f32[576,128]{1,0:T(8,128)S(1)}, u32[]{:S(2)}, u32[]{:S(2)}) collective-permute-start(f32[576,128]{1,0:T(8,128)S(1)} %get-tuple-element.91), channel_id=1, source_target_pairs={{0,8},{8,0},{16,24},{24,16},{1,9},{9,1},{17,25},{25,17},{2,10},{10... | collective-permute-start | bytes 884744 | tf_op jit(solution)/shard_map/ppermute | solution.py:41
  43.8 9.8 %collective-permute-start.14 = (f32[576,128]{1,0:T(8,128)S(1)}, f32[576,128]{1,0:T(8,128)S(1)}, u32[]{:S(2)}, u32[]{:S(2)}) collective-permute-start(f32[576,128]{1,0:T(8,128)S(1)} %get-tuple-element.92), channel_id=1, source_target_pairs={{8,16},{16,8},{24,0},{0,24},{9,17},{17,9},{25,1},{1,25},{10,18},{1... | collective-permute-start | bytes 884744 | tf_op jit(solution)/shard_map/ppermute | solution.py:41
  44.5 8.2 %collective-permute-start.17 = (f32[512,128]{1,0:T(8,128)S(1)}, f32[512,128]{1,0:T(8,128)S(1)}, u32[]{:S(2)}, u32[]{:S(2)}) collective-permute-start(f32[512,128]{1,0:T(8,128)S(1)} %get-tuple-element.95), channel_id=1, source_target_pairs={{0,32},{32,0},{64,96},{96,64},{1,33},{33,1},{65,97},{97,65},{2,34}... | collective-permute-start | bytes 786440 | tf_op jit(solution)/shard_map/ppermute | solution.py:41
  44.5 7.0 %collective-permute-start.15 = (f32[288,128]{1,0:T(8,128)S(1)}, f32[288,128]{1,0:T(8,128)S(1)}, u32[]{:S(2)}, u32[]{:S(2)}) collective-permute-start(f32[288,128]{1,0:T(8,128)S(1)} %get-tuple-element.93), channel_id=1, source_target_pairs={{1,2},{2,1},{3,4},{4,3},{5,6},{6,5},{7,0},{0,7},{9,10},{10,9},{11,... | collective-permute-start | bytes 442376 | tf_op jit(solution)/shard_map/ppermute | solution.py:41
  47.9 4.8 %collective-permute-start.16 = (f32[288,128]{1,0:T(8,128)S(1)}, f32[288,128]{1,0:T(8,128)S(1)}, u32[]{:S(2)}, u32[]{:S(2)}) collective-permute-start(f32[288,128]{1,0:T(8,128)S(1)} %get-tuple-element.94), channel_id=1, source_target_pairs={{0,1},{1,0},{2,3},{3,2},{4,5},{5,4},{6,7},{7,6},{8,9},{9,8},{10,11... | collective-permute-start | bytes 442376 | tf_op jit(solution)/shard_map/ppermute | solution.py:41
  48.1 5.6 %copy-start.5 = (f32[2,4,128]{2,1,0:T(4,128)S(1)}, f32[2,4,128]{2,1,0:T(4,128)}, u32[]{:S(2)}) copy-start(f32[2,4,128]{2,1,0:T(4,128)} %thetas.5) | copy-start | bytes 12292
  58.0 6.6 %collective-permute-start.21 = (f32[256,128]{1,0:T(8,128)S(1)}, f32[256,128]{1,0:T(8,128)S(1)}, u32[]{:S(2)}, u32[]{:S(2)}) collective-permute-start(f32[256,128]{1,0:T(8,128)S(1)} %get-tuple-element.101), channel_id=1, source_target_pairs={{1,2},{2,1},{3,4},{4,3},{5,6},{6,5},{7,0},{0,7},{9,10},{10,9},{11,... | collective-permute-start | bytes 393224 | tf_op jit(solution)/shard_map/ppermute | solution.py:41
  58.3 18.2 %collective-permute-start.18 = (f32[512,128]{1,0:T(8,128)S(1)}, f32[512,128]{1,0:T(8,128)S(1)}, u32[]{:S(2)}, u32[]{:S(2)}) collective-permute-start(f32[512,128]{1,0:T(8,128)S(1)} %get-tuple-element.98), channel_id=1, source_target_pairs={{32,64},{64,32},{96,0},{0,96},{33,65},{65,33},{97,1},{1,97},{34,66... | collective-permute-start | bytes 786440 | tf_op jit(solution)/shard_map/ppermute | solution.py:41
  62.0 14.5 %collective-permute-start.19 = (f32[512,128]{1,0:T(8,128)S(1)}, f32[512,128]{1,0:T(8,128)S(1)}, u32[]{:S(2)}, u32[]{:S(2)}) collective-permute-start(f32[512,128]{1,0:T(8,128)S(1)} %get-tuple-element.99), channel_id=1, source_target_pairs={{0,8},{8,0},{16,24},{24,16},{1,9},{9,1},{17,25},{25,17},{2,10},{10... | collective-permute-start | bytes 786440 | tf_op jit(solution)/shard_map/ppermute | solution.py:41
  62.0 14.5 %collective-permute-start.20 = (f32[512,128]{1,0:T(8,128)S(1)}, f32[512,128]{1,0:T(8,128)S(1)}, u32[]{:S(2)}, u32[]{:S(2)}) collective-permute-start(f32[512,128]{1,0:T(8,128)S(1)} %get-tuple-element.100), channel_id=1, source_target_pairs={{8,16},{16,8},{24,0},{0,24},{9,17},{17,9},{25,1},{1,25},{10,18},{1... | collective-permute-start | bytes 786440 | tf_op jit(solution)/shard_map/ppermute | solution.py:41
  63.3 13.2 %collective-permute-start.23 = (f32[512,128]{1,0:T(8,128)S(1)}, f32[512,128]{1,0:T(8,128)S(1)}, u32[]{:S(2)}, u32[]{:S(2)}) collective-permute-start(f32[512,128]{1,0:T(8,128)S(1)} %get-tuple-element.103), channel_id=1, source_target_pairs={{0,32},{32,0},{64,96},{96,64},{1,33},{33,1},{65,97},{97,65},{2,34}... | collective-permute-start | bytes 786440 | tf_op jit(solution)/shard_map/ppermute | solution.py:41
  64.6 6.6 %collective-permute-start.22 = (f32[256,128]{1,0:T(8,128)S(1)}, f32[256,128]{1,0:T(8,128)S(1)}, u32[]{:S(2)}, u32[]{:S(2)}) collective-permute-start(f32[256,128]{1,0:T(8,128)S(1)} %get-tuple-element.102), channel_id=1, source_target_pairs={{0,1},{1,0},{2,3},{3,2},{4,5},{5,4},{6,7},{7,6},{8,9},{9,8},{10,11... | collective-permute-start | bytes 393224 | tf_op jit(solution)/shard_map/ppermute | solution.py:41
  64.6 2.2 %copy-start.1 = (f32[8192,128]{1,0:T(8,128)S(1)}, f32[8192,128]{1,0:T(8,128)}, u32[]{:S(2)}) copy-start(f32[8192,128]{1,0:T(8,128)} %copy-done) | copy-start | bytes 12582916
  71.2 10.0 %collective-permute-start.24 = (f32[512,128]{1,0:T(8,128)S(1)}, f32[512,128]{1,0:T(8,128)S(1)}, u32[]{:S(2)}, u32[]{:S(2)}) collective-permute-start(f32[512,128]{1,0:T(8,128)S(1)} %get-tuple-element.106), channel_id=1, source_target_pairs={{32,64},{64,32},{96,0},{0,96},{33,65},{65,33},{97,1},{1,97},{34,66... | collective-permute-start | bytes 786440 | tf_op jit(solution)/shard_map/ppermute | solution.py:41
  77.8 13.4 %collective-permute-start.25 = (f32[544,128]{1,0:T(8,128)S(1)}, f32[544,128]{1,0:T(8,128)S(1)}, u32[]{:S(2)}, u32[]{:S(2)}) collective-permute-start(f32[544,128]{1,0:T(8,128)S(1)} %get-tuple-element.108), channel_id=1, source_target_pairs={{0,8},{8,0},{16,24},{24,16},{1,9},{9,1},{17,25},{25,17},{2,10},{10... | collective-permute-start | bytes 835592 | tf_op jit(solution)/shard_map/ppermute | solution.py:41
  77.9 13.4 %collective-permute-start.26 = (f32[544,128]{1,0:T(8,128)S(1)}, f32[544,128]{1,0:T(8,128)S(1)}, u32[]{:S(2)}, u32[]{:S(2)}) collective-permute-start(f32[544,128]{1,0:T(8,128)S(1)} %get-tuple-element.109), channel_id=1, source_target_pairs={{8,16},{16,8},{24,0},{0,24},{9,17},{17,9},{25,1},{1,25},{10,18},{1... | collective-permute-start | bytes 835592 | tf_op jit(solution)/shard_map/ppermute | solution.py:41
  79.0 12.2 %collective-permute-start.29 = (f32[512,128]{1,0:T(8,128)S(1)}, f32[512,128]{1,0:T(8,128)S(1)}, u32[]{:S(2)}, u32[]{:S(2)}) collective-permute-start(f32[512,128]{1,0:T(8,128)S(1)} %get-tuple-element.112), channel_id=1, source_target_pairs={{0,32},{32,0},{64,96},{96,64},{1,33},{33,1},{65,97},{97,65},{2,34}... | collective-permute-start | bytes 786440 | tf_op jit(solution)/shard_map/ppermute | solution.py:41
  79.3 7.1 %collective-permute-start.27 = (f32[272,128]{1,0:T(8,128)S(1)}, f32[272,128]{1,0:T(8,128)S(1)}, u32[]{:S(2)}, u32[]{:S(2)}) collective-permute-start(f32[272,128]{1,0:T(8,128)S(1)} %get-tuple-element.110), channel_id=1, source_target_pairs={{1,2},{2,1},{3,4},{4,3},{5,6},{6,5},{7,0},{0,7},{9,10},{10,9},{11,... | collective-permute-start | bytes 417800 | tf_op jit(solution)/shard_map/ppermute | solution.py:41
  81.1 10.1 %collective-permute-start.28 = (f32[272,128]{1,0:T(8,128)S(1)}, f32[272,128]{1,0:T(8,128)S(1)}, u32[]{:S(2)}, u32[]{:S(2)}) collective-permute-start(f32[272,128]{1,0:T(8,128)S(1)} %get-tuple-element.111), channel_id=1, source_target_pairs={{0,1},{1,0},{2,3},{3,2},{4,5},{5,4},{6,7},{7,6},{8,9},{9,8},{10,11... | collective-permute-start | bytes 417800 | tf_op jit(solution)/shard_map/ppermute | solution.py:41
  86.3 10.1 %collective-permute-start.30 = (f32[512,128]{1,0:T(8,128)S(1)}, f32[512,128]{1,0:T(8,128)S(1)}, u32[]{:S(2)}, u32[]{:S(2)}) collective-permute-start(f32[512,128]{1,0:T(8,128)S(1)} %get-tuple-element.116), channel_id=1, source_target_pairs={{32,64},{64,32},{96,0},{0,96},{33,65},{65,33},{97,1},{1,97},{34,66... | collective-permute-start | bytes 786440 | tf_op jit(solution)/shard_map/ppermute | solution.py:41
  92.7 8.9 %collective-permute-start.31 = (f32[576,128]{1,0:T(8,128)S(1)}, f32[576,128]{1,0:T(8,128)S(1)}, u32[]{:S(2)}, u32[]{:S(2)}) collective-permute-start(f32[576,128]{1,0:T(8,128)S(1)} %get-tuple-element.119), channel_id=1, source_target_pairs={{0,8},{8,0},{16,24},{24,16},{1,9},{9,1},{17,25},{25,17},{2,10},{10... | collective-permute-start | bytes 884744 | tf_op jit(solution)/shard_map/ppermute | solution.py:41
  92.8 9.8 %collective-permute-start.32 = (f32[576,128]{1,0:T(8,128)S(1)}, f32[576,128]{1,0:T(8,128)S(1)}, u32[]{:S(2)}, u32[]{:S(2)}) collective-permute-start(f32[576,128]{1,0:T(8,128)S(1)} %get-tuple-element.120), channel_id=1, source_target_pairs={{8,16},{16,8},{24,0},{0,24},{9,17},{17,9},{25,1},{1,25},{10,18},{1... | collective-permute-start | bytes 884744 | tf_op jit(solution)/shard_map/ppermute | solution.py:41
  94.6 7.0 %collective-permute-start.35 = (f32[512,128]{1,0:T(8,128)S(1)}, f32[512,128]{1,0:T(8,128)S(1)}, u32[]{:S(2)}, u32[]{:S(2)}) collective-permute-start(f32[512,128]{1,0:T(8,128)S(1)} %get-tuple-element.123), channel_id=1, source_target_pairs={{0,32},{32,0},{64,96},{96,64},{1,33},{33,1},{65,97},{97,65},{2,34}... | collective-permute-start | bytes 786440 | tf_op jit(solution)/shard_map/ppermute | solution.py:41
  94.6 7.0 %collective-permute-start.33 = (f32[288,128]{1,0:T(8,128)S(1)}, f32[288,128]{1,0:T(8,128)S(1)}, u32[]{:S(2)}, u32[]{:S(2)}) collective-permute-start(f32[288,128]{1,0:T(8,128)S(1)} %get-tuple-element.121), channel_id=1, source_target_pairs={{1,2},{2,1},{3,4},{4,3},{5,6},{6,5},{7,0},{0,7},{9,10},{10,9},{11,... | collective-permute-start | bytes 442376 | tf_op jit(solution)/shard_map/ppermute | solution.py:41
  96.4 5.2 %collective-permute-start.34 = (f32[288,128]{1,0:T(8,128)S(1)}, f32[288,128]{1,0:T(8,128)S(1)}, u32[]{:S(2)}, u32[]{:S(2)}) collective-permute-start(f32[288,128]{1,0:T(8,128)S(1)} %get-tuple-element.122), channel_id=1, source_target_pairs={{0,1},{1,0},{2,3},{3,2},{4,5},{5,4},{6,7},{7,6},{8,9},{9,8},{10,11... | collective-permute-start | bytes 442376 | tf_op jit(solution)/shard_map/ppermute | solution.py:41
  96.4 6.1 %copy-start.2 = (f32[8192,128]{1,0:T(8,128)S(1)}, f32[8192,128]{1,0:T(8,128)}, u32[]{:S(2)}) copy-start(f32[8192,128]{1,0:T(8,128)} %copy-done) | copy-start | bytes 12582916
where the time goes:
time: 109 us
  starting transfers between devices  38.9 us (36%)
  Pallas kernels  37.3 us (34%)
  waiting for transfers between devices  29.1 us (27%)
  local copies, waits for them, and re-layouts  3.11 us (3%)
    ppermute x36, starting transfers between devices, swap(): return lax.ppermute(x, axis, pairs)  38.9 us
    pallas_call x17, Pallas kernels, call(): pl.pallas_call(kernel, out_shape=out_shape, in_specs=[HBM if i in in_hbm...  37.3 us
    ppermute x36, waiting for transfers between devices, swap(): return lax.ppermute(x, axis, pairs)  29.1 us
    unnamed x12, local copies, waits for them, and re-layouts  3.11 us
  transfers between devices with their start and end apart: 36, of which 13 were waited for; matrix products, arithmetic and copies ran while one was open for 0% of the time, Pallas kernels for 20%

commit v1 on v0

--- a/solution.py
+++ b/solution.py
@@ -16,6 +16,7 @@
 LINE = {"gy": NZ, "gz": NY}
 CROSS = ("gx", 1)
 LOCALS = (("gy", 0), ("gy", 1), ("gz", 1), ("gz", 0), ("gx", 0))
+FACE_ROWS = 2 * (FACE["gy"] + FACE["gz"])
 SCALES = 16
 
 F32 = jnp.float32
@@ -90,41 +91,48 @@
 
 
 def copy_plane(src, base, dst):
-    def body(i):
-        at = pl.multiple_of(i * 64, 64)
-        dst[pl.ds(at, 64), :] = src[pl.ds(pl.multiple_of(base + at, 64), 64), :]
-
-    loop(PLANE // 64, body)
-
-
-def emit_face(w, axis, kind, send):
+    for i in range(PLANE // 128):
+        rows = pl.ds(i * 128, 128)
+        dst[rows, :] = src[pl.ds(pl.multiple_of(base + i * 128, 128), 128), :]
+
+
+def batches(axis):
+    size = 8 if axis == "gz" else 4
+    return [range(g, g + size) for g in range(0, NX, size)]
+
+
+def emit_face(w, axis, kind, send, only=None):
     at = face_slices(axis, kind)
-
-    def body(i):
-        src, dst = at(i)
-        send[dst, :] = w[src, :]
-
-    loop(NX, body)
-
-
-def emit_locals(w, sends, ghosts=()):
+    for group in batches(axis) if only is None else [only]:
+        got = [w[at(i)[0], :] for i in group]
+        for i, v in zip(group, got):
+            send[at(i)[1], :] = v
+
+
+def fix_faces(half, w, a2, halos, cross, sends=None):
+    todo = [(a, k, h, None if sends is None else s) for (a, k), h, s in zip(LOCALS, halos, sends or [None] * 5)]
+    order = [t for t in todo if t[0] == "gz"] + [t for t in todo if t[0] == "gy"]
+    for axis, kind, halo, send in order + [(*CROSS, cross, None), todo[-1]]:
+        at = face_slices(axis, kind)
+        for group in batches(axis):
+            got = []
+            for i in group:
+                dst, src = at(i)
+                r = a2[dst, :] * halo[src, :]
+                got.append(w[dst, :] + (0.5 * r if half else r))
+            for i, v in zip(group, got):
+                w[at(i)[0], :] = v
+                if send is not None and axis != "gz":
+                    send[at(i)[1], :] = v
+    for axis, kind, _, send in order if sends else ():
+        emit_face(w, axis, kind, send, (0, NX - 1) if axis == "gy" else None)
+
+
+def emit_ghost_lines(ghosts, sends):
     for (axis, kind), send in zip(LOCALS, sends):
-        emit_face(w, axis, kind, send)
         if axis != "gx":
             for i, g in enumerate(ghosts):
                 send[line_rows(axis, i), :] = g[plane_line(axis, kind), :]
-
-
-def fix_faces(half, w, a2, halos, cross):
-    for (axis, kind), halo in list(zip(LOCALS, halos))[::-1] + [(CROSS, cross)]:
-        at = face_slices(axis, kind)
-
-        def body(i, at=at, halo=halo):
-            dst, src = at(i)
-            r = a2[dst, :] * halo[src, :]
-            w[dst, :] = w[dst, :] + (0.5 * r if half else r)
-
-        loop(NX, body)
 
 
 def fix_lines(half, g, a2, halos, i):
@@ -204,41 +212,51 @@
         emit(j, jnp.broadcast_to(st[:NZ, j : j + 1], (NZ, C)))
 
 
-def start_kernel(feat, scales, w0, sb, d1, d2, d3, *rest):
-    sends, (buf, sems) = rest[:5], rest[5:]
+def start_kernel(feat, scales, fv, sb, d1, d2, d3, *rest):
+    sends, (sv, sems) = rest[:5], rest[5:]
+    first = pltpu.make_async_copy(scales, sv, sems.at[NX])
+    first.start()
 
     def copy(i):
-        rows = pl.ds(pl.multiple_of(i * PLANE, PLANE), PLANE)
-        return pltpu.make_async_copy(feat.at[rows, :], buf.at[rows, :], sems.at[i])
+        rows = pl.ds(i * PLANE, PLANE)
+        return pltpu.make_async_copy(feat.at[rows, :], fv.at[rows, :], sems.at[i])
 
     for i in range(NX):
         copy(i).start()
+    first.wait()
+    for i in range(NX):
+
+        def emit(j, b, i=i):
+            sb[pl.ds(i * PLANE + j * NZ, NZ), :] = b
+
+        spread(sv[i], emit)
     for i in range(NX):
         copy(i).wait()
-
-        def emit(j, b, i=i):
-            rows = pl.ds(i * PLANE + j * NZ, NZ)
-            sb[rows, :] = b
-            w0[rows, :] = b * buf[rows, :]
-
-        spread(scales[i], emit)
     up = side(*CROSS)
     for depth, d in ((1, d1), (2, d2), (3, d3)):
-        copy_plane(w0, cross_base(depth), d)
+        base = cross_base(depth)
+        for i in range(PLANE // 128):
+            rows = pl.ds(pl.multiple_of(base + i * 128, 128), 128)
+            d[pl.ds(i * 128, 128), :] = sb[rows, :] * fv[rows, :]
         if depth < 3:
             d[PLANE:, :] = jnp.zeros((SCALES, C), F32)
-            d[PLANE:, :NZ] = scales[up * (NX - depth) + (1 - up) * (depth - 1)]
-    emit_locals(w0, sends)
-
-
-def aux_kernel(sb, weights, a2, rs, w4):
+            d[PLANE:, :NZ] = sv[up * (NX - depth) + (1 - up) * (depth - 1)]
+    for (axis, kind), send in zip(LOCALS, sends):
+        at = face_slices(axis, kind)
+        for group in batches(axis):
+            got = [sb[at(i)[0], :] * fv[at(i)[0], :] for i in group]
+            for i, v in zip(group, got):
+                send[at(i)[1], :] = v
+
+
+def aux_kernel(sb, fv, weights, w0, a2, w4):
     def body(i):
-        rows = pl.ds(pl.multiple_of(i * 64, 64), 64)
+        rows = pl.ds(pl.multiple_of(i * 128, 128), 128)
         s = sb[rows, :]
+        w0[rows, :] = s * fv[rows, :]
         a2[rows, :] = -2.0 * (s * s)
-        rs[rows, :] = 1.0 / s
-
-    loop(ROWS // 64, body, 2)
+
+    loop(ROWS // 128, body, 1)
     for layer in range(2):
         w = weights[layer]
         hi = w.astype(jnp.bfloat16)
@@ -272,16 +290,16 @@
 
 def fix1_kernel(w_in, a2, d1, *rest):
     halos, w, sends = rest[:5], rest[5], rest[6:]
-    fix_faces(True, w, a2, halos, d1)
-    emit_locals(w, sends, (d1,))
+    fix_faces(True, w, a2, halos, d1, sends)
+    emit_ghost_lines((d1,), sends)
 
 
 def fix2_kernel(w_in, a2, d2, p1, a2g1, *rest):
     halos, w, w1g1, sends = rest[:5], rest[5], rest[6], rest[7:]
     ghost_add(True, p1, a2g1, d2, w1g1)
     fix_lines(True, w1g1, a2g1, halos, 0)
-    fix_faces(False, w, a2, halos, w1g1)
-    emit_locals(w, sends, (w1g1, d2))
+    fix_faces(False, w, a2, halos, w1g1, sends)
+    emit_ghost_lines((w1g1, d2), sends)
 
 
 def fix3(w, a2, d3, p2, q1, a2g1, a2g2, halos, g2, g1):
@@ -292,7 +310,7 @@
     fix_faces(False, w, a2, halos, g1)
 
 
-def mixed(layer, ws, rs, thetas, w4, rows):
+def mixed(layer, ws, a2, thetas, w4, rows, scaled):
     t = None
     for k, w in enumerate(ws):
         term = thetas[layer, k : k + 1, :] * w[rows, :]
@@ -300,71 +318,69 @@
     hi = t.astype(jnp.bfloat16)
     lo = (t - hi.astype(F32)).astype(jnp.bfloat16)
     both = jnp.dot(jnp.concatenate([hi, lo], axis=1), w4[layer], preferred_element_type=F32)
-    v = (both[:, :C] + both[:, C:]) * rs[rows, :]
-    return v / (1.0 + jnp.exp(-v))
-
-
-def face_mix_kernel(layer, w3_in, a2, d3, p2, q1, a2g1, a2g2, w0, w1, w2, sb, rs, thetas, w4, *rest):
+    q = -0.5 * a2[rows, :]
+    r = lax.rsqrt(q)
+    h = (both[:, :C] + both[:, C:]) * (0.5 * r)
+    out = h + h * jnp.tanh(h)
+    return (q * r) * out if scaled else out
+
+
+def face_mix_kernel(layer, w3_in, a2, d3, p2, q1, a2g1, a2g2, w0, w1, w2, thetas, w4, *rest):
     halos, w3, d1, sends, (g2, g1, ft) = rest[:5], rest[5], rest[6], rest[7:12], rest[12:]
     fix3(w3, a2, d3, p2, q1, a2g1, a2g2, halos, g2, g1)
     ws = (w0, w1, w2, w3)
-    for (axis, kind), send in [(CROSS, d1)] + list(zip(LOCALS, sends)):
+    at_row = 0
+    for (axis, kind), send in zip(LOCALS, sends):
+        if axis == "gx":
+            continue
         at = face_slices(axis, kind)
-        size = FACE[axis]
-        if axis == "gx":
-            base = side(axis, kind) * ((NX - 1) * PLANE)
-
-            def body(i, base=base, send=send):
-                rows = pl.ds(pl.multiple_of(base + i * 256, 256), 256)
-                send[pl.ds(pl.multiple_of(i * 256, 256), 256), :] = sb[rows, :] * mixed(
-                    layer, ws, rs, thetas, w4, rows
-                )
-
-            loop(size // 256, body, True)
-            continue
-
-        def gather(i, at=at):
-            src, dst = at(i)
-            for k, w in enumerate(ws + (rs, sb)):
-                ft[k, dst, :] = w[src, :]
-
-        loop(NX, gather)
-
-        def body(i, send=send):
-            rows = pl.ds(pl.multiple_of(i * 256, 256), 256)
-            send[rows, :] = ft[5, rows, :] * mixed(
-                layer, tuple(ft.at[k] for k in range(4)), ft.at[4], thetas, w4, rows
-            )
-
-        loop(size // 256, body, True)
-
-
-def mix_kernel(layer, w0, w1, w2, w3, sb, rs, thetas, w4, out, d2, d3):
+        for group in batches(axis):
+            for k, w in enumerate(ws + (a2,)):
+                got = [w[at(i)[0], :] for i in group]
+                for i, v in zip(group, got):
+                    ft[k, pl.ds(at_row + i * LINE[axis], LINE[axis]), :] = v
+        at_row += FACE[axis]
+    for axis, kind, send in ((*CROSS, d1), (*LOCALS[-1], sends[-1])):
+        base = side(axis, kind) * ((NX - 1) * PLANE)
+        for i in range(PLANE // 256):
+            rows = pl.ds(pl.multiple_of(base + i * 256, 256), 256)
+            send[pl.ds(i * 256, 256), :] = mixed(layer, ws, a2, thetas, w4, rows, True)
+    at_row = 0
+    fts = tuple(ft.at[k] for k in range(4))
+    for (axis, kind), send in zip(LOCALS[:-1], sends):
+        for i in range(FACE[axis] // 256):
+            rows = pl.ds(at_row + i * 256, 256)
+            send[pl.ds(i * 256, 256), :] = mixed(layer, fts, ft.at[4], thetas, w4, rows, True)
+        at_row += FACE[axis]
+
+
+def mix_kernel(layer, w0, w1, w2, w3, a2, thetas, w4, out, d2, d3):
     def body(i):
         rows = pl.ds(pl.multiple_of(i * 256, 256), 256)
-        out[rows, :] = sb[rows, :] * mixed(layer, (w0, w1, w2, w3), rs, thetas, w4, rows)
-
-    loop(ROWS // 256, body, 2)
+        out[rows, :] = mixed(layer, (w0, w1, w2, w3), a2, thetas, w4, rows, True)
+
+    loop(ROWS // 256, body, 4)
     copy_plane(out, cross_base(2), d2)
     copy_plane(out, cross_base(3), d3)
 
 
-def last_kernel(layer, w3_in, a2, d3, p2, q1, a2g1, a2g2, w0, w1, w2, rs, thetas, w4, *rest):
+def last_kernel(layer, w3_in, a2, d3, p2, q1, a2g1, a2g2, w0, w1, w2, thetas, w4, *rest):
     halos, (w3, out), (g2, g1, buf, sems) = rest[:5], rest[5:7], rest[7:]
     fix3(w3, a2, d3, p2, q1, a2g1, a2g2, halos, g2, g1)
+    step = 1024
 
     def copy(i):
-        rows = pl.ds(pl.multiple_of(i * PLANE, PLANE), PLANE)
+        rows = pl.ds(pl.multiple_of(i * step, step), step)
         return pltpu.make_async_copy(buf.at[rows, :], out.at[rows, :], sems.at[i])
 
     def body(i):
-        for h in range(2):
-            rows = pl.ds(pl.multiple_of(i * PLANE + h * 256, 256), 256)
-            buf[rows, :] = mixed(layer, (w0, w1, w2, w3), rs, thetas, w4, rows)
+        for h in range(step // 256):
+            rows = pl.ds(pl.multiple_of(i * step + h * 256, 256), 256)
+            buf[rows, :] = mixed(layer, (w0, w1, w2, w3), a2, thetas, w4, rows, False)
         copy(i).start()
 
-    loop(NX, body, 1)
-    loop(NX, lambda i: copy(i).wait(), 1)
+    loop(ROWS // step, body, 1)
+    loop(ROWS // step, lambda i: copy(i).wait(), 1)
 
 
 def call(kernel, out_shape, args, in_hbm=(), out_hbm=(), scratch=(), aliases=None, mib=1):
@@ -383,27 +399,23 @@
     shape = features.shape
     feat = pltpu.with_memory_space_constraint(features.reshape(ROWS, C), pltpu.HBM)
     block, plane = arr(ROWS), arr(PLANE)
-    dma = [pltpu.VMEM((ROWS, C), F32), pltpu.SemaphoreType.DMA((NX,))]
+    scales = pltpu.with_memory_space_constraint(scales, pltpu.HBM)
     ghosts = [pltpu.VMEM((PLANE, C), F32)] * 2
-    w0, sb, s1, s2, s3, *sends = call(
+    fv, sb, s1, s2, s3, *sends = call(
         start_kernel,
         [block, block, arr(PLANE + SCALES), arr(PLANE + SCALES), plane] + locals_out(0),
         (feat, scales),
-        in_hbm=(0,),
-        scratch=dma,
-        mib=6,
+        in_hbm=(0, 1),
+        scratch=[pltpu.VMEM(scales.shape, F32), pltpu.SemaphoreType.DMA((NX + 1,))],
     )
     for layer in range(2):
         last = layer == 1
         if last:
-            w0, s2, s3 = call(
-                functools.partial(mix_kernel, 0), [block, plane, plane], (w0, w1, w2, w3, sb, rs, thetas, w4)
-            )
+            w0, s2, s3 = call(functools.partial(mix_kernel, 0), [block, plane, plane], (w0, w1, w2, w3, a2, thetas, w4))
         (d1,), halos, (d2,) = exchange(sends, cross=s1, late=s2)
         if not last:
-            a2, rs, w4 = call(
-                aux_kernel, [block, block, jax.ShapeDtypeStruct((2, 2 * C, 2 * C), jnp.bfloat16)], (sb, weights)
-            )
+            w4 = jax.ShapeDtypeStruct((2, 2 * C, 2 * C), jnp.bfloat16)
+            w0, a2, w4 = call(aux_kernel, [block, block, w4], (sb, fv, weights))
         (w1,) = call(local1_kernel, [block], (w0, a2))
         w1, *sends = call(fix1_kernel, [block] + locals_out(1), (w1, a2, d1, *halos), aliases={0: 0})
         _, halos, (d3,) = exchange(sends, late=s3)
@@ -422,18 +434,18 @@
             w3, s1, *sends = call(
                 functools.partial(face_mix_kernel, layer),
                 [block, plane] + locals_out(0),
-                (*tail, sb, rs, thetas, w4, *halos),
-                scratch=ghosts + [pltpu.VMEM((6, PLANE, C), F32)],
-                mib=6,
+                (*tail, thetas, w4, *halos),
+                scratch=ghosts + [pltpu.VMEM((5, FACE_ROWS, C), F32)],
+                mib=7,
                 aliases={0: 0},
             )
         else:
             _, out = call(
                 functools.partial(last_kernel, layer),
                 [block, block],
-                (*tail, rs, thetas, w4, *halos),
+                (*tail, thetas, w4, *halos),
                 out_hbm=(1,),
-                scratch=ghosts + dma,
+                scratch=ghosts + [pltpu.VMEM((ROWS, C), F32), pltpu.SemaphoreType.DMA((8,))],
                 mib=8,
                 aliases={0: 0},
             )

time: 109 us -> 101 us (0.927)
  the two profiles are of different devices: /device:TPU:1 before, /device:TPU:6 now
where the time goes in v1:
time: 101 us; the launch traced here: 99.6 us
  waiting for transfers between devices  36.8 us (36%)
  starting transfers between devices  31.5 us (31%)
  Pallas kernels  30.9 us (31%)
    ppermute x36, waiting for transfers between devices, swap(): return lax.ppermute(x, axis, pairs)  36.8 us
    ppermute x36, starting transfers between devices, swap(): return lax.ppermute(x, axis, pairs)  31.5 us
    pallas_call x17, Pallas kernels, call(): pl.pallas_call(kernel, out_shape=out_shape, in_specs=[HBM if i in in_hbm...  30.9 us
  transfers between devices with their start and end apart: 36, of which 15 were waited for; matrix products, arithmetic and copies ran while one was open for 0% of the time, Pallas kernels for 19%

profile of v1, /device:TPU:6, one launch (start us, length us, event | category | flops | bytes accessed | tf_op | source)
XLA Modules:
  0.0 99.6 jit_solution(4634073759296866408)
XLA Ops:
  0.0 3.5 %shard_map.46 = (f32[8192,128]{1,0:T(8,128)S(1)}, f32[8192,128]{1,0:T(8,128)S(1)}, f32[528,128]{1,0:T(8,128)S(1)}, f32[528,128]{1,0:T(8,128)S(1)}, f32[512,128]{...) custom-call(f32[8192,128]{1,0:T(8,128)} %bitcast.2, ...), custom_call_target="tpu_custom_call" | custom-call | tf_op jit(solution)/shard_map/pallas_call | solution.py:387
  3.5 5.1 %collective-permute-start.3 = (f32[256,128]{1,0:T(8,128)S(1)}, f32[256,128]{1,0:T(8,128)S(1)}, u32[]{:S(2)}, u32[]{:S(2)}) collective-permute-start(f32[256,128]{1,0:T(8,128)S(1)} %get-tuple-element.72), channel_id=1, source_target_pairs={{1,2},{2,1},{3,4},{4,3},{5,6},{6,5},{7,0},{0,7},{9,10},{10,9},{11,... | collective-permute-start | bytes 393224 | tf_op jit(solution)/shard_map/ppermute | solution.py:42
  8.6 2.1 %collective-permute-start = (f32[528,128]{1,0:T(8,128)S(1)}, f32[528,128]{1,0:T(8,128)S(1)}, u32[]{:S(2)}, u32[]{:S(2)}) collective-permute-start(f32[528,128]{1,0:T(8,128)S(1)} %get-tuple-element.69), channel_id=1, source_target_pairs={{32,64},{64,32},{96,0},{0,96},{33,65},{65,33},{97,1},{1,97},{34,66... | collective-permute-start | bytes 811016 | tf_op jit(solution)/shard_map/ppermute | solution.py:42
  10.7 0.8 collective-permute-start.1
  11.5 1.1 %collective-permute-start.2 = (f32[512,128]{1,0:T(8,128)S(1)}, f32[512,128]{1,0:T(8,128)S(1)}, u32[]{:S(2)}, u32[]{:S(2)}) collective-permute-start(f32[512,128]{1,0:T(8,128)S(1)} %get-tuple-element.71), channel_id=1, source_target_pairs={{8,16},{16,8},{24,0},{0,24},{9,17},{17,9},{25,1},{1,25},{10,18},{1... | collective-permute-start | bytes 786440 | tf_op jit(solution)/shard_map/ppermute | solution.py:42
  13.1 4.0 %collective-permute-done.4.rest_3_ = f32[256,128]{1,0:T(8,128)S(1)} collective-permute-done((f32[256,128]{1,0:T(8,128)S(1)}, f32[256,128]{1,0:T(8,128)S(1)}, u32[]{:S(2)}, u32[]{:S(2)}) %collective-permute-start.4) | collective-permute-done | bytes 131104 | tf_op jit(solution)/shard_map/ppermute | solution.py:42
  17.2 1.0 shard_map.47
  18.2 1.5 %shard_map.48.w_in = f32[8192,128]{1,0:T(8,128)S(1)} custom-call(f32[8192,128]{1,0:T(8,128)S(1)} %get-tuple-element.67.w0, f32[8192,128]{1,0:T(8,128)S(1)} %get-tuple-element.68.a2), custom_call_target="tpu_custom_call" | custom-call | tf_op jit(solution)/shard_map/pallas_call | solution.py:387
  19.9 1.8 %collective-permute-done.2.rest_1_ = f32[512,128]{1,0:T(8,128)S(1)} collective-permute-done((f32[512,128]{1,0:T(8,128)S(1)}, f32[512,128]{1,0:T(8,128)S(1)}, u32[]{:S(2)}, u32[]{:S(2)}) %collective-permute-start.2) | collective-permute-done | bytes 262176 | tf_op jit(solution)/shard_map/ppermute | solution.py:42
  21.6 1.1 %shard_map.49 = (f32[8192,128]{1,0:T(8,128)S(1)}, f32[544,128]{1,0:T(8,128)S(1)}, f32[544,128]{1,0:T(8,128)S(1)}, f32[272,128]{1,0:T(8,128)S(1)}, f32[272,128]{1,0:T(8,128)S(1)}, /*index=5*/f32[512,128]{1,0:T(8,128)S(1)}) custom-call(f32[8192,128]{1,0:T(8,128)S(1)} %shard_map.48.w_in, ...), custom_call_target="tpu_custom_call", output_to_operand_aliasing={{0}: (0, {})} | custom-call | tf_op jit(solution)/shard_map/pallas_call | solution.py:387
  22.8 1.2 %collective-permute-start.8 = (f32[544,128]{1,0:T(8,128)S(1)}, f32[544,128]{1,0:T(8,128)S(1)}, u32[]{:S(2)}, u32[]{:S(2)}) collective-permute-start(f32[544,128]{1,0:T(8,128)S(1)} %get-tuple-element.80), channel_id=1, source_target_pairs={{8,16},{16,8},{24,0},{0,24},{9,17},{17,9},{25,1},{1,25},{10,18},{1... | collective-permute-start | bytes 835592 | tf_op jit(solution)/shard_map/ppermute | solution.py:42
  24.0 1.2 %collective-permute-start.9 = (f32[272,128]{1,0:T(8,128)S(1)}, f32[272,128]{1,0:T(8,128)S(1)}, u32[]{:S(2)}, u32[]{:S(2)}) collective-permute-start(f32[272,128]{1,0:T(8,128)S(1)} %get-tuple-element.81), channel_id=1, source_target_pairs={{1,2},{2,1},{3,4},{4,3},{5,6},{6,5},{7,0},{0,7},{9,10},{10,9},{11,... | collective-permute-start | bytes 417800 | tf_op jit(solution)/shard_map/ppermute | solution.py:42
  25.2 1.8 %collective-permute-done.6.d2.d = f32[528,128]{1,0:T(8,128)S(1)} collective-permute-done((f32[528,128]{1,0:T(8,128)S(1)}, f32[528,128]{1,0:T(8,128)S(1)}, u32[]{:S(2)}, u32[]{:S(2)}) %collective-permute-start.6) | collective-permute-done | bytes 270368 | tf_op jit(solution)/shard_map/ppermute | solution.py:42
  27.1 5.2 %collective-permute-done.9.rest_2_ = f32[272,128]{1,0:T(8,128)S(1)} collective-permute-done((f32[272,128]{1,0:T(8,128)S(1)}, f32[272,128]{1,0:T(8,128)S(1)}, u32[]{:S(2)}, u32[]{:S(2)}) %collective-permute-start.9) | collective-permute-done | bytes 139296 | tf_op jit(solution)/shard_map/ppermute | solution.py:42
  32.2 1.2 %collective-permute-start.12 = (f32[512,128]{1,0:T(8,128)S(1)}, f32[512,128]{1,0:T(8,128)S(1)}, u32[]{:S(2)}, u32[]{:S(2)}) collective-permute-start(f32[512,128]{1,0:T(8,128)S(1)} %get-tuple-element.87), channel_id=1, source_target_pairs={{32,64},{64,32},{96,0},{0,96},{33,65},{65,33},{97,1},{1,97},{34,66... | collective-permute-start | bytes 786440 | tf_op jit(solution)/shard_map/ppermute | solution.py:42
  33.7 1.6 %shard_map.51 = (f32[8192,128]{1,0:T(8,128)S(1)}, f32[512,128]{1,0:T(8,128)S(1)}) custom-call(f32[8192,128]{1,0:T(8,128)S(1)} %get-tuple-element.75.w1, f32[8192,128]{1,0:T(8,128)S(1)} %get-tuple-element.68.a2, f32[8192,128]{1,0:T(8,128)S(1)} %get-tuple-element.67.w0, f32[528,128]{1,0:T(8,128)S(1)} %collective-permute-done.d1.d, f32[512,128]{1,0:T(8,128)S(1)} %shard_map.50.a2g1), custom_call_target="tpu_custom_call" | custom-call | tf_op jit(solution)/shard_map/pallas_call | solution.py:387
  35.4 1.2 %shard_map.52 = (f32[8192,128]{1,0:T(8,128)S(1)}, f32[512,128]{1,0:T(8,128)S(1)}, f32[576,128]{1,0:T(8,128)S(1)}, f32[576,128]{1,0:T(8,128)S(1)}, f32[288,128]{1...) custom-call(f32[8192,128]{1,0:T(8,128)S(1)} %get-tuple-element.76.w_in, ...), custom_call_target="tpu_custom_call", output_to_operand_aliasing={{0}: (0, {})} | custom-call | tf_op jit(solution)/shard_map/pallas_call | solution.py:387
  36.7 2.6 %collective-permute-start.14 = (f32[576,128]{1,0:T(8,128)S(1)}, f32[576,128]{1,0:T(8,128)S(1)}, u32[]{:S(2)}, u32[]{:S(2)}) collective-permute-start(f32[576,128]{1,0:T(8,128)S(1)} %get-tuple-element.92), channel_id=1, source_target_pairs={{8,16},{16,8},{24,0},{0,24},{9,17},{17,9},{25,1},{1,25},{10,18},{1... | collective-permute-start | bytes 884744 | tf_op jit(solution)/shard_map/ppermute | solution.py:42
  39.6 2.5 %collective-permute-done.12.d3 = f32[512,128]{1,0:T(8,128)S(1)} collective-permute-done((f32[512,128]{1,0:T(8,128)S(1)}, f32[512,128]{1,0:T(8,128)S(1)}, u32[]{:S(2)}, u32[]{:S(2)}) %collective-permute-start.12) | collective-permute-done | bytes 262176 | tf_op jit(solution)/shard_map/ppermute | solution.py:42
  42.4 1.7 %shard_map.54 = (f32[8192,128]{1,0:T(8,128)S(1)}, f32[512,128]{1,0:T(8,128)S(1)}, f32[512,128]{1,0:T(8,128)S(1)}) custom-call(f32[8192,128]{1,0:T(8,128)S(1)} %get-tuple-element.84.w2, f32[8192,128]{1,0:T(8,128)S(1)} %get-tuple-element.68.a2, f32[8192,128]{1,0:T(8,128)S(1)} %get-tuple-element.75.w1, f32[528,128]{1,0:T(8,128)S(1)} %collective-permute-done.d1.d, ...), custom_call_target="tpu_custom_call" | custom-call | tf_op jit(solution)/shard_map/pallas_call | solution.py:387
  44.1 3.6 %collective-permute-done.15.rest_2_ = f32[288,128]{1,0:T(8,128)S(1)} collective-permute-done((f32[288,128]{1,0:T(8,128)S(1)}, f32[288,128]{1,0:T(8,128)S(1)}, u32[]{:S(2)}, u32[]{:S(2)}) %collective-permute-start.15) | collective-permute-done | bytes 147488 | tf_op jit(solution)/shard_map/ppermute | solution.py:42
  47.9 3.2 %shard_map.55 = (f32[8192,128]{1,0:T(8,128)S(1)}, f32[512,128]{1,0:T(8,128)S(1)}, f32[512,128]{1,0:T(8,128)S(1)}, f32[512,128]{1,0:T(8,128)S(1)}, f32[256,128]{1...) custom-call(f32[8192,128]{1,0:T(8,128)S(1)} %get-tuple-element.86.w3_in, ...), custom_call_target="tpu_custom_call", output_to_operand_aliasing={{0}: (0, {})} | custom-call | tf_op jit(solution)/shard_map/pallas_call | solution.py:387
  51.1 1.7 %collective-permute-start.21 = (f32[256,128]{1,0:T(8,128)S(1)}, f32[256,128]{1,0:T(8,128)S(1)}, u32[]{:S(2)}, u32[]{:S(2)}) collective-permute-start(f32[256,128]{1,0:T(8,128)S(1)} %get-tuple-element.101), channel_id=1, source_target_pairs={{1,2},{2,1},{3,4},{4,3},{5,6},{6,5},{7,0},{0,7},{9,10},{10,9},{11,... | collective-permute-start | bytes 393224 | tf_op jit(solution)/shard_map/ppermute | solution.py:42
  52.8 0.7 collective-permute-start.18
  53.5 0.5 collective-permute-start.19
  53.9 2.0 %collective-permute-start.20 = (f32[512,128]{1,0:T(8,128)S(1)}, f32[512,128]{1,0:T(8,128)S(1)}, u32[]{:S(2)}, u32[]{:S(2)}) collective-permute-start(f32[512,128]{1,0:T(8,128)S(1)} %get-tuple-element.100), channel_id=1, source_target_pairs={{8,16},{16,8},{24,0},{0,24},{9,17},{17,9},{25,1},{1,25},{10,18},{1... | collective-permute-start | bytes 786440 | tf_op jit(solution)/shard_map/ppermute | solution.py:42
  56.0 0.6 collective-permute-start.23
  56.5 2.5 %collective-permute-done.21.rest_2_ = f32[256,128]{1,0:T(8,128)S(1)} collective-permute-done((f32[256,128]{1,0:T(8,128)S(1)}, f32[256,128]{1,0:T(8,128)S(1)}, u32[]{:S(2)}, u32[]{:S(2)}) %collective-permute-start.21) | collective-permute-done | bytes 131104 | tf_op jit(solution)/shard_map/ppermute | solution.py:42
  59.0 3.5 %shard_map.56 = (f32[8192,128]{1,0:T(8,128)S(1)}, f32[512,128]{1,0:T(8,128)S(1)}, f32[512,128]{1,0:T(8,128)S(1)}) custom-call(f32[8192,128]{1,0:T(8,128)S(1)} %get-tuple-element.67.w0, f32[8192,128]{1,0:T(8,128)S(1)} %get-tuple-element.75.w1, f32[8192,128]{1,0:T(8,128)S(1)} %get-tuple-element.84.w2, f32[8192,128]{1,0:T(8,128)S(1)} %get-tuple-element.96.w3, ...), custom_call_target="tpu_custom_call" | custom-call | tf_op jit(solution)/shard_map/pallas_call | solution.py:387
  62.6 1.5 %collective-permute-done.22.rest_3_ = f32[256,128]{1,0:T(8,128)S(1)} collective-permute-done((f32[256,128]{1,0:T(8,128)S(1)}, f32[256,128]{1,0:T(8,128)S(1)}, u32[]{:S(2)}, u32[]{:S(2)}) %collective-permute-start.22) | collective-permute-done | bytes 131104 | tf_op jit(solution)/shard_map/ppermute | solution.py:42
  64.0 1.5 %shard_map.57.w_in = f32[8192,128]{1,0:T(8,128)S(1)} custom-call(f32[8192,128]{1,0:T(8,128)S(1)} %get-tuple-element.97.w0, f32[8192,128]{1,0:T(8,128)S(1)} %get-tuple-element.68.a2), custom_call_target="tpu_custom_call" | custom-call | tf_op jit(solution)/shard_map/pallas_call | solution.py:387
  65.6 1.1 %shard_map.58 = (f32[8192,128]{1,0:T(8,128)S(1)}, f32[544,128]{1,0:T(8,128)S(1)}, f32[544,128]{1,0:T(8,128)S(1)}, f32[272,128]{1,0:T(8,128)S(1)}, f32[272,128]{1,0:T(8,128)S(1)}, /*index=5*/f32[512,128]{1,0:T(8,128)S(1)}) custom-call(f32[8192,128]{1,0:T(8,128)S(1)} %shard_map.57.w_in, ...), custom_call_target="tpu_custom_call", output_to_operand_aliasing={{0}: (0, {})} | custom-call | tf_op jit(solution)/shard_map/pallas_call | solution.py:387
  66.7 2.0 %collective-permute-start.25 = (f32[544,128]{1,0:T(8,128)S(1)}, f32[544,128]{1,0:T(8,128)S(1)}, u32[]{:S(2)}, u32[]{:S(2)}) collective-permute-start(f32[544,128]{1,0:T(8,128)S(1)} %get-tuple-element.108), channel_id=1, source_target_pairs={{0,8},{8,0},{16,24},{24,16},{1,9},{9,1},{17,25},{25,17},{2,10},{10... | collective-permute-start | bytes 835592 | tf_op jit(solution)/shard_map/ppermute | solution.py:42
  68.7 2.0 %collective-permute-start.26 = (f32[544,128]{1,0:T(8,128)S(1)}, f32[544,128]{1,0:T(8,128)S(1)}, u32[]{:S(2)}, u32[]{:S(2)}) collective-permute-start(f32[544,128]{1,0:T(8,128)S(1)} %get-tuple-element.109), channel_id=1, source_target_pairs={{8,16},{16,8},{24,0},{0,24},{9,17},{17,9},{25,1},{1,25},{10,18},{1... | collective-permute-start | bytes 835592 | tf_op jit(solution)/shard_map/ppermute | solution.py:42
  70.8 1.0 %collective-permute-start.27 = (f32[272,128]{1,0:T(8,128)S(1)}, f32[272,128]{1,0:T(8,128)S(1)}, u32[]{:S(2)}, u32[]{:S(2)}) collective-permute-start(f32[272,128]{1,0:T(8,128)S(1)} %get-tuple-element.110), channel_id=1, source_target_pairs={{1,2},{2,1},{3,4},{4,3},{5,6},{6,5},{7,0},{0,7},{9,10},{10,9},{11,... | collective-permute-start | bytes 417800 | tf_op jit(solution)/shard_map/ppermute | solution.py:42
  71.8 1.4 %collective-permute-done.24.d2 = f32[512,128]{1,0:T(8,128)S(1)} collective-permute-done((f32[512,128]{1,0:T(8,128)S(1)}, f32[512,128]{1,0:T(8,128)S(1)}, u32[]{:S(2)}, u32[]{:S(2)}) %collective-permute-start.24) | collective-permute-done | bytes 262176 | tf_op jit(solution)/shard_map/ppermute | solution.py:42
  73.2 0.7 collective-permute-start.28
  73.9 5.1 %collective-permute-done.27.rest_2_ = f32[272,128]{1,0:T(8,128)S(1)} collective-permute-done((f32[272,128]{1,0:T(8,128)S(1)}, f32[272,128]{1,0:T(8,128)S(1)}, u32[]{:S(2)}, u32[]{:S(2)}) %collective-permute-start.27) | collective-permute-done | bytes 139296 | tf_op jit(solution)/shard_map/ppermute | solution.py:42
  78.9 1.3 %collective-permute-start.30 = (f32[512,128]{1,0:T(8,128)S(1)}, f32[512,128]{1,0:T(8,128)S(1)}, u32[]{:S(2)}, u32[]{:S(2)}) collective-permute-start(f32[512,128]{1,0:T(8,128)S(1)} %get-tuple-element.116), channel_id=1, source_target_pairs={{32,64},{64,32},{96,0},{0,96},{33,65},{65,33},{97,1},{1,97},{34,66... | collective-permute-start | bytes 786440 | tf_op jit(solution)/shard_map/ppermute | solution.py:42
  80.3 1.6 %shard_map.59 = (f32[8192,128]{1,0:T(8,128)S(1)}, f32[512,128]{1,0:T(8,128)S(1)}) custom-call(f32[8192,128]{1,0:T(8,128)S(1)} %get-tuple-element.104.w1, f32[8192,128]{1,0:T(8,128)S(1)} %get-tuple-element.68.a2, f32[8192,128]{1,0:T(8,128)S(1)} %get-tuple-element.97.w0, f32[512,128]{1,0:T(8,128)S(1)} %collective-permute-done.18.d1, f32[512,128]{1,0:T(8,128)S(1)} %shard_map.50.a2g1), custom_call_target="tpu_custom_call" | custom-call | tf_op jit(solution)/shard_map/pallas_call | solution.py:387
  81.9 1.2 %shard_map.60 = (f32[8192,128]{1,0:T(8,128)S(1)}, f32[512,128]{1,0:T(8,128)S(1)}, f32[576,128]{1,0:T(8,128)S(1)}, f32[576,128]{1,0:T(8,128)S(1)}, f32[288,128]{1...) custom-call(f32[8192,128]{1,0:T(8,128)S(1)} %get-tuple-element.105.w_in, ...), custom_call_target="tpu_custom_call", output_to_operand_aliasing={{0}: (0, {})} | custom-call | tf_op jit(solution)/shard_map/pallas_call | solution.py:387
  83.2 1.3 %collective-permute-start.32 = (f32[576,128]{1,0:T(8,128)S(1)}, f32[576,128]{1,0:T(8,128)S(1)}, u32[]{:S(2)}, u32[]{:S(2)}) collective-permute-start(f32[576,128]{1,0:T(8,128)S(1)} %get-tuple-element.120), channel_id=1, source_target_pairs={{8,16},{16,8},{24,0},{0,24},{9,17},{17,9},{25,1},{1,25},{10,18},{1... | collective-permute-start | bytes 884744 | tf_op jit(solution)/shard_map/ppermute | solution.py:42
  84.5 1.1 %collective-permute-start.35 = (f32[512,128]{1,0:T(8,128)S(1)}, f32[512,128]{1,0:T(8,128)S(1)}, u32[]{:S(2)}, u32[]{:S(2)}) collective-permute-start(f32[512,128]{1,0:T(8,128)S(1)} %get-tuple-element.123), channel_id=1, source_target_pairs={{0,32},{32,0},{64,96},{96,64},{1,33},{33,1},{65,97},{97,65},{2,34}... | collective-permute-start | bytes 786440 | tf_op jit(solution)/shard_map/ppermute | solution.py:42
  85.6 3.2 %collective-permute-done.30.d3 = f32[512,128]{1,0:T(8,128)S(1)} collective-permute-done((f32[512,128]{1,0:T(8,128)S(1)}, f32[512,128]{1,0:T(8,128)S(1)}, u32[]{:S(2)}, u32[]{:S(2)}) %collective-permute-start.30) | collective-permute-done | bytes 262176 | tf_op jit(solution)/shard_map/ppermute | solution.py:42
  88.8 1.7 %shard_map.61 = (f32[8192,128]{1,0:T(8,128)S(1)}, f32[512,128]{1,0:T(8,128)S(1)}, f32[512,128]{1,0:T(8,128)S(1)}) custom-call(f32[8192,128]{1,0:T(8,128)S(1)} %get-tuple-element.113.w2, f32[8192,128]{1,0:T(8,128)S(1)} %get-tuple-element.68.a2, f32[8192,128]{1,0:T(8,128)S(1)} %get-tuple-element.104.w1, f32[512,128]{1,0:T(8,128)S(1)} %collective-permute-done.18.d1, ...), custom_call_target="tpu_custom_call" | custom-call | tf_op jit(solution)/shard_map/pallas_call | solution.py:387
  90.5 2.9 %collective-permute-done.33.rest_2_ = f32[288,128]{1,0:T(8,128)S(1)} collective-permute-done((f32[288,128]{1,0:T(8,128)S(1)}, f32[288,128]{1,0:T(8,128)S(1)}, u32[]{:S(2)}, u32[]{:S(2)}) %collective-permute-start.33) | collective-permute-done | bytes 147488 | tf_op jit(solution)/shard_map/ppermute | solution.py:42
  93.4 1.1 %collective-permute-done.34.rest_3_ = f32[288,128]{1,0:T(8,128)S(1)} collective-permute-done((f32[288,128]{1,0:T(8,128)S(1)}, f32[288,128]{1,0:T(8,128)S(1)}, u32[]{:S(2)}, u32[]{:S(2)}) %collective-permute-start.34) | collective-permute-done | bytes 147488 | tf_op jit(solution)/shard_map/ppermute | solution.py:42
  94.5 5.0 %shard_map.62 = (f32[8192,128]{1,0:T(8,128)S(1)}, f32[8192,128]{1,0:T(8,128)}) custom-call(f32[8192,128]{1,0:T(8,128)S(1)} %get-tuple-element.115.w3_in, f32[8192,128]{1,0:T(8,128)S(1)} %get-tuple-element.68.a2, f32[512,128]{1,0:T(8,128)S(1)} %collective-permute-done.30.d3, f32[512,128]{1,0:T(8,128)S(1)} %get-tuple-element.117.p2, ...), custom_call_target="tpu_custom_call", output_to_operand_aliasing={{0}: (0, {})} | custom-call | tf_op jit(solution)/shard_map/pallas_call | solution.py:387
  (45 shorter events, 2.1 us)
Async XLA Ops:
  0.0 17.2 %copy-start = (f32[2,128,128]{2,1,0:T(8,128)S(1)}, f32[2,128,128]{2,1,0:T(8,128)}, u32[]{:S(2)}) copy-start(f32[2,128,128]{2,1,0:T(8,128)} %weights.1) | copy-start | bytes 393220
  3.5 9.2 %collective-permute-start.3 = (f32[256,128]{1,0:T(8,128)S(1)}, f32[256,128]{1,0:T(8,128)S(1)}, u32[]{:S(2)}, u32[]{:S(2)}) collective-permute-start(f32[256,128]{1,0:T(8,128)S(1)} %get-tuple-element.72), channel_id=1, source_target_pairs={{1,2},{2,1},{3,4},{4,3},{5,6},{6,5},{7,0},{0,7},{9,10},{10,9},{11,... | collective-permute-start | bytes 393224 | tf_op jit(solution)/shard_map/ppermute | solution.py:42
  8.6 13.0 %collective-permute-start = (f32[528,128]{1,0:T(8,128)S(1)}, f32[528,128]{1,0:T(8,128)S(1)}, u32[]{:S(2)}, u32[]{:S(2)}) collective-permute-start(f32[528,128]{1,0:T(8,128)S(1)} %get-tuple-element.69), channel_id=1, source_target_pairs={{32,64},{64,32},{96,0},{0,96},{33,65},{65,33},{97,1},{1,97},{34,66... | collective-permute-start | bytes 811016 | tf_op jit(solution)/shard_map/ppermute | solution.py:42
  10.7 6.4 %collective-permute-start.4 = (f32[256,128]{1,0:T(8,128)S(1)}, f32[256,128]{1,0:T(8,128)S(1)}, u32[]{:S(2)}, u32[]{:S(2)}) collective-permute-start(f32[256,128]{1,0:T(8,128)S(1)} %get-tuple-element.73), channel_id=1, source_target_pairs={{0,1},{1,0},{2,3},{3,2},{4,5},{5,4},{6,7},{7,6},{8,9},{9,8},{10,11... | collective-permute-start | bytes 393224 | tf_op jit(solution)/shard_map/ppermute | solution.py:42
  10.7 9.2 %collective-permute-start.1 = (f32[512,128]{1,0:T(8,128)S(1)}, f32[512,128]{1,0:T(8,128)S(1)}, u32[]{:S(2)}, u32[]{:S(2)}) collective-permute-start(f32[512,128]{1,0:T(8,128)S(1)} %get-tuple-element.70), channel_id=1, source_target_pairs={{0,8},{8,0},{16,24},{24,16},{1,9},{9,1},{17,25},{25,17},{2,10},{10... | collective-permute-start | bytes 786440 | tf_op jit(solution)/shard_map/ppermute | solution.py:42
  11.5 10.1 %collective-permute-start.2 = (f32[512,128]{1,0:T(8,128)S(1)}, f32[512,128]{1,0:T(8,128)S(1)}, u32[]{:S(2)}, u32[]{:S(2)}) collective-permute-start(f32[512,128]{1,0:T(8,128)S(1)} %get-tuple-element.71), channel_id=1, source_target_pairs={{8,16},{16,8},{24,0},{0,24},{9,17},{17,9},{25,1},{1,25},{10,18},{1... | collective-permute-start | bytes 786440 | tf_op jit(solution)/shard_map/ppermute | solution.py:42
  12.7 9.0 %collective-permute-start.5 = (f32[512,128]{1,0:T(8,128)S(1)}, f32[512,128]{1,0:T(8,128)S(1)}, u32[]{:S(2)}, u32[]{:S(2)}) collective-permute-start(f32[512,128]{1,0:T(8,128)S(1)} %get-tuple-element.74), channel_id=1, source_target_pairs={{0,32},{32,0},{64,96},{96,64},{1,33},{33,1},{65,97},{97,65},{2,34}... | collective-permute-start | bytes 786440 | tf_op jit(solution)/shard_map/ppermute | solution.py:42
  17.0 10.0 %collective-permute-start.6 = (f32[528,128]{1,0:T(8,128)S(1)}, f32[528,128]{1,0:T(8,128)S(1)}, u32[]{:S(2)}, u32[]{:S(2)}) collective-permute-start(f32[528,128]{1,0:T(8,128)S(1)} %get-tuple-element.77), channel_id=1, source_target_pairs={{32,64},{64,32},{96,0},{0,96},{33,65},{65,33},{97,1},{1,97},{34,66... | collective-permute-start | bytes 811016 | tf_op jit(solution)/shard_map/ppermute | solution.py:42
  22.7 12.6 %collective-permute-start.7 = (f32[544,128]{1,0:T(8,128)S(1)}, f32[544,128]{1,0:T(8,128)S(1)}, u32[]{:S(2)}, u32[]{:S(2)}) collective-permute-start(f32[544,128]{1,0:T(8,128)S(1)} %get-tuple-element.79), channel_id=1, source_target_pairs={{0,8},{8,0},{16,24},{24,16},{1,9},{9,1},{17,25},{25,17},{2,10},{10... | collective-permute-start | bytes 835592 | tf_op jit(solution)/shard_map/ppermute | solution.py:42
  22.8 12.6 %collective-permute-start.8 = (f32[544,128]{1,0:T(8,128)S(1)}, f32[544,128]{1,0:T(8,128)S(1)}, u32[]{:S(2)}, u32[]{:S(2)}) collective-permute-start(f32[544,128]{1,0:T(8,128)S(1)} %get-tuple-element.80), channel_id=1, source_target_pairs={{8,16},{16,8},{24,0},{0,24},{9,17},{17,9},{25,1},{1,25},{10,18},{1... | collective-permute-start | bytes 835592 | tf_op jit(solution)/shard_map/ppermute | solution.py:42
  24.0 11.3 %collective-permute-start.11 = (f32[512,128]{1,0:T(8,128)S(1)}, f32[512,128]{1,0:T(8,128)S(1)}, u32[]{:S(2)}, u32[]{:S(2)}) collective-permute-start(f32[512,128]{1,0:T(8,128)S(1)} %get-tuple-element.83), channel_id=1, source_target_pairs={{0,32},{32,0},{64,96},{96,64},{1,33},{33,1},{65,97},{97,65},{2,34}... | collective-permute-start | bytes 786440 | tf_op jit(solution)/shard_map/ppermute | solution.py:42
  24.0 8.2 %collective-permute-start.9 = (f32[272,128]{1,0:T(8,128)S(1)}, f32[272,128]{1,0:T(8,128)S(1)}, u32[]{:S(2)}, u32[]{:S(2)}) collective-permute-start(f32[272,128]{1,0:T(8,128)S(1)} %get-tuple-element.81), channel_id=1, source_target_pairs={{1,2},{2,1},{3,4},{4,3},{5,6},{6,5},{7,0},{0,7},{9,10},{10,9},{11,... | collective-permute-start | bytes 417800 | tf_op jit(solution)/shard_map/ppermute | solution.py:42
  27.1 8.3 %collective-permute-start.10 = (f32[272,128]{1,0:T(8,128)S(1)}, f32[272,128]{1,0:T(8,128)S(1)}, u32[]{:S(2)}, u32[]{:S(2)}) collective-permute-start(f32[272,128]{1,0:T(8,128)S(1)} %get-tuple-element.82), channel_id=1, source_target_pairs={{0,1},{1,0},{2,3},{3,2},{4,5},{5,4},{6,7},{7,6},{8,9},{9,8},{10,11... | collective-permute-start | bytes 417800 | tf_op jit(solution)/shard_map/ppermute | solution.py:42
  32.2 9.9 %collective-permute-start.12 = (f32[512,128]{1,0:T(8,128)S(1)}, f32[512,128]{1,0:T(8,128)S(1)}, u32[]{:S(2)}, u32[]{:S(2)}) collective-permute-start(f32[512,128]{1,0:T(8,128)S(1)} %get-tuple-element.87), channel_id=1, source_target_pairs={{32,64},{64,32},{96,0},{0,96},{33,65},{65,33},{97,1},{1,97},{34,66... | collective-permute-start | bytes 786440 | tf_op jit(solution)/shard_map/ppermute | solution.py:42
  36.6 11.3 %collective-permute-start.13 = (f32[576,128]{1,0:T(8,128)S(1)}, f32[576,128]{1,0:T(8,128)S(1)}, u32[]{:S(2)}, u32[]{:S(2)}) collective-permute-start(f32[576,128]{1,0:T(8,128)S(1)} %get-tuple-element.91), channel_id=1, source_target_pairs={{0,8},{8,0},{16,24},{24,16},{1,9},{9,1},{17,25},{25,17},{2,10},{10... | collective-permute-start | bytes 884744 | tf_op jit(solution)/shard_map/ppermute | solution.py:42
  36.7 11.1 %collective-permute-start.14 = (f32[576,128]{1,0:T(8,128)S(1)}, f32[576,128]{1,0:T(8,128)S(1)}, u32[]{:S(2)}, u32[]{:S(2)}) collective-permute-start(f32[576,128]{1,0:T(8,128)S(1)} %get-tuple-element.92), channel_id=1, source_target_pairs={{8,16},{16,8},{24,0},{0,24},{9,17},{17,9},{25,1},{1,25},{10,18},{1... | collective-permute-start | bytes 884744 | tf_op jit(solution)/shard_map/ppermute | solution.py:42
  39.3 8.5 %collective-permute-start.17 = (f32[512,128]{1,0:T(8,128)S(1)}, f32[512,128]{1,0:T(8,128)S(1)}, u32[]{:S(2)}, u32[]{:S(2)}) collective-permute-start(f32[512,128]{1,0:T(8,128)S(1)} %get-tuple-element.95), channel_id=1, source_target_pairs={{0,32},{32,0},{64,96},{96,64},{1,33},{33,1},{65,97},{97,65},{2,34}... | collective-permute-start | bytes 786440 | tf_op jit(solution)/shard_map/ppermute | solution.py:42
  39.6 8.1 %collective-permute-start.15 = (f32[288,128]{1,0:T(8,128)S(1)}, f32[288,128]{1,0:T(8,128)S(1)}, u32[]{:S(2)}, u32[]{:S(2)}) collective-permute-start(f32[288,128]{1,0:T(8,128)S(1)} %get-tuple-element.93), channel_id=1, source_target_pairs={{1,2},{2,1},{3,4},{4,3},{5,6},{6,5},{7,0},{0,7},{9,10},{10,9},{11,... | collective-permute-start | bytes 442376 | tf_op jit(solution)/shard_map/ppermute | solution.py:42
  42.2 5.7 %collective-permute-start.16 = (f32[288,128]{1,0:T(8,128)S(1)}, f32[288,128]{1,0:T(8,128)S(1)}, u32[]{:S(2)}, u32[]{:S(2)}) collective-permute-start(f32[288,128]{1,0:T(8,128)S(1)} %get-tuple-element.94), channel_id=1, source_target_pairs={{0,1},{1,0},{2,3},{3,2},{4,5},{5,4},{6,7},{7,6},{8,9},{9,8},{10,11... | collective-permute-start | bytes 442376 | tf_op jit(solution)/shard_map/ppermute | solution.py:42
  42.4 5.5 %copy-start.1 = (f32[2,4,128]{2,1,0:T(4,128)S(1)}, f32[2,4,128]{2,1,0:T(4,128)}, u32[]{:S(2)}) copy-start(f32[2,4,128]{2,1,0:T(4,128)} %thetas.5) | copy-start | bytes 12292
  51.1 7.9 %collective-permute-start.21 = (f32[256,128]{1,0:T(8,128)S(1)}, f32[256,128]{1,0:T(8,128)S(1)}, u32[]{:S(2)}, u32[]{:S(2)}) collective-permute-start(f32[256,128]{1,0:T(8,128)S(1)} %get-tuple-element.101), channel_id=1, source_target_pairs={{1,2},{2,1},{3,4},{4,3},{5,6},{6,5},{7,0},{0,7},{9,10},{10,9},{11,... | collective-permute-start | bytes 393224 | tf_op jit(solution)/shard_map/ppermute | solution.py:42
  52.8 12.8 %collective-permute-start.18 = (f32[512,128]{1,0:T(8,128)S(1)}, f32[512,128]{1,0:T(8,128)S(1)}, u32[]{:S(2)}, u32[]{:S(2)}) collective-permute-start(f32[512,128]{1,0:T(8,128)S(1)} %get-tuple-element.98), channel_id=1, source_target_pairs={{32,64},{64,32},{96,0},{0,96},{33,65},{65,33},{97,1},{1,97},{34,66... | collective-permute-start | bytes 786440 | tf_op jit(solution)/shard_map/ppermute | solution.py:42
  53.5 12.1 %collective-permute-start.19 = (f32[512,128]{1,0:T(8,128)S(1)}, f32[512,128]{1,0:T(8,128)S(1)}, u32[]{:S(2)}, u32[]{:S(2)}) collective-permute-start(f32[512,128]{1,0:T(8,128)S(1)} %get-tuple-element.99), channel_id=1, source_target_pairs={{0,8},{8,0},{16,24},{24,16},{1,9},{9,1},{17,25},{25,17},{2,10},{10... | collective-permute-start | bytes 786440 | tf_op jit(solution)/shard_map/ppermute | solution.py:42
  53.9 11.6 %collective-permute-start.20 = (f32[512,128]{1,0:T(8,128)S(1)}, f32[512,128]{1,0:T(8,128)S(1)}, u32[]{:S(2)}, u32[]{:S(2)}) collective-permute-start(f32[512,128]{1,0:T(8,128)S(1)} %get-tuple-element.100), channel_id=1, source_target_pairs={{8,16},{16,8},{24,0},{0,24},{9,17},{17,9},{25,1},{1,25},{10,18},{1... | collective-permute-start | bytes 786440 | tf_op jit(solution)/shard_map/ppermute | solution.py:42
  56.0 9.6 %collective-permute-start.23 = (f32[512,128]{1,0:T(8,128)S(1)}, f32[512,128]{1,0:T(8,128)S(1)}, u32[]{:S(2)}, u32[]{:S(2)}) collective-permute-start(f32[512,128]{1,0:T(8,128)S(1)} %get-tuple-element.103), channel_id=1, source_target_pairs={{0,32},{32,0},{64,96},{96,64},{1,33},{33,1},{65,97},{97,65},{2,34}... | collective-permute-start | bytes 786440 | tf_op jit(solution)/shard_map/ppermute | solution.py:42
  59.0 5.0 %collective-permute-start.22 = (f32[256,128]{1,0:T(8,128)S(1)}, f32[256,128]{1,0:T(8,128)S(1)}, u32[]{:S(2)}, u32[]{:S(2)}) collective-permute-start(f32[256,128]{1,0:T(8,128)S(1)} %get-tuple-element.102), channel_id=1, source_target_pairs={{0,1},{1,0},{2,3},{3,2},{4,5},{5,4},{6,7},{7,6},{8,9},{9,8},{10,11... | collective-permute-start | bytes 393224 | tf_op jit(solution)/shard_map/ppermute | solution.py:42
  64.0 9.2 %collective-permute-start.24 = (f32[512,128]{1,0:T(8,128)S(1)}, f32[512,128]{1,0:T(8,128)S(1)}, u32[]{:S(2)}, u32[]{:S(2)}) collective-permute-start(f32[512,128]{1,0:T(8,128)S(1)} %get-tuple-element.106), channel_id=1, source_target_pairs={{32,64},{64,32},{96,0},{0,96},{33,65},{65,33},{97,1},{1,97},{34,66... | collective-permute-start | bytes 786440 | tf_op jit(solution)/shard_map/ppermute | solution.py:42
  66.7 15.2 %collective-permute-start.25 = (f32[544,128]{1,0:T(8,128)S(1)}, f32[544,128]{1,0:T(8,128)S(1)}, u32[]{:S(2)}, u32[]{:S(2)}) collective-permute-start(f32[544,128]{1,0:T(8,128)S(1)} %get-tuple-element.108), channel_id=1, source_target_pairs={{0,8},{8,0},{16,24},{24,16},{1,9},{9,1},{17,25},{25,17},{2,10},{10... | collective-permute-start | bytes 835592 | tf_op jit(solution)/shard_map/ppermute | solution.py:42
  68.7 13.2 %collective-permute-start.26 = (f32[544,128]{1,0:T(8,128)S(1)}, f32[544,128]{1,0:T(8,128)S(1)}, u32[]{:S(2)}, u32[]{:S(2)}) collective-permute-start(f32[544,128]{1,0:T(8,128)S(1)} %get-tuple-element.109), channel_id=1, source_target_pairs={{8,16},{16,8},{24,0},{0,24},{9,17},{17,9},{25,1},{1,25},{10,18},{1... | collective-permute-start | bytes 835592 | tf_op jit(solution)/shard_map/ppermute | solution.py:42
  70.7 11.1 %collective-permute-start.29 = (f32[512,128]{1,0:T(8,128)S(1)}, f32[512,128]{1,0:T(8,128)S(1)}, u32[]{:S(2)}, u32[]{:S(2)}) collective-permute-start(f32[512,128]{1,0:T(8,128)S(1)} %get-tuple-element.112), channel_id=1, source_target_pairs={{0,32},{32,0},{64,96},{96,64},{1,33},{33,1},{65,97},{97,65},{2,34}... | collective-permute-start | bytes 786440 | tf_op jit(solution)/shard_map/ppermute | solution.py:42
  70.8 8.2 %collective-permute-start.27 = (f32[272,128]{1,0:T(8,128)S(1)}, f32[272,128]{1,0:T(8,128)S(1)}, u32[]{:S(2)}, u32[]{:S(2)}) collective-permute-start(f32[272,128]{1,0:T(8,128)S(1)} %get-tuple-element.110), channel_id=1, source_target_pairs={{1,2},{2,1},{3,4},{4,3},{5,6},{6,5},{7,0},{0,7},{9,10},{10,9},{11,... | collective-permute-start | bytes 417800 | tf_op jit(solution)/shard_map/ppermute | solution.py:42
  73.2 8.7 %collective-permute-start.28 = (f32[272,128]{1,0:T(8,128)S(1)}, f32[272,128]{1,0:T(8,128)S(1)}, u32[]{:S(2)}, u32[]{:S(2)}) collective-permute-start(f32[272,128]{1,0:T(8,128)S(1)} %get-tuple-element.111), channel_id=1, source_target_pairs={{0,1},{1,0},{2,3},{3,2},{4,5},{5,4},{6,7},{7,6},{8,9},{9,8},{10,11... | collective-permute-start | bytes 417800 | tf_op jit(solution)/shard_map/ppermute | solution.py:42
  78.9 9.9 %collective-permute-start.30 = (f32[512,128]{1,0:T(8,128)S(1)}, f32[512,128]{1,0:T(8,128)S(1)}, u32[]{:S(2)}, u32[]{:S(2)}) collective-permute-start(f32[512,128]{1,0:T(8,128)S(1)} %get-tuple-element.116), channel_id=1, source_target_pairs={{32,64},{64,32},{96,0},{0,96},{33,65},{65,33},{97,1},{1,97},{34,66... | collective-permute-start | bytes 786440 | tf_op jit(solution)/shard_map/ppermute | solution.py:42
  83.1 11.4 %collective-permute-start.31 = (f32[576,128]{1,0:T(8,128)S(1)}, f32[576,128]{1,0:T(8,128)S(1)}, u32[]{:S(2)}, u32[]{:S(2)}) collective-permute-start(f32[576,128]{1,0:T(8,128)S(1)} %get-tuple-element.119), channel_id=1, source_target_pairs={{0,8},{8,0},{16,24},{24,16},{1,9},{9,1},{17,25},{25,17},{2,10},{10... | collective-permute-start | bytes 884744 | tf_op jit(solution)/shard_map/ppermute | solution.py:42
  83.2 11.3 %collective-permute-start.32 = (f32[576,128]{1,0:T(8,128)S(1)}, f32[576,128]{1,0:T(8,128)S(1)}, u32[]{:S(2)}, u32[]{:S(2)}) collective-permute-start(f32[576,128]{1,0:T(8,128)S(1)} %get-tuple-element.120), channel_id=1, source_target_pairs={{8,16},{16,8},{24,0},{0,24},{9,17},{17,9},{25,1},{1,25},{10,18},{1... | collective-permute-start | bytes 884744 | tf_op jit(solution)/shard_map/ppermute | solution.py:42
  84.5 10.0 %collective-permute-start.35 = (f32[512,128]{1,0:T(8,128)S(1)}, f32[512,128]{1,0:T(8,128)S(1)}, u32[]{:S(2)}, u32[]{:S(2)}) collective-permute-start(f32[512,128]{1,0:T(8,128)S(1)} %get-tuple-element.123), channel_id=1, source_target_pairs={{0,32},{32,0},{64,96},{96,64},{1,33},{33,1},{65,97},{97,65},{2,34}... | collective-permute-start | bytes 786440 | tf_op jit(solution)/shard_map/ppermute | solution.py:42
  85.6 7.9 %collective-permute-start.33 = (f32[288,128]{1,0:T(8,128)S(1)}, f32[288,128]{1,0:T(8,128)S(1)}, u32[]{:S(2)}, u32[]{:S(2)}) collective-permute-start(f32[288,128]{1,0:T(8,128)S(1)} %get-tuple-element.121), channel_id=1, source_target_pairs={{1,2},{2,1},{3,4},{4,3},{5,6},{6,5},{7,0},{0,7},{9,10},{10,9},{11,... | collective-permute-start | bytes 442376 | tf_op jit(solution)/shard_map/ppermute | solution.py:42
  88.8 5.7 %collective-permute-start.34 = (f32[288,128]{1,0:T(8,128)S(1)}, f32[288,128]{1,0:T(8,128)S(1)}, u32[]{:S(2)}, u32[]{:S(2)}) collective-permute-start(f32[288,128]{1,0:T(8,128)S(1)} %get-tuple-element.122), channel_id=1, source_target_pairs={{0,1},{1,0},{2,3},{3,2},{4,5},{5,4},{6,7},{7,6},{8,9},{9,8},{10,11... | collective-permute-start | bytes 442376 | tf_op jit(solution)/shard_map/ppermute | solution.py:42

commit v2 on v1

--- a/solution.py
+++ b/solution.py
@@ -16,7 +16,6 @@
 LINE = {"gy": NZ, "gz": NY}
 CROSS = ("gx", 1)
 LOCALS = (("gy", 0), ("gy", 1), ("gz", 1), ("gz", 0), ("gx", 0))
-FACE_ROWS = 2 * (FACE["gy"] + FACE["gz"])
 SCALES = 16
 
 F32 = jnp.float32
@@ -101,20 +100,20 @@
     return [range(g, g + size) for g in range(0, NX, size)]
 
 
-def emit_face(w, axis, kind, send, only=None):
+def emit_face(w, axis, kind, send):
     at = face_slices(axis, kind)
-    for group in batches(axis) if only is None else [only]:
+    for group in batches(axis):
         got = [w[at(i)[0], :] for i in group]
         for i, v in zip(group, got):
             send[at(i)[1], :] = v
 
 
-def fix_faces(half, w, a2, halos, cross, sends=None):
-    todo = [(a, k, h, None if sends is None else s) for (a, k), h, s in zip(LOCALS, halos, sends or [None] * 5)]
-    order = [t for t in todo if t[0] == "gz"] + [t for t in todo if t[0] == "gy"]
-    for axis, kind, halo, send in order + [(*CROSS, cross, None), todo[-1]]:
-        at = face_slices(axis, kind)
-        for group in batches(axis):
+def fix_faces(half, w, a2, zfaces, halos, cross, sends):
+    local = list(zip(LOCALS, halos, sends))
+    plain = [(CROSS, cross)] + [(k, h) for k, h, _ in local if k[0] == "gx"] + [(k, h) for k, h, _ in local if k[0] == "gy"]
+    for key, halo in plain:
+        at = face_slices(*key)
+        for group in batches(key[0]):
             got = []
             for i in group:
                 dst, src = at(i)
@@ -122,10 +121,20 @@
                 got.append(w[dst, :] + (0.5 * r if half else r))
             for i, v in zip(group, got):
                 w[at(i)[0], :] = v
-                if send is not None and axis != "gz":
-                    send[at(i)[1], :] = v
-    for axis, kind, _, send in order if sends else ():
-        emit_face(w, axis, kind, send, (0, NX - 1) if axis == "gy" else None)
+    for ((key, halo, send), face) in zip([t for t in local if t[0][0] == "gz"], zfaces):
+        at = face_slices(*key)
+        for group in batches("gz"):
+            got = []
+            for i in group:
+                dst, src = at(i)
+                r = face[src, :] * halo[src, :]
+                got.append(w[dst, :] + (0.5 * r if half else r))
+            for i, v in zip(group, got):
+                w[at(i)[0], :] = v
+                send[at(i)[1], :] = v
+    for (axis, kind), _, send in local:
+        if axis != "gz" and send is not None:
+            emit_face(w, axis, kind, send)
 
 
 def emit_ghost_lines(ghosts, sends):
@@ -212,7 +221,39 @@
         emit(j, jnp.broadcast_to(st[:NZ, j : j + 1], (NZ, C)))
 
 
-def start_kernel(feat, scales, fv, sb, d1, d2, d3, *rest):
+def fill_cross(d, depth, values, sv):
+    base = cross_base(depth)
+    for i in range(PLANE // 128):
+        rows = pl.ds(pl.multiple_of(base + i * 128, 128), 128)
+        d[pl.ds(i * 128, 128), :] = values(rows)
+    if sv is not None:
+        up = side(*CROSS)
+        d[PLANE:, :] = jnp.zeros((SCALES, C), F32)
+        d[PLANE:, :NZ] = sv[up * (NX - depth) + (1 - up) * (depth - 1)]
+
+
+def first_kernel(feat, scales, d1, buf, sv, sems):
+    up = side(*CROSS)
+    two = [
+        pltpu.make_async_copy(scales.at[up * (NX - 1)], sv, sems.at[0]),
+        pltpu.make_async_copy(feat.at[pl.ds(cross_base(1), PLANE), :], buf, sems.at[1]),
+    ]
+    for c in two:
+        c.start()
+    two[0].wait()
+    tile = sv[...]
+    d1[PLANE:, :] = jnp.zeros((SCALES, C), F32)
+    d1[PLANE:, :NZ] = tile
+    two[1].wait()
+
+    def emit(j, b):
+        rows = pl.ds(j * NZ, NZ)
+        d1[rows, :] = b * buf[rows, :]
+
+    spread(tile, emit)
+
+
+def start_kernel(feat, scales, fv, sb, d2, d3, *rest):
     sends, (sv, sems) = rest[:5], rest[5:]
     first = pltpu.make_async_copy(scales, sv, sems.at[NX])
     first.start()
@@ -232,15 +273,8 @@
         spread(sv[i], emit)
     for i in range(NX):
         copy(i).wait()
-    up = side(*CROSS)
-    for depth, d in ((1, d1), (2, d2), (3, d3)):
-        base = cross_base(depth)
-        for i in range(PLANE // 128):
-            rows = pl.ds(pl.multiple_of(base + i * 128, 128), 128)
-            d[pl.ds(i * 128, 128), :] = sb[rows, :] * fv[rows, :]
-        if depth < 3:
-            d[PLANE:, :] = jnp.zeros((SCALES, C), F32)
-            d[PLANE:, :NZ] = sv[up * (NX - depth) + (1 - up) * (depth - 1)]
+    fill_cross(d2, 2, lambda rows: sb[rows, :] * fv[rows, :], sv)
+    fill_cross(d3, 3, lambda rows: sb[rows, :] * fv[rows, :], None)
     for (axis, kind), send in zip(LOCALS, sends):
         at = face_slices(axis, kind)
         for group in batches(axis):
@@ -249,7 +283,7 @@
                 send[at(i)[1], :] = v
 
 
-def aux_kernel(sb, fv, weights, w0, a2, w4):
+def aux_kernel(sb, fv, weights, w0, a2, w4, *faces):
     def body(i):
         rows = pl.ds(pl.multiple_of(i * 128, 128), 128)
         s = sb[rows, :]
@@ -257,6 +291,8 @@
         a2[rows, :] = -2.0 * (s * s)
 
     loop(ROWS // 128, body, 1)
+    for (axis, kind), face in zip(LOCALS, faces):
+        emit_face(a2, axis, kind, face)
     for layer in range(2):
         w = weights[layer]
         hi = w.astype(jnp.bfloat16)
@@ -288,26 +324,26 @@
     ghost_pass(False, w1g1, w1, cross_base(1), a2g1, d1, q1)
 
 
-def fix1_kernel(w_in, a2, d1, *rest):
+def fix1_kernel(w_in, a2, z1, z0, d1, *rest):
     halos, w, sends = rest[:5], rest[5], rest[6:]
-    fix_faces(True, w, a2, halos, d1, sends)
+    fix_faces(True, w, a2, (z1, z0), halos, d1, sends)
     emit_ghost_lines((d1,), sends)
 
 
-def fix2_kernel(w_in, a2, d2, p1, a2g1, *rest):
+def fix2_kernel(w_in, a2, z1, z0, d2, p1, a2g1, *rest):
     halos, w, w1g1, sends = rest[:5], rest[5], rest[6], rest[7:]
     ghost_add(True, p1, a2g1, d2, w1g1)
     fix_lines(True, w1g1, a2g1, halos, 0)
-    fix_faces(False, w, a2, halos, w1g1, sends)
+    fix_faces(False, w, a2, (z1, z0), halos, w1g1, sends)
     emit_ghost_lines((w1g1, d2), sends)
 
 
-def fix3(w, a2, d3, p2, q1, a2g1, a2g2, halos, g2, g1):
+def fix3(w, a2, zfaces, d3, p2, q1, a2g1, a2g2, halos, g2, g1, faces):
     ghost_add(True, p2, a2g2, d3, g2)
     fix_lines(True, g2, a2g2, halos, 1)
     ghost_add(False, q1, a2g1, g2, g1)
     fix_lines(False, g1, a2g1, halos, 0)
-    fix_faces(False, w, a2, halos, g1)
+    fix_faces(False, w, a2, zfaces, halos, g1, (*faces, None))
 
 
 def mixed(layer, ws, a2, thetas, w4, rows, scaled):
@@ -325,62 +361,80 @@
     return (q * r) * out if scaled else out
 
 
-def face_mix_kernel(layer, w3_in, a2, d3, p2, q1, a2g1, a2g2, w0, w1, w2, thetas, w4, *rest):
-    halos, w3, d1, sends, (g2, g1, ft) = rest[:5], rest[5], rest[6], rest[7:12], rest[12:]
-    fix3(w3, a2, d3, p2, q1, a2g1, a2g2, halos, g2, g1)
-    ws = (w0, w1, w2, w3)
-    at_row = 0
-    for (axis, kind), send in zip(LOCALS, sends):
-        if axis == "gx":
-            continue
+def mix_planes(layer, ws, a2, thetas, w4, key, dst, scaled, at=0):
+    base = side(*key) * ((NX - 1) * PLANE)
+    for i in range(PLANE // 256):
+        rows = pl.ds(pl.multiple_of(base + i * 256, 256), 256)
+        dst[pl.ds(at + i * 256, 256), :] = mixed(layer, ws, a2, thetas, w4, rows, scaled)
+
+
+def cross_mix_kernel(layer, w3_in, a2, z1, z0, d3, p2, q1, a2g1, a2g2, w0, w1, w2, thetas, w4, *rest):
+    halos, w3, d1, faces, (g2, g1) = rest[:5], rest[5], rest[6], rest[7:11], rest[11:]
+    fix3(w3, a2, (z1, z0), d3, p2, q1, a2g1, a2g2, halos, g2, g1, faces)
+    mix_planes(layer, (w0, w1, w2, w3), a2, thetas, w4, CROSS, d1, True)
+
+
+def mix_faces(layer, f, thetas, w4, outs, scaled):
+    for (axis, _), (*ws, a2), out in zip(LOCALS, f, outs):
+        for i in range(FACE[axis] // 256):
+            rows = pl.ds(i * 256, 256)
+            out[rows, :] = mixed(layer, ws, a2, thetas, w4, rows, scaled)
+
+
+def face_mix_kernel(layer, a2, w0, w1, w2, w3, thetas, w4, *rest):
+    f, sends = [rest[i :20:4] for i in range(4)], rest[20:]
+    mix_faces(layer, f, thetas, w4, sends, True)
+    mix_planes(layer, (w0, w1, w2, w3), a2, thetas, w4, LOCALS[-1], sends[-1], True)
+
+
+def inner_mix_kernel(layer, scaled, w0, w1, w2, w3, a2, thetas, w4, out):
+    def body(i):
+        rows = pl.ds(pl.multiple_of(PLANE + i * 256, 256), 256)
+        out[rows, :] = mixed(layer, (w0, w1, w2, w3), a2, thetas, w4, rows, scaled)
+
+    loop((ROWS - 2 * PLANE) // 256, body, 4)
+
+
+def put_faces(out, faces):
+    for (axis, kind), face in zip(LOCALS, faces):
         at = face_slices(axis, kind)
         for group in batches(axis):
-            for k, w in enumerate(ws + (a2,)):
-                got = [w[at(i)[0], :] for i in group]
-                for i, v in zip(group, got):
-                    ft[k, pl.ds(at_row + i * LINE[axis], LINE[axis]), :] = v
-        at_row += FACE[axis]
-    for axis, kind, send in ((*CROSS, d1), (*LOCALS[-1], sends[-1])):
-        base = side(axis, kind) * ((NX - 1) * PLANE)
-        for i in range(PLANE // 256):
-            rows = pl.ds(pl.multiple_of(base + i * 256, 256), 256)
-            send[pl.ds(i * 256, 256), :] = mixed(layer, ws, a2, thetas, w4, rows, True)
-    at_row = 0
-    fts = tuple(ft.at[k] for k in range(4))
-    for (axis, kind), send in zip(LOCALS[:-1], sends):
-        for i in range(FACE[axis] // 256):
-            rows = pl.ds(at_row + i * 256, 256)
-            send[pl.ds(i * 256, 256), :] = mixed(layer, fts, ft.at[4], thetas, w4, rows, True)
-        at_row += FACE[axis]
-
-
-def mix_kernel(layer, w0, w1, w2, w3, a2, thetas, w4, out, d2, d3):
-    def body(i):
-        rows = pl.ds(pl.multiple_of(i * 256, 256), 256)
-        out[rows, :] = mixed(layer, (w0, w1, w2, w3), a2, thetas, w4, rows, True)
-
-    loop(ROWS // 256, body, 4)
+            got = [face[at(i)[1], :] for i in group]
+            for i, v in zip(group, got):
+                out[at(i)[0], :] = v
+
+
+def merge_kernel(inner, d1, *rest):
+    sends, out, d2, d3 = rest[:5], *rest[5:]
+    put_faces(out, sends)
+    base = cross_base(1)
+    for i in range(PLANE // 128):
+        out[pl.ds(pl.multiple_of(base + i * 128, 128), 128), :] = d1[pl.ds(i * 128, 128), :]
     copy_plane(out, cross_base(2), d2)
     copy_plane(out, cross_base(3), d3)
 
 
-def last_kernel(layer, w3_in, a2, d3, p2, q1, a2g1, a2g2, w0, w1, w2, thetas, w4, *rest):
-    halos, (w3, out), (g2, g1, buf, sems) = rest[:5], rest[5:7], rest[7:]
-    fix3(w3, a2, d3, p2, q1, a2g1, a2g2, halos, g2, g1)
-    step = 1024
+def last_kernel(layer, w3_in, a2, z1, z0, d3, p2, q1, a2g1, a2g2, w0, w1, w2, thetas, w4, inner, *rest):
+    halos, known = rest[:5], rest[5:21]
+    (w3, hidden, out), (g2, g1), faces, done, sems = rest[21:24], rest[24:26], rest[26:30], rest[30:34], rest[34]
+    fix3(w3, a2, (z1, z0), d3, p2, q1, a2g1, a2g2, halos, g2, g1, faces)
 
     def copy(i):
-        rows = pl.ds(pl.multiple_of(i * step, step), step)
-        return pltpu.make_async_copy(buf.at[rows, :], out.at[rows, :], sems.at[i])
-
-    def body(i):
-        for h in range(step // 256):
-            rows = pl.ds(pl.multiple_of(i * step + h * 256, 256), 256)
-            buf[rows, :] = mixed(layer, (w0, w1, w2, w3), a2, thetas, w4, rows, False)
+        rows = pl.ds(pl.multiple_of(i * PLANE, PLANE), PLANE)
+        return pltpu.make_async_copy(hidden.at[rows, :], out.at[rows, :], sems.at[i])
+
+    f = [(*known[i:12:4], faces[i], known[12 + i]) for i in range(4)]
+    mix_faces(layer, f, thetas, w4, done, False)
+    put_faces(hidden, done)
+    for i in range(1, NX - 1):
         copy(i).start()
-
-    loop(ROWS // step, body, 1)
-    loop(ROWS // step, lambda i: copy(i).wait(), 1)
+    for i in range(2 * PLANE // 256):
+        plane, part = divmod(i, PLANE // 256)
+        rows = pl.ds(plane * (NX - 1) * PLANE + part * 256, 256)
+        hidden[rows, :] = mixed(layer, (w0, w1, w2, w3), a2, thetas, w4, rows, False)
+    copy(0).start()
+    copy(NX - 1).start()
+    loop(NX, lambda i: copy(i).wait(), 1)
 
 
 def call(kernel, out_shape, args, in_hbm=(), out_hbm=(), scratch=(), aliases=None, mib=1):
@@ -401,9 +455,16 @@
     block, plane = arr(ROWS), arr(PLANE)
     scales = pltpu.with_memory_space_constraint(scales, pltpu.HBM)
     ghosts = [pltpu.VMEM((PLANE, C), F32)] * 2
-    fv, sb, s1, s2, s3, *sends = call(
+    (s1,) = call(
+        first_kernel,
+        [arr(PLANE + SCALES)],
+        (feat, scales),
+        in_hbm=(0, 1),
+        scratch=[pltpu.VMEM((PLANE, C), F32), pltpu.VMEM((NY, NZ), F32), pltpu.SemaphoreType.DMA((2,))],
+    )
+    fv, sb, s2, s3, *sends = call(
         start_kernel,
-        [block, block, arr(PLANE + SCALES), arr(PLANE + SCALES), plane] + locals_out(0),
+        [block, block, arr(PLANE + SCALES), plane] + locals_out(0),
         (feat, scales),
         in_hbm=(0, 1),
         scratch=[pltpu.VMEM(scales.shape, F32), pltpu.SemaphoreType.DMA((NX + 1,))],
@@ -411,43 +472,54 @@
     for layer in range(2):
         last = layer == 1
         if last:
-            w0, s2, s3 = call(functools.partial(mix_kernel, 0), [block, plane, plane], (w0, w1, w2, w3, a2, thetas, w4))
+            w0, s2, s3 = call(merge_kernel, [block, plane, plane], (inner, s1, *sends), aliases={0: 0})
+        known = [sends[:4]]
         (d1,), halos, (d2,) = exchange(sends, cross=s1, late=s2)
         if not last:
             w4 = jax.ShapeDtypeStruct((2, 2 * C, 2 * C), jnp.bfloat16)
-            w0, a2, w4 = call(aux_kernel, [block, block, w4], (sb, fv, weights))
+            w0, a2, w4, *af = call(aux_kernel, [block, block, w4] + locals_out(0)[:4], (sb, fv, weights))
+            main = (a2, af[2], af[3])
         (w1,) = call(local1_kernel, [block], (w0, a2))
-        w1, *sends = call(fix1_kernel, [block] + locals_out(1), (w1, a2, d1, *halos), aliases={0: 0})
+        w1, *sends = call(fix1_kernel, [block] + locals_out(1), (w1, *main, d1, *halos), aliases={0: 0})
+        known.append(sends[:4])
         _, halos, (d3,) = exchange(sends, late=s3)
         if not last:
             (a2g1,) = call(ghost_aux_kernel, [plane], (d1,))
         w2, p1 = call(local2_kernel, [block, plane], (w1, a2, w0, d1, a2g1))
         w2, w1g1, *sends = call(
-            fix2_kernel, [block, plane] + locals_out(2), (w2, a2, d2, p1, a2g1, *halos), aliases={0: 0}
+            fix2_kernel, [block, plane] + locals_out(2), (w2, *main, d2, p1, a2g1, *halos), aliases={0: 0}
         )
+        known.append(sends[:4])
         _, halos, _ = exchange(sends)
         if not last:
             (a2g2,) = call(ghost_aux_kernel, [plane], (d2,))
         w3, p2, q1 = call(local3_kernel, [block, plane, plane], (w2, a2, w1, d1, d2, w1g1, a2g1, a2g2))
-        tail = (w3, a2, d3, p2, q1, a2g1, a2g2, w0, w1, w2)
+        (inner,) = call(functools.partial(inner_mix_kernel, layer, not last), [block], (w0, w1, w2, w3, a2, thetas, w4))
+        tail = (w3, *main, d3, p2, q1, a2g1, a2g2, w0, w1, w2, thetas, w4)
         if not last:
-            w3, s1, *sends = call(
-                functools.partial(face_mix_kernel, layer),
-                [block, plane] + locals_out(0),
-                (*tail, thetas, w4, *halos),
-                scratch=ghosts + [pltpu.VMEM((5, FACE_ROWS, C), F32)],
-                mib=7,
+            w3, s1, *faces = call(
+                functools.partial(cross_mix_kernel, layer),
+                [block, plane] + locals_out(0)[:4],
+                (*tail, *halos),
+                scratch=ghosts,
                 aliases={0: 0},
             )
+            sends = call(
+                functools.partial(face_mix_kernel, layer),
+                locals_out(0),
+                (a2, w0, w1, w2, w3, thetas, w4, *sum(map(list, known), []), *faces, *af),
+            )
         else:
-            _, out = call(
+            small = [pltpu.VMEM(a.shape, F32) for a in locals_out(0)[:4]]
+            n = len(tail)
+            _, _, out = call(
                 functools.partial(last_kernel, layer),
-                [block, block],
-                (*tail, thetas, w4, *halos),
-                out_hbm=(1,),
-                scratch=ghosts + [pltpu.VMEM((ROWS, C), F32), pltpu.SemaphoreType.DMA((8,))],
-                mib=8,
-                aliases={0: 0},
+                [block, block, block],
+                (*tail, inner, *halos, *sum(map(list, known), []), *af),
+                out_hbm=(2,),
+                scratch=ghosts + small + small + [pltpu.SemaphoreType.DMA((NX,))],
+                mib=3,
+                aliases={0: 0, n: 1},
             )
     return out.reshape(shape)
 

time: 101 us -> 99.6 us (0.986)
  the two profiles are of different devices: /device:TPU:6 before, /device:TPU:1 now
where the time goes in v2:
time: 99.6 us; the launch traced here: 99.4 us
  starting transfers between devices  43.6 us (44%)
  Pallas kernels  30.8 us (31%)
  waiting for transfers between devices  24.5 us (25%)
    ppermute x36, starting transfers between devices, swap(): return lax.ppermute(x, axis, pairs)  43.6 us
    pallas_call x21, Pallas kernels, call(): pl.pallas_call(kernel, out_shape=out_shape, in_specs=[HBM if i in in_hbm...  30.8 us
    ppermute x36, waiting for transfers between devices, swap(): return lax.ppermute(x, axis, pairs)  24.5 us
  transfers between devices with their start and end apart: 36, of which 12 were waited for; matrix products, arithmetic and copies ran while one was open for 0% of the time, Pallas kernels for 22%

profile of v2, /device:TPU:1, one launch (start us, length us, event | category | flops | bytes accessed | tf_op | source)
XLA Modules:
  0.0 99.4 jit_solution(13832669453370199632)
XLA Ops:
  0.0 3.5 %shard_map.46 = (f32[8192,128]{1,0:T(8,128)S(1)}, f32[8192,128]{1,0:T(8,128)S(1)}, f32[528,128]{1,0:T(8,128)S(1)}, f32[512,128]{1,0:T(8,128)S(1)}, f32[512,128]{...) custom-call(f32[8192,128]{1,0:T(8,128)} %bitcast.2, ...), custom_call_target="tpu_custom_call" | custom-call | tf_op jit(solution)/shard_map/pallas_call | solution.py:441
  3.5 5.7 %collective-permute-start.3 = (f32[256,128]{1,0:T(8,128)S(1)}, f32[256,128]{1,0:T(8,128)S(1)}, u32[]{:S(2)}, u32[]{:S(2)}) collective-permute-start(f32[256,128]{1,0:T(8,128)S(1)} %get-tuple-element.80.rest_2_), channel_id=1, source_target_pairs={{1,2},{2,1},{3,4},{4,3},{5,6},{6,5},{7,0},{0,7},{9,10},{10,9},{11,... | collective-permute-start | bytes 393224 | tf_op jit(solution)/shard_map/ppermute | solution.py:41
  9.1 1.2 %shard_map.49 = f32[528,128]{1,0:T(8,128)S(1)} custom-call(f32[8192,128]{1,0:T(8,128)} %bitcast.3, f32[16,16,32]{2,1,0:T(8,128)} %scales.3), custom_call_target="tpu_custom_call" | custom-call | tf_op jit(solution)/shard_map/pallas_call | solution.py:441
  10.4 3.5 %collective-permute-start = (f32[528,128]{1,0:T(8,128)S(1)}, f32[528,128]{1,0:T(8,128)S(1)}, u32[]{:S(2)}, u32[]{:S(2)}) collective-permute-start(f32[528,128]{1,0:T(8,128)S(1)} %shard_map.49), channel_id=1, source_target_pairs={{32,64},{64,32},{96,0},{0,96},{33,65},{65,33},{97,1},{1,97},{34,66... | collective-permute-start | bytes 811016 | tf_op jit(solution)/shard_map/ppermute | solution.py:41
  13.9 1.2 %collective-permute-start.1 = (f32[512,128]{1,0:T(8,128)S(1)}, f32[512,128]{1,0:T(8,128)S(1)}, u32[]{:S(2)}, u32[]{:S(2)}) collective-permute-start(f32[512,128]{1,0:T(8,128)S(1)} %get-tuple-element.78.rest_0_), channel_id=1, source_target_pairs={{0,8},{8,0},{16,24},{24,16},{1,9},{9,1},{17,25},{25,17},{2,10},{10... | collective-permute-start | bytes 786440 | tf_op jit(solution)/shard_map/ppermute | solution.py:41
  15.1 1.8 %collective-permute-start.2 = (f32[512,128]{1,0:T(8,128)S(1)}, f32[512,128]{1,0:T(8,128)S(1)}, u32[]{:S(2)}, u32[]{:S(2)}) collective-permute-start(f32[512,128]{1,0:T(8,128)S(1)} %get-tuple-element.79.rest_1_), channel_id=1, source_target_pairs={{8,16},{16,8},{24,0},{0,24},{9,17},{17,9},{25,1},{1,25},{10,18},{1... | collective-permute-start | bytes 786440 | tf_op jit(solution)/shard_map/ppermute | solution.py:41
  16.9 4.1 %collective-permute-done.4.rest_3_ = f32[256,128]{1,0:T(8,128)S(1)} collective-permute-done((f32[256,128]{1,0:T(8,128)S(1)}, f32[256,128]{1,0:T(8,128)S(1)}, u32[]{:S(2)}, u32[]{:S(2)}) %collective-permute-start.4) | collective-permute-done | bytes 131104 | tf_op jit(solution)/shard_map/ppermute | solution.py:41
  21.1 2.2 %collective-permute-start.6 = (f32[528,128]{1,0:T(8,128)S(1)}, f32[528,128]{1,0:T(8,128)S(1)}, u32[]{:S(2)}, u32[]{:S(2)}) collective-permute-start(f32[528,128]{1,0:T(8,128)S(1)} %get-tuple-element.85), channel_id=1, source_target_pairs={{32,64},{64,32},{96,0},{0,96},{33,65},{65,33},{97,1},{1,97},{34,66... | collective-permute-start | bytes 811016 | tf_op jit(solution)/shard_map/ppermute | solution.py:41
  23.2 1.3 %shard_map.47 = (f32[8192,128]{1,0:T(8,128)S(1)}, f32[8192,128]{1,0:T(8,128)S(1)}, bf16[2,256,256]{2,1,0:T(8,128)(2,1)S(1)}, f32[512,128]{1,0:T(8,128)S(1)}, f32...) custom-call(f32[8192,128]{1,0:T(8,128)S(1)} %get-tuple-element.72.sb, ...), custom_call_target="tpu_custom_call" | custom-call | tf_op jit(solution)/shard_map/pallas_call | solution.py:441
  24.5 1.5 %shard_map.48.w_in = f32[8192,128]{1,0:T(8,128)S(1)} custom-call(f32[8192,128]{1,0:T(8,128)S(1)} %get-tuple-element.74.w0, f32[8192,128]{1,0:T(8,128)S(1)} %get-tuple-element.75.a2), custom_call_target="tpu_custom_call" | custom-call | tf_op jit(solution)/shard_map/pallas_call | solution.py:441
  26.1 0.6 shard_map.50
  27.1 0.6 collective-permute-start.8
  27.9 3.0 %collective-permute-start.9 = (f32[272,128]{1,0:T(8,128)S(1)}, f32[272,128]{1,0:T(8,128)S(1)}, u32[]{:S(2)}, u32[]{:S(2)}) collective-permute-start(f32[272,128]{1,0:T(8,128)S(1)} %get-tuple-element.89.rest_6_), channel_id=1, source_target_pairs={{1,2},{2,1},{3,4},{4,3},{5,6},{6,5},{7,0},{0,7},{9,10},{10,9},{11,... | collective-permute-start | bytes 417800 | tf_op jit(solution)/shard_map/ppermute | solution.py:41
  31.0 4.0 %collective-permute-done.9.rest_2_ = f32[272,128]{1,0:T(8,128)S(1)} collective-permute-done((f32[272,128]{1,0:T(8,128)S(1)}, f32[272,128]{1,0:T(8,128)S(1)}, u32[]{:S(2)}, u32[]{:S(2)}) %collective-permute-start.9) | collective-permute-done | bytes 139296 | tf_op jit(solution)/shard_map/ppermute | solution.py:41
  34.9 3.5 %collective-permute-start.12 = (f32[512,128]{1,0:T(8,128)S(1)}, f32[512,128]{1,0:T(8,128)S(1)}, u32[]{:S(2)}, u32[]{:S(2)}) collective-permute-start(f32[512,128]{1,0:T(8,128)S(1)} %get-tuple-element.96), channel_id=1, source_target_pairs={{32,64},{64,32},{96,0},{0,96},{33,65},{65,33},{97,1},{1,97},{34,66... | collective-permute-start | bytes 786440 | tf_op jit(solution)/shard_map/ppermute | solution.py:41
  38.7 1.6 %shard_map.52 = (f32[8192,128]{1,0:T(8,128)S(1)}, f32[512,128]{1,0:T(8,128)S(1)}) custom-call(f32[8192,128]{1,0:T(8,128)S(1)} %get-tuple-element.83.w1, f32[8192,128]{1,0:T(8,128)S(1)} %get-tuple-element.75.a2, f32[8192,128]{1,0:T(8,128)S(1)} %get-tuple-element.74.w0, f32[528,128]{1,0:T(8,128)S(1)} %collective-permute-done.d1.d, f32[512,128]{1,0:T(8,128)S(1)} %shard_map.51.a2g1), custom_call_target="tpu_custom_call" | custom-call | tf_op jit(solution)/shard_map/pallas_call | solution.py:441
  40.4 0.8 shard_map.53
  41.2 0.8 collective-permute-start.13
  42.0 1.8 %collective-permute-start.14 = (f32[576,128]{1,0:T(8,128)S(1)}, f32[576,128]{1,0:T(8,128)S(1)}, u32[]{:S(2)}, u32[]{:S(2)}) collective-permute-start(f32[576,128]{1,0:T(8,128)S(1)} %get-tuple-element.100.rest_9_), channel_id=1, source_target_pairs={{8,16},{16,8},{24,0},{0,24},{9,17},{17,9},{25,1},{1,25},{10,18},{1... | collective-permute-start | bytes 884744 | tf_op jit(solution)/shard_map/ppermute | solution.py:41
  43.8 1.6 %collective-permute-done.12.d3 = f32[512,128]{1,0:T(8,128)S(1)} collective-permute-done((f32[512,128]{1,0:T(8,128)S(1)}, f32[512,128]{1,0:T(8,128)S(1)}, u32[]{:S(2)}, u32[]{:S(2)}) %collective-permute-start.12) | collective-permute-done | bytes 262176 | tf_op jit(solution)/shard_map/ppermute | solution.py:41
  45.7 1.7 %shard_map.55 = (f32[8192,128]{1,0:T(8,128)S(1)}, f32[512,128]{1,0:T(8,128)S(1)}, f32[512,128]{1,0:T(8,128)S(1)}) custom-call(f32[8192,128]{1,0:T(8,128)S(1)} %get-tuple-element.92.w2, f32[8192,128]{1,0:T(8,128)S(1)} %get-tuple-element.75.a2, f32[8192,128]{1,0:T(8,128)S(1)} %get-tuple-element.83.w1, f32[528,128]{1,0:T(8,128)S(1)} %collective-permute-done.d1.d, ...), custom_call_target="tpu_custom_call" | custom-call | tf_op jit(solution)/shard_map/pallas_call | solution.py:441
  47.4 3.1 %shard_map.56.inner = f32[8192,128]{1,0:T(8,128)S(1)} custom-call(f32[8192,128]{1,0:T(8,128)S(1)} %get-tuple-element.74.w0, f32[8192,128]{1,0:T(8,128)S(1)} %get-tuple-element.83.w1, f32[8192,128]{1,0:T(8,128)S(1)} %get-tuple-element.92.w2, f32[8192,128]{1,0:T(8,128)S(1)} %get-tuple-element.94.w3.w3_in, f32[8192,128]{1,0:T(8,128)S(1)} %get-tuple-element.75.a2, ...), custom_call_target="tpu_custom_call" | custom-call | tf_op jit(solution)/shard_map/pallas_call | solution.py:441
  50.8 1.2 %collective-permute-done.14.rest_1_ = f32[576,128]{1,0:T(8,128)S(1)} collective-permute-done((f32[576,128]{1,0:T(8,128)S(1)}, f32[576,128]{1,0:T(8,128)S(1)}, u32[]{:S(2)}, u32[]{:S(2)}) %collective-permute-start.14) | collective-permute-done | bytes 294944 | tf_op jit(solution)/shard_map/ppermute | solution.py:41
  52.0 1.2 %shard_map.57 = (f32[8192,128]{1,0:T(8,128)S(1)}, f32[512,128]{1,0:T(8,128)S(1)}, f32[512,128]{1,0:T(8,128)S(1)}, f32[512,128]{1,0:T(8,128)S(1)}, f32[256,128]{1,0:T(8,128)S(1)}, /*index=5*/f32[256,128]{1,0:T(8,128)S(1)}) custom-call(f32[8192,128]{1,0:T(8,128)S(1)} %get-tuple-element.94.w3.w3_in, ...), custom_call_target="tpu_custom_call", output_to_operand_aliasing={{0}: (0, {})} | custom-call | tf_op jit(solution)/shard_map/pallas_call | solution.py:441
  53.2 0.9 shard_map.58
  54.0 0.9 collective-permute-start.21
  55.0 1.2 %collective-permute-start.23 = (f32[512,128]{1,0:T(8,128)S(1)}, f32[512,128]{1,0:T(8,128)S(1)}, u32[]{:S(2)}, u32[]{:S(2)}) collective-permute-start(f32[512,128]{1,0:T(8,128)S(1)} %get-tuple-element.116.rest_4_), channel_id=1, source_target_pairs={{0,32},{32,0},{64,96},{96,64},{1,33},{33,1},{65,97},{97,65},{2,34}... | collective-permute-start | bytes 786440 | tf_op jit(solution)/shard_map/ppermute | solution.py:41
  56.5 0.6 collective-permute-start.20
  57.1 3.1 %collective-permute-start.18 = (f32[512,128]{1,0:T(8,128)S(1)}, f32[512,128]{1,0:T(8,128)S(1)}, u32[]{:S(2)}, u32[]{:S(2)}) collective-permute-start(f32[512,128]{1,0:T(8,128)S(1)} %get-tuple-element.104.d1), channel_id=1, source_target_pairs={{32,64},{64,32},{96,0},{0,96},{33,65},{65,33},{97,1},{1,97},{34,66... | collective-permute-start | bytes 786440 | tf_op jit(solution)/shard_map/ppermute | solution.py:41
  60.2 0.7 collective-permute-done.21.rest_2_
  61.3 3.7 %collective-permute-done.22.rest_3_ = f32[256,128]{1,0:T(8,128)S(1)} collective-permute-done((f32[256,128]{1,0:T(8,128)S(1)}, f32[256,128]{1,0:T(8,128)S(1)}, u32[]{:S(2)}, u32[]{:S(2)}) %collective-permute-start.22) | collective-permute-done | bytes 131104 | tf_op jit(solution)/shard_map/ppermute | solution.py:41
  65.0 2.7 %collective-permute-start.24 = (f32[512,128]{1,0:T(8,128)S(1)}, f32[512,128]{1,0:T(8,128)S(1)}, u32[]{:S(2)}, u32[]{:S(2)}) collective-permute-start(f32[512,128]{1,0:T(8,128)S(1)} %get-tuple-element.120), channel_id=1, source_target_pairs={{32,64},{64,32},{96,0},{0,96},{33,65},{65,33},{97,1},{1,97},{34,66... | collective-permute-start | bytes 786440 | tf_op jit(solution)/shard_map/ppermute | solution.py:41
  67.7 1.5 %shard_map.60.w_in = f32[8192,128]{1,0:T(8,128)S(1)} custom-call(f32[8192,128]{1,0:T(8,128)S(1)} %get-tuple-element.117.w0, f32[8192,128]{1,0:T(8,128)S(1)} %get-tuple-element.75.a2), custom_call_target="tpu_custom_call" | custom-call | tf_op jit(solution)/shard_map/pallas_call | solution.py:441
  69.3 0.6 shard_map.61
  70.3 1.8 %collective-permute-start.26 = (f32[544,128]{1,0:T(8,128)S(1)}, f32[544,128]{1,0:T(8,128)S(1)}, u32[]{:S(2)}, u32[]{:S(2)}) collective-permute-start(f32[544,128]{1,0:T(8,128)S(1)} %get-tuple-element.123.rest_10_), channel_id=1, source_target_pairs={{8,16},{16,8},{24,0},{0,24},{9,17},{17,9},{25,1},{1,25},{10,18},{1... | collective-permute-start | bytes 835592 | tf_op jit(solution)/shard_map/ppermute | solution.py:41
  72.1 1.5 %collective-permute-start.27 = (f32[272,128]{1,0:T(8,128)S(1)}, f32[272,128]{1,0:T(8,128)S(1)}, u32[]{:S(2)}, u32[]{:S(2)}) collective-permute-start(f32[272,128]{1,0:T(8,128)S(1)} %get-tuple-element.124.rest_11_), channel_id=1, source_target_pairs={{1,2},{2,1},{3,4},{4,3},{5,6},{6,5},{7,0},{0,7},{9,10},{10,9},{11,... | collective-permute-start | bytes 417800 | tf_op jit(solution)/shard_map/ppermute | solution.py:41
  74.3 4.7 %collective-permute-done.27.rest_2_ = f32[272,128]{1,0:T(8,128)S(1)} collective-permute-done((f32[272,128]{1,0:T(8,128)S(1)}, f32[272,128]{1,0:T(8,128)S(1)}, u32[]{:S(2)}, u32[]{:S(2)}) %collective-permute-start.27) | collective-permute-done | bytes 139296 | tf_op jit(solution)/shard_map/ppermute | solution.py:41
  79.0 3.3 %collective-permute-start.30 = (f32[512,128]{1,0:T(8,128)S(1)}, f32[512,128]{1,0:T(8,128)S(1)}, u32[]{:S(2)}, u32[]{:S(2)}) collective-permute-start(f32[512,128]{1,0:T(8,128)S(1)} %get-tuple-element.130), channel_id=1, source_target_pairs={{32,64},{64,32},{96,0},{0,96},{33,65},{65,33},{97,1},{1,97},{34,66... | collective-permute-start | bytes 786440 | tf_op jit(solution)/shard_map/ppermute | solution.py:41
  82.2 1.6 %shard_map.62 = (f32[8192,128]{1,0:T(8,128)S(1)}, f32[512,128]{1,0:T(8,128)S(1)}) custom-call(f32[8192,128]{1,0:T(8,128)S(1)} %get-tuple-element.118.w1, f32[8192,128]{1,0:T(8,128)S(1)} %get-tuple-element.75.a2, f32[8192,128]{1,0:T(8,128)S(1)} %get-tuple-element.117.w0, f32[512,128]{1,0:T(8,128)S(1)} %collective-permute-done.18.d1, ...), custom_call_target="tpu_custom_call" | custom-call | tf_op jit(solution)/shard_map/pallas_call | solution.py:441
  83.9 0.7 shard_map.63
  84.6 0.8 collective-permute-start.31
  85.5 0.9 collective-permute-start.32
  86.4 0.9 collective-permute-start.33
  87.2 1.5 %collective-permute-done.30.d3 = f32[512,128]{1,0:T(8,128)S(1)} collective-permute-done((f32[512,128]{1,0:T(8,128)S(1)}, f32[512,128]{1,0:T(8,128)S(1)}, u32[]{:S(2)}, u32[]{:S(2)}) %collective-permute-start.30) | collective-permute-done | bytes 262176 | tf_op jit(solution)/shard_map/ppermute | solution.py:41
  88.7 1.7 %shard_map.64 = (f32[8192,128]{1,0:T(8,128)S(1)}, f32[512,128]{1,0:T(8,128)S(1)}, f32[512,128]{1,0:T(8,128)S(1)}) custom-call(f32[8192,128]{1,0:T(8,128)S(1)} %get-tuple-element.127.w2, f32[8192,128]{1,0:T(8,128)S(1)} %get-tuple-element.75.a2, f32[8192,128]{1,0:T(8,128)S(1)} %get-tuple-element.118.w1, f32[512,128]{1,0:T(8,128)S(1)} %collective-permute-done.18.d1, ...), custom_call_target="tpu_custom_call" | custom-call | tf_op jit(solution)/shard_map/pallas_call | solution.py:441
  90.4 2.6 %shard_map.65.inner = f32[8192,128]{1,0:T(8,128)S(1)} custom-call(f32[8192,128]{1,0:T(8,128)S(1)} %get-tuple-element.117.w0, f32[8192,128]{1,0:T(8,128)S(1)} %get-tuple-element.118.w1, f32[8192,128]{1,0:T(8,128)S(1)} %get-tuple-element.127.w2, f32[8192,128]{1,0:T(8,128)S(1)} %get-tuple-element.129.w3.w3_in, f32[8192,128]{1,0:T(8,128)S(1)} %get-tuple-element.75.a2, ...), custom_call_target="tpu_custom_call" | custom-call | tf_op jit(solution)/shard_map/pallas_call | solution.py:441
  93.4 2.1 %collective-permute-done.32.rest_1_ = f32[576,128]{1,0:T(8,128)S(1)} collective-permute-done((f32[576,128]{1,0:T(8,128)S(1)}, f32[576,128]{1,0:T(8,128)S(1)}, u32[]{:S(2)}, u32[]{:S(2)}) %collective-permute-start.32) | collective-permute-done | bytes 294944 | tf_op jit(solution)/shard_map/ppermute | solution.py:41
  95.5 3.8 %shard_map.66 = (f32[8192,128]{1,0:T(8,128)S(1)}, f32[8192,128]{1,0:T(8,128)S(1)}, f32[8192,128]{1,0:T(8,128)}) custom-call(f32[8192,128]{1,0:T(8,128)S(1)} %get-tuple-element.129.w3.w3_in, f32[8192,128]{1,0:T(8,128)S(1)} %get-tuple-element.75.a2, ...), custom_call_target="tpu_custom_call", output_to_operand_aliasing={{0}: (0, {}), {1}: (14, {})} | custom-call | tf_op jit(solution)/shard_map/pallas_call | solution.py:441
  (49 shorter events, 3.5 us)
Async XLA Ops:
  0.0 23.2 %copy-start = (f32[2,128,128]{2,1,0:T(8,128)S(1)}, f32[2,128,128]{2,1,0:T(8,128)}, u32[]{:S(2)}) copy-start(f32[2,128,128]{2,1,0:T(8,128)} %weights.1) | copy-start | bytes 393220
  3.5 13.5 %collective-permute-start.3 = (f32[256,128]{1,0:T(8,128)S(1)}, f32[256,128]{1,0:T(8,128)S(1)}, u32[]{:S(2)}, u32[]{:S(2)}) collective-permute-start(f32[256,128]{1,0:T(8,128)S(1)} %get-tuple-element.80.rest_2_), channel_id=1, source_target_pairs={{1,2},{2,1},{3,4},{4,3},{5,6},{6,5},{7,0},{0,7},{9,10},{10,9},{11,... | collective-permute-start | bytes 393224 | tf_op jit(solution)/shard_map/ppermute | solution.py:41
  10.4 15.7 %collective-permute-start = (f32[528,128]{1,0:T(8,128)S(1)}, f32[528,128]{1,0:T(8,128)S(1)}, u32[]{:S(2)}, u32[]{:S(2)}) collective-permute-start(f32[528,128]{1,0:T(8,128)S(1)} %shard_map.49), channel_id=1, source_target_pairs={{32,64},{64,32},{96,0},{0,96},{33,65},{65,33},{97,1},{1,97},{34,66... | collective-permute-start | bytes 811016 | tf_op jit(solution)/shard_map/ppermute | solution.py:41
  13.9 12.2 %collective-permute-start.5 = (f32[512,128]{1,0:T(8,128)S(1)}, f32[512,128]{1,0:T(8,128)S(1)}, u32[]{:S(2)}, u32[]{:S(2)}) collective-permute-start(f32[512,128]{1,0:T(8,128)S(1)} %get-tuple-element.82), channel_id=1, source_target_pairs={{0,32},{32,0},{64,96},{96,64},{1,33},{33,1},{65,97},{97,65},{2,34}... | collective-permute-start | bytes 786440 | tf_op jit(solution)/shard_map/ppermute | solution.py:41
  13.9 12.2 %collective-permute-start.1 = (f32[512,128]{1,0:T(8,128)S(1)}, f32[512,128]{1,0:T(8,128)S(1)}, u32[]{:S(2)}, u32[]{:S(2)}) collective-permute-start(f32[512,128]{1,0:T(8,128)S(1)} %get-tuple-element.78.rest_0_), channel_id=1, source_target_pairs={{0,8},{8,0},{16,24},{24,16},{1,9},{9,1},{17,25},{25,17},{2,10},{10... | collective-permute-start | bytes 786440 | tf_op jit(solution)/shard_map/ppermute | solution.py:41
  15.1 11.0 %collective-permute-start.2 = (f32[512,128]{1,0:T(8,128)S(1)}, f32[512,128]{1,0:T(8,128)S(1)}, u32[]{:S(2)}, u32[]{:S(2)}) collective-permute-start(f32[512,128]{1,0:T(8,128)S(1)} %get-tuple-element.79.rest_1_), channel_id=1, source_target_pairs={{8,16},{16,8},{24,0},{0,24},{9,17},{17,9},{25,1},{1,25},{10,18},{1... | collective-permute-start | bytes 786440 | tf_op jit(solution)/shard_map/ppermute | solution.py:41
  16.9 4.1 %collective-permute-start.4 = (f32[256,128]{1,0:T(8,128)S(1)}, f32[256,128]{1,0:T(8,128)S(1)}, u32[]{:S(2)}, u32[]{:S(2)}) collective-permute-start(f32[256,128]{1,0:T(8,128)S(1)} %get-tuple-element.81.rest_3_), channel_id=1, source_target_pairs={{0,1},{1,0},{2,3},{3,2},{4,5},{5,4},{6,7},{7,6},{8,9},{9,8},{10,11... | collective-permute-start | bytes 393224 | tf_op jit(solution)/shard_map/ppermute | solution.py:41
  21.1 9.9 %collective-permute-start.6 = (f32[528,128]{1,0:T(8,128)S(1)}, f32[528,128]{1,0:T(8,128)S(1)}, u32[]{:S(2)}, u32[]{:S(2)}) collective-permute-start(f32[528,128]{1,0:T(8,128)S(1)} %get-tuple-element.85), channel_id=1, source_target_pairs={{32,64},{64,32},{96,0},{0,96},{33,65},{65,33},{97,1},{1,97},{34,66... | collective-permute-start | bytes 811016 | tf_op jit(solution)/shard_map/ppermute | solution.py:41
  26.7 13.6 %collective-permute-start.7 = (f32[544,128]{1,0:T(8,128)S(1)}, f32[544,128]{1,0:T(8,128)S(1)}, u32[]{:S(2)}, u32[]{:S(2)}) collective-permute-start(f32[544,128]{1,0:T(8,128)S(1)} %get-tuple-element.87.rest_4_), channel_id=1, source_target_pairs={{0,8},{8,0},{16,24},{24,16},{1,9},{9,1},{17,25},{25,17},{2,10},{10... | collective-permute-start | bytes 835592 | tf_op jit(solution)/shard_map/ppermute | solution.py:41
  27.1 13.2 %collective-permute-start.8 = (f32[544,128]{1,0:T(8,128)S(1)}, f32[544,128]{1,0:T(8,128)S(1)}, u32[]{:S(2)}, u32[]{:S(2)}) collective-permute-start(f32[544,128]{1,0:T(8,128)S(1)} %get-tuple-element.88.rest_5_), channel_id=1, source_target_pairs={{8,16},{16,8},{24,0},{0,24},{9,17},{17,9},{25,1},{1,25},{10,18},{1... | collective-permute-start | bytes 835592 | tf_op jit(solution)/shard_map/ppermute | solution.py:41
  27.8 12.6 %collective-permute-start.11 = (f32[512,128]{1,0:T(8,128)S(1)}, f32[512,128]{1,0:T(8,128)S(1)}, u32[]{:S(2)}, u32[]{:S(2)}) collective-permute-start(f32[512,128]{1,0:T(8,128)S(1)} %get-tuple-element.91), channel_id=1, source_target_pairs={{0,32},{32,0},{64,96},{96,64},{1,33},{33,1},{65,97},{97,65},{2,34}... | collective-permute-start | bytes 786440 | tf_op jit(solution)/shard_map/ppermute | solution.py:41
  27.9 7.0 %collective-permute-start.9 = (f32[272,128]{1,0:T(8,128)S(1)}, f32[272,128]{1,0:T(8,128)S(1)}, u32[]{:S(2)}, u32[]{:S(2)}) collective-permute-start(f32[272,128]{1,0:T(8,128)S(1)} %get-tuple-element.89.rest_6_), channel_id=1, source_target_pairs={{1,2},{2,1},{3,4},{4,3},{5,6},{6,5},{7,0},{0,7},{9,10},{10,9},{11,... | collective-permute-start | bytes 417800 | tf_op jit(solution)/shard_map/ppermute | solution.py:41
  31.0 9.4 %collective-permute-start.10 = (f32[272,128]{1,0:T(8,128)S(1)}, f32[272,128]{1,0:T(8,128)S(1)}, u32[]{:S(2)}, u32[]{:S(2)}) collective-permute-start(f32[272,128]{1,0:T(8,128)S(1)} %get-tuple-element.90.rest_7_), channel_id=1, source_target_pairs={{0,1},{1,0},{2,3},{3,2},{4,5},{5,4},{6,7},{7,6},{8,9},{9,8},{10,11... | collective-permute-start | bytes 417800 | tf_op jit(solution)/shard_map/ppermute | solution.py:41
  34.9 10.4 %collective-permute-start.12 = (f32[512,128]{1,0:T(8,128)S(1)}, f32[512,128]{1,0:T(8,128)S(1)}, u32[]{:S(2)}, u32[]{:S(2)}) collective-permute-start(f32[512,128]{1,0:T(8,128)S(1)} %get-tuple-element.96), channel_id=1, source_target_pairs={{32,64},{64,32},{96,0},{0,96},{33,65},{65,33},{97,1},{1,97},{34,66... | collective-permute-start | bytes 786440 | tf_op jit(solution)/shard_map/ppermute | solution.py:41
  41.2 9.7 %collective-permute-start.13 = (f32[576,128]{1,0:T(8,128)S(1)}, f32[576,128]{1,0:T(8,128)S(1)}, u32[]{:S(2)}, u32[]{:S(2)}) collective-permute-start(f32[576,128]{1,0:T(8,128)S(1)} %get-tuple-element.99.rest_8_), channel_id=1, source_target_pairs={{0,8},{8,0},{16,24},{24,16},{1,9},{9,1},{17,25},{25,17},{2,10},{10... | collective-permute-start | bytes 884744 | tf_op jit(solution)/shard_map/ppermute | solution.py:41
  42.0 10.0 %collective-permute-start.14 = (f32[576,128]{1,0:T(8,128)S(1)}, f32[576,128]{1,0:T(8,128)S(1)}, u32[]{:S(2)}, u32[]{:S(2)}) collective-permute-start(f32[576,128]{1,0:T(8,128)S(1)} %get-tuple-element.100.rest_9_), channel_id=1, source_target_pairs={{8,16},{16,8},{24,0},{0,24},{9,17},{17,9},{25,1},{1,25},{10,18},{1... | collective-permute-start | bytes 884744 | tf_op jit(solution)/shard_map/ppermute | solution.py:41
  43.8 7.0 %collective-permute-start.17 = (f32[512,128]{1,0:T(8,128)S(1)}, f32[512,128]{1,0:T(8,128)S(1)}, u32[]{:S(2)}, u32[]{:S(2)}) collective-permute-start(f32[512,128]{1,0:T(8,128)S(1)} %get-tuple-element.103), channel_id=1, source_target_pairs={{0,32},{32,0},{64,96},{96,64},{1,33},{33,1},{65,97},{97,65},{2,34}... | collective-permute-start | bytes 786440 | tf_op jit(solution)/shard_map/ppermute | solution.py:41
  43.8 7.0 %collective-permute-start.15 = (f32[288,128]{1,0:T(8,128)S(1)}, f32[288,128]{1,0:T(8,128)S(1)}, u32[]{:S(2)}, u32[]{:S(2)}) collective-permute-start(f32[288,128]{1,0:T(8,128)S(1)} %get-tuple-element.101.rest_10_), channel_id=1, source_target_pairs={{1,2},{2,1},{3,4},{4,3},{5,6},{6,5},{7,0},{0,7},{9,10},{10,9},{11,... | collective-permute-start | bytes 442376 | tf_op jit(solution)/shard_map/ppermute | solution.py:41
  45.4 5.4 %collective-permute-start.16 = (f32[288,128]{1,0:T(8,128)S(1)}, f32[288,128]{1,0:T(8,128)S(1)}, u32[]{:S(2)}, u32[]{:S(2)}) collective-permute-start(f32[288,128]{1,0:T(8,128)S(1)} %get-tuple-element.102.rest_11_), channel_id=1, source_target_pairs={{0,1},{1,0},{2,3},{3,2},{4,5},{5,4},{6,7},{7,6},{8,9},{9,8},{10,11... | collective-permute-start | bytes 442376 | tf_op jit(solution)/shard_map/ppermute | solution.py:41
  45.6 1.7 %copy-start.1 = (f32[2,4,128]{2,1,0:T(4,128)S(1)}, f32[2,4,128]{2,1,0:T(4,128)}, u32[]{:S(2)}) copy-start(f32[2,4,128]{2,1,0:T(4,128)} %thetas.9) | copy-start | bytes 12292
  54.0 6.9 %collective-permute-start.21 = (f32[256,128]{1,0:T(8,128)S(1)}, f32[256,128]{1,0:T(8,128)S(1)}, u32[]{:S(2)}, u32[]{:S(2)}) collective-permute-start(f32[256,128]{1,0:T(8,128)S(1)} %get-tuple-element.114.rest_2_.rest_7_), channel_id=1, source_target_pairs={{1,2},{2,1},{3,4},{4,3},{5,6},{6,5},{7,0},{0,7},{9,10},{10,9},{11,... | collective-permute-start | bytes 393224 | tf_op jit(solution)/shard_map/ppermute | solution.py:41
  55.0 14.3 %collective-permute-start.23 = (f32[512,128]{1,0:T(8,128)S(1)}, f32[512,128]{1,0:T(8,128)S(1)}, u32[]{:S(2)}, u32[]{:S(2)}) collective-permute-start(f32[512,128]{1,0:T(8,128)S(1)} %get-tuple-element.116.rest_4_), channel_id=1, source_target_pairs={{0,32},{32,0},{64,96},{96,64},{1,33},{33,1},{65,97},{97,65},{2,34}... | collective-permute-start | bytes 786440 | tf_op jit(solution)/shard_map/ppermute | solution.py:41
  56.2 13.0 %collective-permute-start.19 = (f32[512,128]{1,0:T(8,128)S(1)}, f32[512,128]{1,0:T(8,128)S(1)}, u32[]{:S(2)}, u32[]{:S(2)}) collective-permute-start(f32[512,128]{1,0:T(8,128)S(1)} %get-tuple-element.112.rest_0_.rest_5_), channel_id=1, source_target_pairs={{0,8},{8,0},{16,24},{24,16},{1,9},{9,1},{17,25},{25,17},{2,10},{10... | collective-permute-start | bytes 786440 | tf_op jit(solution)/shard_map/ppermute | solution.py:41
  56.5 12.7 %collective-permute-start.20 = (f32[512,128]{1,0:T(8,128)S(1)}, f32[512,128]{1,0:T(8,128)S(1)}, u32[]{:S(2)}, u32[]{:S(2)}) collective-permute-start(f32[512,128]{1,0:T(8,128)S(1)} %get-tuple-element.113.rest_1_.rest_6_), channel_id=1, source_target_pairs={{8,16},{16,8},{24,0},{0,24},{9,17},{17,9},{25,1},{1,25},{10,18},{1... | collective-permute-start | bytes 786440 | tf_op jit(solution)/shard_map/ppermute | solution.py:41
  57.1 12.1 %collective-permute-start.18 = (f32[512,128]{1,0:T(8,128)S(1)}, f32[512,128]{1,0:T(8,128)S(1)}, u32[]{:S(2)}, u32[]{:S(2)}) collective-permute-start(f32[512,128]{1,0:T(8,128)S(1)} %get-tuple-element.104.d1), channel_id=1, source_target_pairs={{32,64},{64,32},{96,0},{0,96},{33,65},{65,33},{97,1},{1,97},{34,66... | collective-permute-start | bytes 786440 | tf_op jit(solution)/shard_map/ppermute | solution.py:41
  60.9 4.1 %collective-permute-start.22 = (f32[256,128]{1,0:T(8,128)S(1)}, f32[256,128]{1,0:T(8,128)S(1)}, u32[]{:S(2)}, u32[]{:S(2)}) collective-permute-start(f32[256,128]{1,0:T(8,128)S(1)} %get-tuple-element.115.rest_3_.rest_8_), channel_id=1, source_target_pairs={{0,1},{1,0},{2,3},{3,2},{4,5},{5,4},{6,7},{7,6},{8,9},{9,8},{10,11... | collective-permute-start | bytes 393224 | tf_op jit(solution)/shard_map/ppermute | solution.py:41
  65.0 9.0 %collective-permute-start.24 = (f32[512,128]{1,0:T(8,128)S(1)}, f32[512,128]{1,0:T(8,128)S(1)}, u32[]{:S(2)}, u32[]{:S(2)}) collective-permute-start(f32[512,128]{1,0:T(8,128)S(1)} %get-tuple-element.120), channel_id=1, source_target_pairs={{32,64},{64,32},{96,0},{0,96},{33,65},{65,33},{97,1},{1,97},{34,66... | collective-permute-start | bytes 786440 | tf_op jit(solution)/shard_map/ppermute | solution.py:41
  69.9 14.0 %collective-permute-start.25 = (f32[544,128]{1,0:T(8,128)S(1)}, f32[544,128]{1,0:T(8,128)S(1)}, u32[]{:S(2)}, u32[]{:S(2)}) collective-permute-start(f32[544,128]{1,0:T(8,128)S(1)} %get-tuple-element.122.rest_9_), channel_id=1, source_target_pairs={{0,8},{8,0},{16,24},{24,16},{1,9},{9,1},{17,25},{25,17},{2,10},{10... | collective-permute-start | bytes 835592 | tf_op jit(solution)/shard_map/ppermute | solution.py:41
  70.3 13.6 %collective-permute-start.26 = (f32[544,128]{1,0:T(8,128)S(1)}, f32[544,128]{1,0:T(8,128)S(1)}, u32[]{:S(2)}, u32[]{:S(2)}) collective-permute-start(f32[544,128]{1,0:T(8,128)S(1)} %get-tuple-element.123.rest_10_), channel_id=1, source_target_pairs={{8,16},{16,8},{24,0},{0,24},{9,17},{17,9},{25,1},{1,25},{10,18},{1... | collective-permute-start | bytes 835592 | tf_op jit(solution)/shard_map/ppermute | solution.py:41
  72.1 11.7 %collective-permute-start.29 = (f32[512,128]{1,0:T(8,128)S(1)}, f32[512,128]{1,0:T(8,128)S(1)}, u32[]{:S(2)}, u32[]{:S(2)}) collective-permute-start(f32[512,128]{1,0:T(8,128)S(1)} %get-tuple-element.126), channel_id=1, source_target_pairs={{0,32},{32,0},{64,96},{96,64},{1,33},{33,1},{65,97},{97,65},{2,34}... | collective-permute-start | bytes 786440 | tf_op jit(solution)/shard_map/ppermute | solution.py:41
  72.1 6.8 %collective-permute-start.27 = (f32[272,128]{1,0:T(8,128)S(1)}, f32[272,128]{1,0:T(8,128)S(1)}, u32[]{:S(2)}, u32[]{:S(2)}) collective-permute-start(f32[272,128]{1,0:T(8,128)S(1)} %get-tuple-element.124.rest_11_), channel_id=1, source_target_pairs={{1,2},{2,1},{3,4},{4,3},{5,6},{6,5},{7,0},{0,7},{9,10},{10,9},{11,... | collective-permute-start | bytes 417800 | tf_op jit(solution)/shard_map/ppermute | solution.py:41
  74.0 9.9 %collective-permute-start.28 = (f32[272,128]{1,0:T(8,128)S(1)}, f32[272,128]{1,0:T(8,128)S(1)}, u32[]{:S(2)}, u32[]{:S(2)}) collective-permute-start(f32[272,128]{1,0:T(8,128)S(1)} %get-tuple-element.125.rest_12_), channel_id=1, source_target_pairs={{0,1},{1,0},{2,3},{3,2},{4,5},{5,4},{6,7},{7,6},{8,9},{9,8},{10,11... | collective-permute-start | bytes 417800 | tf_op jit(solution)/shard_map/ppermute | solution.py:41
  79.0 9.7 %collective-permute-start.30 = (f32[512,128]{1,0:T(8,128)S(1)}, f32[512,128]{1,0:T(8,128)S(1)}, u32[]{:S(2)}, u32[]{:S(2)}) collective-permute-start(f32[512,128]{1,0:T(8,128)S(1)} %get-tuple-element.130), channel_id=1, source_target_pairs={{32,64},{64,32},{96,0},{0,96},{33,65},{65,33},{97,1},{1,97},{34,66... | collective-permute-start | bytes 786440 | tf_op jit(solution)/shard_map/ppermute | solution.py:41
  84.6 8.7 %collective-permute-start.31 = (f32[576,128]{1,0:T(8,128)S(1)}, f32[576,128]{1,0:T(8,128)S(1)}, u32[]{:S(2)}, u32[]{:S(2)}) collective-permute-start(f32[576,128]{1,0:T(8,128)S(1)} %get-tuple-element.133.rest_13_), channel_id=1, source_target_pairs={{0,8},{8,0},{16,24},{24,16},{1,9},{9,1},{17,25},{25,17},{2,10},{10... | collective-permute-start | bytes 884744 | tf_op jit(solution)/shard_map/ppermute | solution.py:41
  85.5 10.0 %collective-permute-start.32 = (f32[576,128]{1,0:T(8,128)S(1)}, f32[576,128]{1,0:T(8,128)S(1)}, u32[]{:S(2)}, u32[]{:S(2)}) collective-permute-start(f32[576,128]{1,0:T(8,128)S(1)} %get-tuple-element.134.rest_14_), channel_id=1, source_target_pairs={{8,16},{16,8},{24,0},{0,24},{9,17},{17,9},{25,1},{1,25},{10,18},{1... | collective-permute-start | bytes 884744 | tf_op jit(solution)/shard_map/ppermute | solution.py:41
  86.4 7.0 %collective-permute-start.35 = (f32[512,128]{1,0:T(8,128)S(1)}, f32[512,128]{1,0:T(8,128)S(1)}, u32[]{:S(2)}, u32[]{:S(2)}) collective-permute-start(f32[512,128]{1,0:T(8,128)S(1)} %get-tuple-element.137), channel_id=1, source_target_pairs={{0,32},{32,0},{64,96},{96,64},{1,33},{33,1},{65,97},{97,65},{2,34}... | collective-permute-start | bytes 786440 | tf_op jit(solution)/shard_map/ppermute | solution.py:41
  86.4 7.0 %collective-permute-start.33 = (f32[288,128]{1,0:T(8,128)S(1)}, f32[288,128]{1,0:T(8,128)S(1)}, u32[]{:S(2)}, u32[]{:S(2)}) collective-permute-start(f32[288,128]{1,0:T(8,128)S(1)} %get-tuple-element.135.rest_15_), channel_id=1, source_target_pairs={{1,2},{2,1},{3,4},{4,3},{5,6},{6,5},{7,0},{0,7},{9,10},{10,9},{11,... | collective-permute-start | bytes 442376 | tf_op jit(solution)/shard_map/ppermute | solution.py:41
  88.7 4.6 %collective-permute-start.34 = (f32[288,128]{1,0:T(8,128)S(1)}, f32[288,128]{1,0:T(8,128)S(1)}, u32[]{:S(2)}, u32[]{:S(2)}) collective-permute-start(f32[288,128]{1,0:T(8,128)S(1)} %get-tuple-element.136.rest_16_), channel_id=1, source_target_pairs={{0,1},{1,0},{2,3},{3,2},{4,5},{5,4},{6,7},{7,6},{8,9},{9,8},{10,11... | collective-permute-start | bytes 442376 | tf_op jit(solution)/shard_map/ppermute | solution.py:41

commit v3 on v2

--- a/solution.py
+++ b/solution.py
@@ -16,6 +16,7 @@
 LINE = {"gy": NZ, "gz": NY}
 CROSS = ("gx", 1)
 LOCALS = (("gy", 0), ("gy", 1), ("gz", 1), ("gz", 0), ("gx", 0))
+EARLY = (1, 9)
 SCALES = 16
 
 F32 = jnp.float32
@@ -221,17 +222,6 @@
         emit(j, jnp.broadcast_to(st[:NZ, j : j + 1], (NZ, C)))
 
 
-def fill_cross(d, depth, values, sv):
-    base = cross_base(depth)
-    for i in range(PLANE // 128):
-        rows = pl.ds(pl.multiple_of(base + i * 128, 128), 128)
-        d[pl.ds(i * 128, 128), :] = values(rows)
-    if sv is not None:
-        up = side(*CROSS)
-        d[PLANE:, :] = jnp.zeros((SCALES, C), F32)
-        d[PLANE:, :NZ] = sv[up * (NX - depth) + (1 - up) * (depth - 1)]
-
-
 def first_kernel(feat, scales, d1, buf, sv, sems):
     up = side(*CROSS)
     two = [
@@ -253,44 +243,46 @@
     spread(tile, emit)
 
 
-def start_kernel(feat, scales, fv, sb, d2, d3, *rest):
-    sends, (sv, sems) = rest[:5], rest[5:]
-    first = pltpu.make_async_copy(scales, sv, sems.at[NX])
-    first.start()
-
-    def copy(i):
-        rows = pl.ds(i * PLANE, PLANE)
-        return pltpu.make_async_copy(feat.at[rows, :], fv.at[rows, :], sems.at[i])
-
-    for i in range(NX):
-        copy(i).start()
-    first.wait()
-    for i in range(NX):
-
-        def emit(j, b, i=i):
-            sb[pl.ds(i * PLANE + j * NZ, NZ), :] = b
-
-        spread(sv[i], emit)
-    for i in range(NX):
-        copy(i).wait()
-    fill_cross(d2, 2, lambda rows: sb[rows, :] * fv[rows, :], sv)
-    fill_cross(d3, 3, lambda rows: sb[rows, :] * fv[rows, :], None)
-    for (axis, kind), send in zip(LOCALS, sends):
-        at = face_slices(axis, kind)
-        for group in batches(axis):
-            got = [sb[at(i)[0], :] * fv[at(i)[0], :] for i in group]
-            for i, v in zip(group, got):
-                send[at(i)[1], :] = v
-
-
-def aux_kernel(sb, fv, weights, w0, a2, w4, *faces):
-    def body(i):
-        rows = pl.ds(pl.multiple_of(i * 128, 128), 128)
-        s = sb[rows, :]
-        w0[rows, :] = s * fv[rows, :]
-        a2[rows, :] = -2.0 * (s * s)
-
-    loop(ROWS // 128, body, 1)
+def start_kernel(fv, sv, d2, d3, *sends):
+    up = side(*CROSS)
+    for depth, d in ((2, d2), (3, d3), (0, sends[-1])):
+        plane = up * (NX - depth) + (1 - up) * (depth - 1) if depth else (1 - up) * (NX - 1)
+        base = pl.multiple_of(plane * PLANE, PLANE)
+        tile = sv[plane]
+
+        def emit(j, b, base=base, d=d):
+            d[pl.ds(j * NZ, NZ), :] = b * fv[pl.ds(pl.multiple_of(base + j * NZ, NZ), NZ), :]
+
+        spread(tile, emit)
+        if depth == 2:
+            d[PLANE:, :] = jnp.zeros((SCALES, C), F32)
+            d[PLANE:, :NZ] = tile
+    for x in range(NX):
+        tile = sv[x]
+        st = jnp.transpose(tile, (1, 0))
+        ends = {
+            "gy": [
+                jnp.broadcast_to(st[:, y : y + 1], (NZ, C)) * fv[pl.ds(x * PLANE + y * NZ, NZ), :] for y in (0, NY - 1)
+            ],
+            "gz": [
+                jnp.broadcast_to(tile[:, z : z + 1], (NY, C)) * fv[pl.ds(x * PLANE + z, NY, stride=NZ), :]
+                for z in (0, NZ - 1)
+            ],
+        }
+        for (axis, kind), send in zip(LOCALS[:-1], sends):
+            low, high = ends[axis]
+            send[pl.ds(x * LINE[axis], LINE[axis]), :] = jnp.where(side(axis, kind) == 1, high, low)
+
+
+def aux_kernel(sv, fv, weights, w0, a2, w4, *faces):
+    for x in range(NX):
+
+        def emit(j, b, x=x):
+            rows = pl.ds(x * PLANE + j * NZ, NZ)
+            w0[rows, :] = b * fv[rows, :]
+            a2[rows, :] = -2.0 * (b * b)
+
+        spread(sv[x], emit)
     for (axis, kind), face in zip(LOCALS, faces):
         emit_face(a2, axis, kind, face)
     for layer in range(2):
@@ -374,10 +366,12 @@
     mix_planes(layer, (w0, w1, w2, w3), a2, thetas, w4, CROSS, d1, True)
 
 
-def mix_faces(layer, f, thetas, w4, outs, scaled):
+def mix_faces(layer, f, thetas, w4, outs, scaled, planes=(0, NX)):
     for (axis, _), (*ws, a2), out in zip(LOCALS, f, outs):
-        for i in range(FACE[axis] // 256):
-            rows = pl.ds(i * 256, 256)
+        start, stop = planes[0] * LINE[axis], planes[1] * LINE[axis]
+        size = min(256, stop - start)
+        for at in range(start, stop, size):
+            rows = pl.ds(at, size)
             out[rows, :] = mixed(layer, ws, a2, thetas, w4, rows, scaled)
 
 
@@ -387,29 +381,37 @@
     mix_planes(layer, (w0, w1, w2, w3), a2, thetas, w4, LOCALS[-1], sends[-1], True)
 
 
+def mix_range(layer, scaled, ws, a2, thetas, w4, out, planes, then=None):
+    for x in range(*planes):
+        for part in range(PLANE // 256):
+            rows = pl.ds(x * PLANE + part * 256, 256)
+            out[rows, :] = mixed(layer, ws, a2, thetas, w4, rows, scaled)
+        if then is not None:
+            then(x)
+
+
 def inner_mix_kernel(layer, scaled, w0, w1, w2, w3, a2, thetas, w4, out):
-    def body(i):
-        rows = pl.ds(pl.multiple_of(PLANE + i * 256, 256), 256)
-        out[rows, :] = mixed(layer, (w0, w1, w2, w3), a2, thetas, w4, rows, scaled)
-
-    loop((ROWS - 2 * PLANE) // 256, body, 4)
-
-
-def put_faces(out, faces):
+    mix_range(layer, scaled, (w0, w1, w2, w3), a2, thetas, w4, out, EARLY)
+
+
+def put_faces(out, faces, planes):
     for (axis, kind), face in zip(LOCALS, faces):
         at = face_slices(axis, kind)
-        for group in batches(axis):
+        for g in range(*planes, 4):
+            group = range(g, min(g + 4, planes[1]))
             got = [face[at(i)[1], :] for i in group]
             for i, v in zip(group, got):
                 out[at(i)[0], :] = v
 
 
-def merge_kernel(inner, d1, *rest):
+def merge_kernel(layer, inner, d1, w0, w1, w2, w3, a2, thetas, w4, *rest):
     sends, out, d2, d3 = rest[:5], *rest[5:]
-    put_faces(out, sends)
-    base = cross_base(1)
-    for i in range(PLANE // 128):
-        out[pl.ds(pl.multiple_of(base + i * 128, 128), 128), :] = d1[pl.ds(i * 128, 128), :]
+    put_faces(out, sends[:-1], EARLY)
+    for key, face in ((CROSS, d1), (LOCALS[-1], sends[-1])):
+        base = side(*key) * ((NX - 1) * PLANE)
+        for i in range(PLANE // 128):
+            out[pl.ds(pl.multiple_of(base + i * 128, 128), 128), :] = face[pl.ds(i * 128, 128), :]
+    mix_range(layer, True, (w0, w1, w2, w3), a2, thetas, w4, out, (EARLY[1], NX - 1))
     copy_plane(out, cross_base(2), d2)
     copy_plane(out, cross_base(3), d3)
 
@@ -420,21 +422,19 @@
     fix3(w3, a2, (z1, z0), d3, p2, q1, a2g1, a2g2, halos, g2, g1, faces)
 
     def copy(i):
-        rows = pl.ds(pl.multiple_of(i * PLANE, PLANE), PLANE)
+        rows = pl.ds(i * PLANE, PLANE)
         return pltpu.make_async_copy(hidden.at[rows, :], out.at[rows, :], sems.at[i])
 
     f = [(*known[i:12:4], faces[i], known[12 + i]) for i in range(4)]
-    mix_faces(layer, f, thetas, w4, done, False)
-    put_faces(hidden, done)
-    for i in range(1, NX - 1):
+    mix_faces(layer, f, thetas, w4, done, False, EARLY)
+    put_faces(hidden, done, EARLY)
+    for i in range(*EARLY):
         copy(i).start()
-    for i in range(2 * PLANE // 256):
-        plane, part = divmod(i, PLANE // 256)
-        rows = pl.ds(plane * (NX - 1) * PLANE + part * 256, 256)
-        hidden[rows, :] = mixed(layer, (w0, w1, w2, w3), a2, thetas, w4, rows, False)
-    copy(0).start()
-    copy(NX - 1).start()
-    loop(NX, lambda i: copy(i).wait(), 1)
+    ws = (w0, w1, w2, w3)
+    for planes in ((0, EARLY[0]), (EARLY[1], NX)):
+        mix_range(layer, False, ws, a2, thetas, w4, hidden, planes, lambda x: copy(x).start())
+    for i in range(NX):
+        copy(i).wait()
 
 
 def call(kernel, out_shape, args, in_hbm=(), out_hbm=(), scratch=(), aliases=None, mib=1):
@@ -451,7 +451,8 @@
 
 def per_device(features, scales, thetas, weights):
     shape = features.shape
-    feat = pltpu.with_memory_space_constraint(features.reshape(ROWS, C), pltpu.HBM)
+    fv, sv = features.reshape(ROWS, C), scales
+    feat = pltpu.with_memory_space_constraint(fv, pltpu.HBM)
     block, plane = arr(ROWS), arr(PLANE)
     scales = pltpu.with_memory_space_constraint(scales, pltpu.HBM)
     ghosts = [pltpu.VMEM((PLANE, C), F32)] * 2
@@ -462,22 +463,21 @@
         in_hbm=(0, 1),
         scratch=[pltpu.VMEM((PLANE, C), F32), pltpu.VMEM((NY, NZ), F32), pltpu.SemaphoreType.DMA((2,))],
     )
-    fv, sb, s2, s3, *sends = call(
-        start_kernel,
-        [block, block, arr(PLANE + SCALES), plane] + locals_out(0),
-        (feat, scales),
-        in_hbm=(0, 1),
-        scratch=[pltpu.VMEM(scales.shape, F32), pltpu.SemaphoreType.DMA((NX + 1,))],
-    )
+    s2, s3, *sends = call(start_kernel, [arr(PLANE + SCALES), plane] + locals_out(0), (fv, sv))
     for layer in range(2):
         last = layer == 1
         if last:
-            w0, s2, s3 = call(merge_kernel, [block, plane, plane], (inner, s1, *sends), aliases={0: 0})
+            w0, s2, s3 = call(
+                functools.partial(merge_kernel, 0),
+                [block, plane, plane],
+                (inner, s1, w0, w1, w2, w3, a2, thetas, w4, *sends),
+                aliases={0: 0},
+            )
         known = [sends[:4]]
         (d1,), halos, (d2,) = exchange(sends, cross=s1, late=s2)
         if not last:
             w4 = jax.ShapeDtypeStruct((2, 2 * C, 2 * C), jnp.bfloat16)
-            w0, a2, w4, *af = call(aux_kernel, [block, block, w4] + locals_out(0)[:4], (sb, fv, weights))
+            w0, a2, w4, *af = call(aux_kernel, [block, block, w4] + locals_out(0)[:4], (sv, fv, weights))
             main = (a2, af[2], af[3])
         (w1,) = call(local1_kernel, [block], (w0, a2))
         w1, *sends = call(fix1_kernel, [block] + locals_out(1), (w1, *main, d1, *halos), aliases={0: 0})

time: 99.6 us -> 100 us (level)
  Pallas kernels: 30.8 us -> 26.8 us
  local copies, waits for them, and re-layouts: 0.01 us -> 3.11 us
  waiting for transfers between devices: 24.5 us -> 26.3 us
    pallas_call x21, Pallas kernels: 30.8 us -> 26.8 us  [call(): pl.pallas_call(kernel, out_shape=out_shape, in_specs=[HBM if i in in_hbm...]
    unnamed x4 -> x12, local copies, waits for them, and re-layouts: 0.01 us -> 3.11 us
    ppermute x36, waiting for transfers between devices: 24.5 us -> 26.3 us  [swap(): return lax.ppermute(x, axis, pairs)]
  transfers between devices with their start and end apart: 36 -> 36, of which waited for: 12 -> 12; matrix products, arithmetic and copies ran while one was open for 0% -> 0% of each run, Pallas kernels for 22% -> 21%
where the time goes in v3:
time: 100 us
  starting transfers between devices  43.5 us (44%)
  Pallas kernels  26.8 us (27%)
  waiting for transfers between devices  26.3 us (26%)
  local copies, waits for them, and re-layouts  3.11 us (3%)
    ppermute x36, starting transfers between devices, swap(): return lax.ppermute(x, axis, pairs)  43.5 us
    pallas_call x21, Pallas kernels, call(): pl.pallas_call(kernel, out_shape=out_shape, in_specs=[HBM if i in in_hbm...  26.8 us
    ppermute x36, waiting for transfers between devices, swap(): return lax.ppermute(x, axis, pairs)  26.3 us
    unnamed x12, local copies, waits for them, and re-layouts  3.11 us
  transfers between devices with their start and end apart: 36, of which 12 were waited for; matrix products, arithmetic and copies ran while one was open for 0% of the time, Pallas kernels for 21%

profile of v3, /device:TPU:1, one launch (start us, length us, event | category | flops | bytes accessed | tf_op | source)
XLA Modules:
  0.0 100.2 jit_solution(3348967264148429066)
XLA Ops:
  0.0 2.2 %copy-done = f32[16,16,32,128]{3,2,1,0:T(8,128)S(1)} copy-done((f32[16,16,32,128]{3,2,1,0:T(8,128)S(1)}, f32[16,16,32,128]{3,2,1,0:T(8,128)}, u32[]{:S(2)}) %copy-start) | copy-done | bytes 4194328
  2.2 0.9 copy-done.2
  3.8 5.7 %collective-permute-start.3 = (f32[256,128]{1,0:T(8,128)S(1)}, f32[256,128]{1,0:T(8,128)S(1)}, u32[]{:S(2)}, u32[]{:S(2)}) collective-permute-start(f32[256,128]{1,0:T(8,128)S(1)} %get-tuple-element.76.rest_2_), channel_id=1, source_target_pairs={{1,2},{2,1},{3,4},{4,3},{5,6},{6,5},{7,0},{0,7},{9,10},{10,9},{11,... | collective-permute-start | bytes 393224 | tf_op jit(solution)/shard_map/ppermute | solution.py:42
  9.5 1.2 %shard_map.48 = f32[528,128]{1,0:T(8,128)S(1)} custom-call(f32[8192,128]{1,0:T(8,128)} %bitcast.2, f32[16,16,32]{2,1,0:T(8,128)} %sv.3), custom_call_target="tpu_custom_call" | custom-call | tf_op jit(solution)/shard_map/pallas_call | solution.py:441
  10.7 3.5 %collective-permute-start = (f32[528,128]{1,0:T(8,128)S(1)}, f32[528,128]{1,0:T(8,128)S(1)}, u32[]{:S(2)}, u32[]{:S(2)}) collective-permute-start(f32[528,128]{1,0:T(8,128)S(1)} %shard_map.48), channel_id=1, source_target_pairs={{32,64},{64,32},{96,0},{0,96},{33,65},{65,33},{97,1},{1,97},{34,66... | collective-permute-start | bytes 811016 | tf_op jit(solution)/shard_map/ppermute | solution.py:42
  14.2 1.2 %collective-permute-start.1 = (f32[512,128]{1,0:T(8,128)S(1)}, f32[512,128]{1,0:T(8,128)S(1)}, u32[]{:S(2)}, u32[]{:S(2)}) collective-permute-start(f32[512,128]{1,0:T(8,128)S(1)} %get-tuple-element.74.rest_0_), channel_id=1, source_target_pairs={{0,8},{8,0},{16,24},{24,16},{1,9},{9,1},{17,25},{25,17},{2,10},{10... | collective-permute-start | bytes 786440 | tf_op jit(solution)/shard_map/ppermute | solution.py:42
  15.4 1.8 %collective-permute-start.2 = (f32[512,128]{1,0:T(8,128)S(1)}, f32[512,128]{1,0:T(8,128)S(1)}, u32[]{:S(2)}, u32[]{:S(2)}) collective-permute-start(f32[512,128]{1,0:T(8,128)S(1)} %get-tuple-element.75.rest_1_), channel_id=1, source_target_pairs={{8,16},{16,8},{24,0},{0,24},{9,17},{17,9},{25,1},{1,25},{10,18},{1... | collective-permute-start | bytes 786440 | tf_op jit(solution)/shard_map/ppermute | solution.py:42
  17.3 4.1 %collective-permute-done.4.rest_3_ = f32[256,128]{1,0:T(8,128)S(1)} collective-permute-done((f32[256,128]{1,0:T(8,128)S(1)}, f32[256,128]{1,0:T(8,128)S(1)}, u32[]{:S(2)}, u32[]{:S(2)}) %collective-permute-start.4) | collective-permute-done | bytes 131104 | tf_op jit(solution)/shard_map/ppermute | solution.py:42
  21.4 2.2 %collective-permute-start.6 = (f32[528,128]{1,0:T(8,128)S(1)}, f32[528,128]{1,0:T(8,128)S(1)}, u32[]{:S(2)}, u32[]{:S(2)}) collective-permute-start(f32[528,128]{1,0:T(8,128)S(1)} %get-tuple-element.81), channel_id=1, source_target_pairs={{32,64},{64,32},{96,0},{0,96},{33,65},{65,33},{97,1},{1,97},{34,66... | collective-permute-start | bytes 811016 | tf_op jit(solution)/shard_map/ppermute | solution.py:42
  23.5 2.1 %shard_map.46 = (f32[8192,128]{1,0:T(8,128)S(1)}, f32[8192,128]{1,0:T(8,128)S(1)}, bf16[2,256,256]{2,1,0:T(8,128)(2,1)S(1)}, f32[512,128]{1,0:T(8,128)S(1)}, f32...) custom-call(f32[16,16,32]{2,1,0:T(8,128)S(1)} %copy-done.3, f32[8192,128]{1,0:T(8,128)S(1)} %bitcast.4, ...), custom_call_target="tpu_custom_call" | custom-call | tf_op jit(solution)/shard_map/pallas_call | solution.py:441
  25.6 1.5 %shard_map.47.w_in = f32[8192,128]{1,0:T(8,128)S(1)} custom-call(f32[8192,128]{1,0:T(8,128)S(1)} %get-tuple-element.70.w0, f32[8192,128]{1,0:T(8,128)S(1)} %get-tuple-element.71.a2), custom_call_target="tpu_custom_call" | custom-call | tf_op jit(solution)/shard_map/pallas_call | solution.py:441
  29.0 3.0 %collective-permute-start.9 = (f32[272,128]{1,0:T(8,128)S(1)}, f32[272,128]{1,0:T(8,128)S(1)}, u32[]{:S(2)}, u32[]{:S(2)}) collective-permute-start(f32[272,128]{1,0:T(8,128)S(1)} %get-tuple-element.85.rest_6_), channel_id=1, source_target_pairs={{1,2},{2,1},{3,4},{4,3},{5,6},{6,5},{7,0},{0,7},{9,10},{10,9},{11,... | collective-permute-start | bytes 417800 | tf_op jit(solution)/shard_map/ppermute | solution.py:42
  32.0 4.0 %collective-permute-done.9.rest_2_ = f32[272,128]{1,0:T(8,128)S(1)} collective-permute-done((f32[272,128]{1,0:T(8,128)S(1)}, f32[272,128]{1,0:T(8,128)S(1)}, u32[]{:S(2)}, u32[]{:S(2)}) %collective-permute-start.9) | collective-permute-done | bytes 139296 | tf_op jit(solution)/shard_map/ppermute | solution.py:42
  36.0 3.5 %collective-permute-start.12 = (f32[512,128]{1,0:T(8,128)S(1)}, f32[512,128]{1,0:T(8,128)S(1)}, u32[]{:S(2)}, u32[]{:S(2)}) collective-permute-start(f32[512,128]{1,0:T(8,128)S(1)} %get-tuple-element.92), channel_id=1, source_target_pairs={{32,64},{64,32},{96,0},{0,96},{33,65},{65,33},{97,1},{1,97},{34,66... | collective-permute-start | bytes 786440 | tf_op jit(solution)/shard_map/ppermute | solution.py:42
  39.8 1.6 %shard_map.52 = (f32[8192,128]{1,0:T(8,128)S(1)}, f32[512,128]{1,0:T(8,128)S(1)}) custom-call(f32[8192,128]{1,0:T(8,128)S(1)} %get-tuple-element.79.w1, f32[8192,128]{1,0:T(8,128)S(1)} %get-tuple-element.71.a2, f32[8192,128]{1,0:T(8,128)S(1)} %get-tuple-element.70.w0, f32[528,128]{1,0:T(8,128)S(1)} %collective-permute-done.d1.d, f32[512,128]{1,0:T(8,128)S(1)} %shard_map.51.a2g1), custom_call_target="tpu_custom_call" | custom-call | tf_op jit(solution)/shard_map/pallas_call | solution.py:441
  41.5 0.8 shard_map.53
  42.2 0.8 collective-permute-start.13
  43.1 1.8 %collective-permute-start.14 = (f32[576,128]{1,0:T(8,128)S(1)}, f32[576,128]{1,0:T(8,128)S(1)}, u32[]{:S(2)}, u32[]{:S(2)}) collective-permute-start(f32[576,128]{1,0:T(8,128)S(1)} %get-tuple-element.96.rest_9_), channel_id=1, source_target_pairs={{8,16},{16,8},{24,0},{0,24},{9,17},{17,9},{25,1},{1,25},{10,18},{1... | collective-permute-start | bytes 884744 | tf_op jit(solution)/shard_map/ppermute | solution.py:42
  44.9 1.6 %collective-permute-done.12.d3 = f32[512,128]{1,0:T(8,128)S(1)} collective-permute-done((f32[512,128]{1,0:T(8,128)S(1)}, f32[512,128]{1,0:T(8,128)S(1)}, u32[]{:S(2)}, u32[]{:S(2)}) %collective-permute-start.12) | collective-permute-done | bytes 262176 | tf_op jit(solution)/shard_map/ppermute | solution.py:42
  46.7 1.7 %shard_map.55 = (f32[8192,128]{1,0:T(8,128)S(1)}, f32[512,128]{1,0:T(8,128)S(1)}, f32[512,128]{1,0:T(8,128)S(1)}) custom-call(f32[8192,128]{1,0:T(8,128)S(1)} %get-tuple-element.88.w2, f32[8192,128]{1,0:T(8,128)S(1)} %get-tuple-element.71.a2, f32[8192,128]{1,0:T(8,128)S(1)} %get-tuple-element.79.w1, f32[528,128]{1,0:T(8,128)S(1)} %collective-permute-done.d1.d, ...), custom_call_target="tpu_custom_call" | custom-call | tf_op jit(solution)/shard_map/pallas_call | solution.py:441
  48.5 1.6 %shard_map.56.inner = f32[8192,128]{1,0:T(8,128)S(1)} custom-call(f32[8192,128]{1,0:T(8,128)S(1)} %get-tuple-element.70.w0, f32[8192,128]{1,0:T(8,128)S(1)} %get-tuple-element.79.w1, f32[8192,128]{1,0:T(8,128)S(1)} %get-tuple-element.88.w2, f32[8192,128]{1,0:T(8,128)S(1)} %get-tuple-element.90.w3.w3_in, f32[8192,128]{1,0:T(8,128)S(1)} %get-tuple-element.71.a2, ...), custom_call_target="tpu_custom_call" | custom-call | tf_op jit(solution)/shard_map/pallas_call | solution.py:441
  50.1 1.8 %collective-permute-done.15.rest_2_ = f32[288,128]{1,0:T(8,128)S(1)} collective-permute-done((f32[288,128]{1,0:T(8,128)S(1)}, f32[288,128]{1,0:T(8,128)S(1)}, u32[]{:S(2)}, u32[]{:S(2)}) %collective-permute-start.15) | collective-permute-done | bytes 147488 | tf_op jit(solution)/shard_map/ppermute | solution.py:42
  51.9 1.2 %collective-permute-done.14.rest_1_ = f32[576,128]{1,0:T(8,128)S(1)} collective-permute-done((f32[576,128]{1,0:T(8,128)S(1)}, f32[576,128]{1,0:T(8,128)S(1)}, u32[]{:S(2)}, u32[]{:S(2)}) %collective-permute-start.14) | collective-permute-done | bytes 294944 | tf_op jit(solution)/shard_map/ppermute | solution.py:42
  53.1 1.2 %shard_map.57 = (f32[8192,128]{1,0:T(8,128)S(1)}, f32[512,128]{1,0:T(8,128)S(1)}, f32[512,128]{1,0:T(8,128)S(1)}, f32[512,128]{1,0:T(8,128)S(1)}, f32[256,128]{1,0:T(8,128)S(1)}, /*index=5*/f32[256,128]{1,0:T(8,128)S(1)}) custom-call(f32[8192,128]{1,0:T(8,128)S(1)} %get-tuple-element.90.w3.w3_in, ...), custom_call_target="tpu_custom_call", output_to_operand_aliasing={{0}: (0, {})} | custom-call | tf_op jit(solution)/shard_map/pallas_call | solution.py:441
  54.2 0.9 shard_map.58
  55.1 0.9 collective-permute-start.21
  56.0 1.2 %collective-permute-start.23 = (f32[512,128]{1,0:T(8,128)S(1)}, f32[512,128]{1,0:T(8,128)S(1)}, u32[]{:S(2)}, u32[]{:S(2)}) collective-permute-start(f32[512,128]{1,0:T(8,128)S(1)} %get-tuple-element.112.rest_4_), channel_id=1, source_target_pairs={{0,32},{32,0},{64,96},{96,64},{1,33},{33,1},{65,97},{97,65},{2,34}... | collective-permute-start | bytes 786440 | tf_op jit(solution)/shard_map/ppermute | solution.py:42
  58.2 3.0 %collective-permute-start.18 = (f32[512,128]{1,0:T(8,128)S(1)}, f32[512,128]{1,0:T(8,128)S(1)}, u32[]{:S(2)}, u32[]{:S(2)}) collective-permute-start(f32[512,128]{1,0:T(8,128)S(1)} %get-tuple-element.100.d1), channel_id=1, source_target_pairs={{32,64},{64,32},{96,0},{0,96},{33,65},{65,33},{97,1},{1,97},{34,66... | collective-permute-start | bytes 786440 | tf_op jit(solution)/shard_map/ppermute | solution.py:42
  61.2 0.7 collective-permute-done.21.rest_2_
  62.0 1.4 %shard_map.59 = (f32[8192,128]{1,0:T(8,128)S(1)}, f32[512,128]{1,0:T(8,128)S(1)}, f32[512,128]{1,0:T(8,128)S(1)}) custom-call(f32[8192,128]{1,0:T(8,128)S(1)} %shard_map.56.inner, f32[512,128]{1,0:T(8,128)S(1)} %get-tuple-element.100.d1, f32[8192,128]{1,0:T(8,128)S(1)} %get-tuple-element.70.w0, ...), custom_call_target="tpu_custom_call", output_to_operand_aliasing={{0}: (0, {})} | custom-call | tf_op jit(solution)/shard_map/pallas_call | solution.py:441
  63.4 2.7 %collective-permute-done.22.rest_3_ = f32[256,128]{1,0:T(8,128)S(1)} collective-permute-done((f32[256,128]{1,0:T(8,128)S(1)}, f32[256,128]{1,0:T(8,128)S(1)}, u32[]{:S(2)}, u32[]{:S(2)}) %collective-permute-start.22) | collective-permute-done | bytes 131104 | tf_op jit(solution)/shard_map/ppermute | solution.py:42
  66.1 2.7 %collective-permute-start.24 = (f32[512,128]{1,0:T(8,128)S(1)}, f32[512,128]{1,0:T(8,128)S(1)}, u32[]{:S(2)}, u32[]{:S(2)}) collective-permute-start(f32[512,128]{1,0:T(8,128)S(1)} %get-tuple-element.116), channel_id=1, source_target_pairs={{32,64},{64,32},{96,0},{0,96},{33,65},{65,33},{97,1},{1,97},{34,66... | collective-permute-start | bytes 786440 | tf_op jit(solution)/shard_map/ppermute | solution.py:42
  68.8 1.5 %shard_map.60.w_in = f32[8192,128]{1,0:T(8,128)S(1)} custom-call(f32[8192,128]{1,0:T(8,128)S(1)} %get-tuple-element.113.w0, f32[8192,128]{1,0:T(8,128)S(1)} %get-tuple-element.71.a2), custom_call_target="tpu_custom_call" | custom-call | tf_op jit(solution)/shard_map/pallas_call | solution.py:441
  71.4 1.8 %collective-permute-start.26 = (f32[544,128]{1,0:T(8,128)S(1)}, f32[544,128]{1,0:T(8,128)S(1)}, u32[]{:S(2)}, u32[]{:S(2)}) collective-permute-start(f32[544,128]{1,0:T(8,128)S(1)} %get-tuple-element.119.rest_10_), channel_id=1, source_target_pairs={{8,16},{16,8},{24,0},{0,24},{9,17},{17,9},{25,1},{1,25},{10,18},{1... | collective-permute-start | bytes 835592 | tf_op jit(solution)/shard_map/ppermute | solution.py:42
  73.2 1.5 %collective-permute-start.27 = (f32[272,128]{1,0:T(8,128)S(1)}, f32[272,128]{1,0:T(8,128)S(1)}, u32[]{:S(2)}, u32[]{:S(2)}) collective-permute-start(f32[272,128]{1,0:T(8,128)S(1)} %get-tuple-element.120.rest_11_), channel_id=1, source_target_pairs={{1,2},{2,1},{3,4},{4,3},{5,6},{6,5},{7,0},{0,7},{9,10},{10,9},{11,... | collective-permute-start | bytes 417800 | tf_op jit(solution)/shard_map/ppermute | solution.py:42
  75.3 4.7 %collective-permute-done.27.rest_2_ = f32[272,128]{1,0:T(8,128)S(1)} collective-permute-done((f32[272,128]{1,0:T(8,128)S(1)}, f32[272,128]{1,0:T(8,128)S(1)}, u32[]{:S(2)}, u32[]{:S(2)}) %collective-permute-start.27) | collective-permute-done | bytes 139296 | tf_op jit(solution)/shard_map/ppermute | solution.py:42
  80.1 3.2 %collective-permute-start.30 = (f32[512,128]{1,0:T(8,128)S(1)}, f32[512,128]{1,0:T(8,128)S(1)}, u32[]{:S(2)}, u32[]{:S(2)}) collective-permute-start(f32[512,128]{1,0:T(8,128)S(1)} %get-tuple-element.126), channel_id=1, source_target_pairs={{32,64},{64,32},{96,0},{0,96},{33,65},{65,33},{97,1},{1,97},{34,66... | collective-permute-start | bytes 786440 | tf_op jit(solution)/shard_map/ppermute | solution.py:42
  83.3 1.6 %shard_map.62 = (f32[8192,128]{1,0:T(8,128)S(1)}, f32[512,128]{1,0:T(8,128)S(1)}) custom-call(f32[8192,128]{1,0:T(8,128)S(1)} %get-tuple-element.114.w1, f32[8192,128]{1,0:T(8,128)S(1)} %get-tuple-element.71.a2, f32[8192,128]{1,0:T(8,128)S(1)} %get-tuple-element.113.w0, f32[512,128]{1,0:T(8,128)S(1)} %collective-permute-done.18.d1, ...), custom_call_target="tpu_custom_call" | custom-call | tf_op jit(solution)/shard_map/pallas_call | solution.py:441
  85.0 0.7 shard_map.63
  85.7 0.8 collective-permute-start.31
  86.6 0.9 collective-permute-start.32
  87.4 0.9 collective-permute-start.33
  88.3 1.5 %collective-permute-done.30.d3 = f32[512,128]{1,0:T(8,128)S(1)} collective-permute-done((f32[512,128]{1,0:T(8,128)S(1)}, f32[512,128]{1,0:T(8,128)S(1)}, u32[]{:S(2)}, u32[]{:S(2)}) %collective-permute-start.30) | collective-permute-done | bytes 262176 | tf_op jit(solution)/shard_map/ppermute | solution.py:42
  89.8 1.7 %shard_map.64 = (f32[8192,128]{1,0:T(8,128)S(1)}, f32[512,128]{1,0:T(8,128)S(1)}, f32[512,128]{1,0:T(8,128)S(1)}) custom-call(f32[8192,128]{1,0:T(8,128)S(1)} %get-tuple-element.123.w2, f32[8192,128]{1,0:T(8,128)S(1)} %get-tuple-element.71.a2, f32[8192,128]{1,0:T(8,128)S(1)} %get-tuple-element.114.w1, f32[512,128]{1,0:T(8,128)S(1)} %collective-permute-done.18.d1, ...), custom_call_target="tpu_custom_call" | custom-call | tf_op jit(solution)/shard_map/pallas_call | solution.py:441
  91.5 1.4 %shard_map.65.inner = f32[8192,128]{1,0:T(8,128)S(1)} custom-call(f32[8192,128]{1,0:T(8,128)S(1)} %get-tuple-element.113.w0, f32[8192,128]{1,0:T(8,128)S(1)} %get-tuple-element.114.w1, f32[8192,128]{1,0:T(8,128)S(1)} %get-tuple-element.123.w2, f32[8192,128]{1,0:T(8,128)S(1)} %get-tuple-element.125.w3.w3_in, f32[8192,128]{1,0:T(8,128)S(1)} %get-tuple-element.71.a2, ...), custom_call_target="tpu_custom_call" | custom-call | tf_op jit(solution)/shard_map/pallas_call | solution.py:441
  92.9 1.6 %collective-permute-done.33.rest_2_ = f32[288,128]{1,0:T(8,128)S(1)} collective-permute-done((f32[288,128]{1,0:T(8,128)S(1)}, f32[288,128]{1,0:T(8,128)S(1)}, u32[]{:S(2)}, u32[]{:S(2)}) %collective-permute-start.33) | collective-permute-done | bytes 147488 | tf_op jit(solution)/shard_map/ppermute | solution.py:42
  94.5 2.1 %collective-permute-done.32.rest_1_ = f32[576,128]{1,0:T(8,128)S(1)} collective-permute-done((f32[576,128]{1,0:T(8,128)S(1)}, f32[576,128]{1,0:T(8,128)S(1)}, u32[]{:S(2)}, u32[]{:S(2)}) %collective-permute-start.32) | collective-permute-done | bytes 294944 | tf_op jit(solution)/shard_map/ppermute | solution.py:42
  96.6 3.4 %shard_map.66 = (f32[8192,128]{1,0:T(8,128)S(1)}, f32[8192,128]{1,0:T(8,128)S(1)}, f32[8192,128]{1,0:T(8,128)}) custom-call(f32[8192,128]{1,0:T(8,128)S(1)} %get-tuple-element.125.w3.w3_in, f32[8192,128]{1,0:T(8,128)S(1)} %get-tuple-element.71.a2, ...), custom_call_target="tpu_custom_call", output_to_operand_aliasing={{0}: (0, {}), {1}: (14, {})} | custom-call | tf_op jit(solution)/shard_map/pallas_call | solution.py:441
  (57 shorter events, 5.7 us)
Async XLA Ops:
  0.0 2.2 %copy-start = (f32[16,16,32,128]{3,2,1,0:T(8,128)S(1)}, f32[16,16,32,128]{3,2,1,0:T(8,128)}, u32[]{:S(2)}) copy-start(f32[16,16,32,128]{3,2,1,0:T(8,128)} %param.4) | copy-start | bytes 12582916
  2.2 0.9 copy-start.2
  3.1 20.4 %copy-start.1 = (f32[16,16,32,128]{3,2,1,0:T(8,128)S(1)}, f32[16,16,32,128]{3,2,1,0:T(8,128)}, u32[]{:S(2)}) copy-start(f32[16,16,32,128]{3,2,1,0:T(8,128)} %param.4) | copy-start | bytes 12582916
  3.1 20.4 %copy-start.3 = (f32[16,16,32]{2,1,0:T(8,128)S(1)}, f32[16,16,32]{2,1,0:T(8,128)}, u32[]{:S(2)}) copy-start(f32[16,16,32]{2,1,0:T(8,128)} %sv.3) | copy-start | bytes 98308
  3.1 20.4 %copy-start.5 = (f32[2,128,128]{2,1,0:T(8,128)S(1)}, f32[2,128,128]{2,1,0:T(8,128)}, u32[]{:S(2)}) copy-start(f32[2,128,128]{2,1,0:T(8,128)} %weights.1) | copy-start | bytes 393220
  3.8 13.5 %collective-permute-start.3 = (f32[256,128]{1,0:T(8,128)S(1)}, f32[256,128]{1,0:T(8,128)S(1)}, u32[]{:S(2)}, u32[]{:S(2)}) collective-permute-start(f32[256,128]{1,0:T(8,128)S(1)} %get-tuple-element.76.rest_2_), channel_id=1, source_target_pairs={{1,2},{2,1},{3,4},{4,3},{5,6},{6,5},{7,0},{0,7},{9,10},{10,9},{11,... | collective-permute-start | bytes 393224 | tf_op jit(solution)/shard_map/ppermute | solution.py:42
  10.7 16.5 %collective-permute-start = (f32[528,128]{1,0:T(8,128)S(1)}, f32[528,128]{1,0:T(8,128)S(1)}, u32[]{:S(2)}, u32[]{:S(2)}) collective-permute-start(f32[528,128]{1,0:T(8,128)S(1)} %shard_map.48), channel_id=1, source_target_pairs={{32,64},{64,32},{96,0},{0,96},{33,65},{65,33},{97,1},{1,97},{34,66... | collective-permute-start | bytes 811016 | tf_op jit(solution)/shard_map/ppermute | solution.py:42
  14.2 12.9 %collective-permute-start.5 = (f32[512,128]{1,0:T(8,128)S(1)}, f32[512,128]{1,0:T(8,128)S(1)}, u32[]{:S(2)}, u32[]{:S(2)}) collective-permute-start(f32[512,128]{1,0:T(8,128)S(1)} %get-tuple-element.78), channel_id=1, source_target_pairs={{0,32},{32,0},{64,96},{96,64},{1,33},{33,1},{65,97},{97,65},{2,34}... | collective-permute-start | bytes 786440 | tf_op jit(solution)/shard_map/ppermute | solution.py:42
  14.2 12.9 %collective-permute-start.1 = (f32[512,128]{1,0:T(8,128)S(1)}, f32[512,128]{1,0:T(8,128)S(1)}, u32[]{:S(2)}, u32[]{:S(2)}) collective-permute-start(f32[512,128]{1,0:T(8,128)S(1)} %get-tuple-element.74.rest_0_), channel_id=1, source_target_pairs={{0,8},{8,0},{16,24},{24,16},{1,9},{9,1},{17,25},{25,17},{2,10},{10... | collective-permute-start | bytes 786440 | tf_op jit(solution)/shard_map/ppermute | solution.py:42
  15.4 11.7 %collective-permute-start.2 = (f32[512,128]{1,0:T(8,128)S(1)}, f32[512,128]{1,0:T(8,128)S(1)}, u32[]{:S(2)}, u32[]{:S(2)}) collective-permute-start(f32[512,128]{1,0:T(8,128)S(1)} %get-tuple-element.75.rest_1_), channel_id=1, source_target_pairs={{8,16},{16,8},{24,0},{0,24},{9,17},{17,9},{25,1},{1,25},{10,18},{1... | collective-permute-start | bytes 786440 | tf_op jit(solution)/shard_map/ppermute | solution.py:42
  17.3 4.1 %collective-permute-start.4 = (f32[256,128]{1,0:T(8,128)S(1)}, f32[256,128]{1,0:T(8,128)S(1)}, u32[]{:S(2)}, u32[]{:S(2)}) collective-permute-start(f32[256,128]{1,0:T(8,128)S(1)} %get-tuple-element.77.rest_3_), channel_id=1, source_target_pairs={{0,1},{1,0},{2,3},{3,2},{4,5},{5,4},{6,7},{7,6},{8,9},{9,8},{10,11... | collective-permute-start | bytes 393224 | tf_op jit(solution)/shard_map/ppermute | solution.py:42
  21.4 10.7 %collective-permute-start.6 = (f32[528,128]{1,0:T(8,128)S(1)}, f32[528,128]{1,0:T(8,128)S(1)}, u32[]{:S(2)}, u32[]{:S(2)}) collective-permute-start(f32[528,128]{1,0:T(8,128)S(1)} %get-tuple-element.81), channel_id=1, source_target_pairs={{32,64},{64,32},{96,0},{0,96},{33,65},{65,33},{97,1},{1,97},{34,66... | collective-permute-start | bytes 811016 | tf_op jit(solution)/shard_map/ppermute | solution.py:42
  27.8 13.6 %collective-permute-start.7 = (f32[544,128]{1,0:T(8,128)S(1)}, f32[544,128]{1,0:T(8,128)S(1)}, u32[]{:S(2)}, u32[]{:S(2)}) collective-permute-start(f32[544,128]{1,0:T(8,128)S(1)} %get-tuple-element.83.rest_4_), channel_id=1, source_target_pairs={{0,8},{8,0},{16,24},{24,16},{1,9},{9,1},{17,25},{25,17},{2,10},{10... | collective-permute-start | bytes 835592 | tf_op jit(solution)/shard_map/ppermute | solution.py:42
  28.2 13.2 %collective-permute-start.8 = (f32[544,128]{1,0:T(8,128)S(1)}, f32[544,128]{1,0:T(8,128)S(1)}, u32[]{:S(2)}, u32[]{:S(2)}) collective-permute-start(f32[544,128]{1,0:T(8,128)S(1)} %get-tuple-element.84.rest_5_), channel_id=1, source_target_pairs={{8,16},{16,8},{24,0},{0,24},{9,17},{17,9},{25,1},{1,25},{10,18},{1... | collective-permute-start | bytes 835592 | tf_op jit(solution)/shard_map/ppermute | solution.py:42
  28.8 12.6 %collective-permute-start.11 = (f32[512,128]{1,0:T(8,128)S(1)}, f32[512,128]{1,0:T(8,128)S(1)}, u32[]{:S(2)}, u32[]{:S(2)}) collective-permute-start(f32[512,128]{1,0:T(8,128)S(1)} %get-tuple-element.87), channel_id=1, source_target_pairs={{0,32},{32,0},{64,96},{96,64},{1,33},{33,1},{65,97},{97,65},{2,34}... | collective-permute-start | bytes 786440 | tf_op jit(solution)/shard_map/ppermute | solution.py:42
  29.0 7.0 %collective-permute-start.9 = (f32[272,128]{1,0:T(8,128)S(1)}, f32[272,128]{1,0:T(8,128)S(1)}, u32[]{:S(2)}, u32[]{:S(2)}) collective-permute-start(f32[272,128]{1,0:T(8,128)S(1)} %get-tuple-element.85.rest_6_), channel_id=1, source_target_pairs={{1,2},{2,1},{3,4},{4,3},{5,6},{6,5},{7,0},{0,7},{9,10},{10,9},{11,... | collective-permute-start | bytes 417800 | tf_op jit(solution)/shard_map/ppermute | solution.py:42
  32.0 9.4 %collective-permute-start.10 = (f32[272,128]{1,0:T(8,128)S(1)}, f32[272,128]{1,0:T(8,128)S(1)}, u32[]{:S(2)}, u32[]{:S(2)}) collective-permute-start(f32[272,128]{1,0:T(8,128)S(1)} %get-tuple-element.86.rest_7_), channel_id=1, source_target_pairs={{0,1},{1,0},{2,3},{3,2},{4,5},{5,4},{6,7},{7,6},{8,9},{9,8},{10,11... | collective-permute-start | bytes 417800 | tf_op jit(solution)/shard_map/ppermute | solution.py:42
  36.0 10.4 %collective-permute-start.12 = (f32[512,128]{1,0:T(8,128)S(1)}, f32[512,128]{1,0:T(8,128)S(1)}, u32[]{:S(2)}, u32[]{:S(2)}) collective-permute-start(f32[512,128]{1,0:T(8,128)S(1)} %get-tuple-element.92), channel_id=1, source_target_pairs={{32,64},{64,32},{96,0},{0,96},{33,65},{65,33},{97,1},{1,97},{34,66... | collective-permute-start | bytes 786440 | tf_op jit(solution)/shard_map/ppermute | solution.py:42
  42.2 9.7 %collective-permute-start.13 = (f32[576,128]{1,0:T(8,128)S(1)}, f32[576,128]{1,0:T(8,128)S(1)}, u32[]{:S(2)}, u32[]{:S(2)}) collective-permute-start(f32[576,128]{1,0:T(8,128)S(1)} %get-tuple-element.95.rest_8_), channel_id=1, source_target_pairs={{0,8},{8,0},{16,24},{24,16},{1,9},{9,1},{17,25},{25,17},{2,10},{10... | collective-permute-start | bytes 884744 | tf_op jit(solution)/shard_map/ppermute | solution.py:42
  43.1 10.0 %collective-permute-start.14 = (f32[576,128]{1,0:T(8,128)S(1)}, f32[576,128]{1,0:T(8,128)S(1)}, u32[]{:S(2)}, u32[]{:S(2)}) collective-permute-start(f32[576,128]{1,0:T(8,128)S(1)} %get-tuple-element.96.rest_9_), channel_id=1, source_target_pairs={{8,16},{16,8},{24,0},{0,24},{9,17},{17,9},{25,1},{1,25},{10,18},{1... | collective-permute-start | bytes 884744 | tf_op jit(solution)/shard_map/ppermute | solution.py:42
  44.9 7.0 %collective-permute-start.17 = (f32[512,128]{1,0:T(8,128)S(1)}, f32[512,128]{1,0:T(8,128)S(1)}, u32[]{:S(2)}, u32[]{:S(2)}) collective-permute-start(f32[512,128]{1,0:T(8,128)S(1)} %get-tuple-element.99), channel_id=1, source_target_pairs={{0,32},{32,0},{64,96},{96,64},{1,33},{33,1},{65,97},{97,65},{2,34}... | collective-permute-start | bytes 786440 | tf_op jit(solution)/shard_map/ppermute | solution.py:42
  44.9 7.0 %collective-permute-start.15 = (f32[288,128]{1,0:T(8,128)S(1)}, f32[288,128]{1,0:T(8,128)S(1)}, u32[]{:S(2)}, u32[]{:S(2)}) collective-permute-start(f32[288,128]{1,0:T(8,128)S(1)} %get-tuple-element.97.rest_10_), channel_id=1, source_target_pairs={{1,2},{2,1},{3,4},{4,3},{5,6},{6,5},{7,0},{0,7},{9,10},{10,9},{11,... | collective-permute-start | bytes 442376 | tf_op jit(solution)/shard_map/ppermute | solution.py:42
  46.5 5.4 %collective-permute-start.16 = (f32[288,128]{1,0:T(8,128)S(1)}, f32[288,128]{1,0:T(8,128)S(1)}, u32[]{:S(2)}, u32[]{:S(2)}) collective-permute-start(f32[288,128]{1,0:T(8,128)S(1)} %get-tuple-element.98.rest_11_), channel_id=1, source_target_pairs={{0,1},{1,0},{2,3},{3,2},{4,5},{5,4},{6,7},{7,6},{8,9},{9,8},{10,11... | collective-permute-start | bytes 442376 | tf_op jit(solution)/shard_map/ppermute | solution.py:42
  46.7 1.7 %copy-start.4 = (f32[2,4,128]{2,1,0:T(4,128)S(1)}, f32[2,4,128]{2,1,0:T(4,128)}, u32[]{:S(2)}) copy-start(f32[2,4,128]{2,1,0:T(4,128)} %thetas.11) | copy-start | bytes 12292
  55.1 6.9 %collective-permute-start.21 = (f32[256,128]{1,0:T(8,128)S(1)}, f32[256,128]{1,0:T(8,128)S(1)}, u32[]{:S(2)}, u32[]{:S(2)}) collective-permute-start(f32[256,128]{1,0:T(8,128)S(1)} %get-tuple-element.110.rest_2_.rest_7_), channel_id=1, source_target_pairs={{1,2},{2,1},{3,4},{4,3},{5,6},{6,5},{7,0},{0,7},{9,10},{10,9},{11,... | collective-permute-start | bytes 393224 | tf_op jit(solution)/shard_map/ppermute | solution.py:42
  56.0 14.3 %collective-permute-start.23 = (f32[512,128]{1,0:T(8,128)S(1)}, f32[512,128]{1,0:T(8,128)S(1)}, u32[]{:S(2)}, u32[]{:S(2)}) collective-permute-start(f32[512,128]{1,0:T(8,128)S(1)} %get-tuple-element.112.rest_4_), channel_id=1, source_target_pairs={{0,32},{32,0},{64,96},{96,64},{1,33},{33,1},{65,97},{97,65},{2,34}... | collective-permute-start | bytes 786440 | tf_op jit(solution)/shard_map/ppermute | solution.py:42
  57.3 13.0 %collective-permute-start.19 = (f32[512,128]{1,0:T(8,128)S(1)}, f32[512,128]{1,0:T(8,128)S(1)}, u32[]{:S(2)}, u32[]{:S(2)}) collective-permute-start(f32[512,128]{1,0:T(8,128)S(1)} %get-tuple-element.108.rest_0_.rest_5_), channel_id=1, source_target_pairs={{0,8},{8,0},{16,24},{24,16},{1,9},{9,1},{17,25},{25,17},{2,10},{10... | collective-permute-start | bytes 786440 | tf_op jit(solution)/shard_map/ppermute | solution.py:42
  57.6 12.7 %collective-permute-start.20 = (f32[512,128]{1,0:T(8,128)S(1)}, f32[512,128]{1,0:T(8,128)S(1)}, u32[]{:S(2)}, u32[]{:S(2)}) collective-permute-start(f32[512,128]{1,0:T(8,128)S(1)} %get-tuple-element.109.rest_1_.rest_6_), channel_id=1, source_target_pairs={{8,16},{16,8},{24,0},{0,24},{9,17},{17,9},{25,1},{1,25},{10,18},{1... | collective-permute-start | bytes 786440 | tf_op jit(solution)/shard_map/ppermute | solution.py:42
  58.2 12.1 %collective-permute-start.18 = (f32[512,128]{1,0:T(8,128)S(1)}, f32[512,128]{1,0:T(8,128)S(1)}, u32[]{:S(2)}, u32[]{:S(2)}) collective-permute-start(f32[512,128]{1,0:T(8,128)S(1)} %get-tuple-element.100.d1), channel_id=1, source_target_pairs={{32,64},{64,32},{96,0},{0,96},{33,65},{65,33},{97,1},{1,97},{34,66... | collective-permute-start | bytes 786440 | tf_op jit(solution)/shard_map/ppermute | solution.py:42
  62.0 4.1 %collective-permute-start.22 = (f32[256,128]{1,0:T(8,128)S(1)}, f32[256,128]{1,0:T(8,128)S(1)}, u32[]{:S(2)}, u32[]{:S(2)}) collective-permute-start(f32[256,128]{1,0:T(8,128)S(1)} %get-tuple-element.111.rest_3_.rest_8_), channel_id=1, source_target_pairs={{0,1},{1,0},{2,3},{3,2},{4,5},{5,4},{6,7},{7,6},{8,9},{9,8},{10,11... | collective-permute-start | bytes 393224 | tf_op jit(solution)/shard_map/ppermute | solution.py:42
  66.1 9.0 %collective-permute-start.24 = (f32[512,128]{1,0:T(8,128)S(1)}, f32[512,128]{1,0:T(8,128)S(1)}, u32[]{:S(2)}, u32[]{:S(2)}) collective-permute-start(f32[512,128]{1,0:T(8,128)S(1)} %get-tuple-element.116), channel_id=1, source_target_pairs={{32,64},{64,32},{96,0},{0,96},{33,65},{65,33},{97,1},{1,97},{34,66... | collective-permute-start | bytes 786440 | tf_op jit(solution)/shard_map/ppermute | solution.py:42
  71.0 14.0 %collective-permute-start.25 = (f32[544,128]{1,0:T(8,128)S(1)}, f32[544,128]{1,0:T(8,128)S(1)}, u32[]{:S(2)}, u32[]{:S(2)}) collective-permute-start(f32[544,128]{1,0:T(8,128)S(1)} %get-tuple-element.118.rest_9_), channel_id=1, source_target_pairs={{0,8},{8,0},{16,24},{24,16},{1,9},{9,1},{17,25},{25,17},{2,10},{10... | collective-permute-start | bytes 835592 | tf_op jit(solution)/shard_map/ppermute | solution.py:42
  71.4 13.5 %collective-permute-start.26 = (f32[544,128]{1,0:T(8,128)S(1)}, f32[544,128]{1,0:T(8,128)S(1)}, u32[]{:S(2)}, u32[]{:S(2)}) collective-permute-start(f32[544,128]{1,0:T(8,128)S(1)} %get-tuple-element.119.rest_10_), channel_id=1, source_target_pairs={{8,16},{16,8},{24,0},{0,24},{9,17},{17,9},{25,1},{1,25},{10,18},{1... | collective-permute-start | bytes 835592 | tf_op jit(solution)/shard_map/ppermute | solution.py:42
  73.2 11.7 %collective-permute-start.29 = (f32[512,128]{1,0:T(8,128)S(1)}, f32[512,128]{1,0:T(8,128)S(1)}, u32[]{:S(2)}, u32[]{:S(2)}) collective-permute-start(f32[512,128]{1,0:T(8,128)S(1)} %get-tuple-element.122), channel_id=1, source_target_pairs={{0,32},{32,0},{64,96},{96,64},{1,33},{33,1},{65,97},{97,65},{2,34}... | collective-permute-start | bytes 786440 | tf_op jit(solution)/shard_map/ppermute | solution.py:42
  73.2 6.8 %collective-permute-start.27 = (f32[272,128]{1,0:T(8,128)S(1)}, f32[272,128]{1,0:T(8,128)S(1)}, u32[]{:S(2)}, u32[]{:S(2)}) collective-permute-start(f32[272,128]{1,0:T(8,128)S(1)} %get-tuple-element.120.rest_11_), channel_id=1, source_target_pairs={{1,2},{2,1},{3,4},{4,3},{5,6},{6,5},{7,0},{0,7},{9,10},{10,9},{11,... | collective-permute-start | bytes 417800 | tf_op jit(solution)/shard_map/ppermute | solution.py:42
  75.1 9.9 %collective-permute-start.28 = (f32[272,128]{1,0:T(8,128)S(1)}, f32[272,128]{1,0:T(8,128)S(1)}, u32[]{:S(2)}, u32[]{:S(2)}) collective-permute-start(f32[272,128]{1,0:T(8,128)S(1)} %get-tuple-element.121.rest_12_), channel_id=1, source_target_pairs={{0,1},{1,0},{2,3},{3,2},{4,5},{5,4},{6,7},{7,6},{8,9},{9,8},{10,11... | collective-permute-start | bytes 417800 | tf_op jit(solution)/shard_map/ppermute | solution.py:42
  80.1 9.7 %collective-permute-start.30 = (f32[512,128]{1,0:T(8,128)S(1)}, f32[512,128]{1,0:T(8,128)S(1)}, u32[]{:S(2)}, u32[]{:S(2)}) collective-permute-start(f32[512,128]{1,0:T(8,128)S(1)} %get-tuple-element.126), channel_id=1, source_target_pairs={{32,64},{64,32},{96,0},{0,96},{33,65},{65,33},{97,1},{1,97},{34,66... | collective-permute-start | bytes 786440 | tf_op jit(solution)/shard_map/ppermute | solution.py:42
  85.7 8.7 %collective-permute-start.31 = (f32[576,128]{1,0:T(8,128)S(1)}, f32[576,128]{1,0:T(8,128)S(1)}, u32[]{:S(2)}, u32[]{:S(2)}) collective-permute-start(f32[576,128]{1,0:T(8,128)S(1)} %get-tuple-element.129.rest_13_), channel_id=1, source_target_pairs={{0,8},{8,0},{16,24},{24,16},{1,9},{9,1},{17,25},{25,17},{2,10},{10... | collective-permute-start | bytes 884744 | tf_op jit(solution)/shard_map/ppermute | solution.py:42
  86.6 10.0 %collective-permute-start.32 = (f32[576,128]{1,0:T(8,128)S(1)}, f32[576,128]{1,0:T(8,128)S(1)}, u32[]{:S(2)}, u32[]{:S(2)}) collective-permute-start(f32[576,128]{1,0:T(8,128)S(1)} %get-tuple-element.130.rest_14_), channel_id=1, source_target_pairs={{8,16},{16,8},{24,0},{0,24},{9,17},{17,9},{25,1},{1,25},{10,18},{1... | collective-permute-start | bytes 884744 | tf_op jit(solution)/shard_map/ppermute | solution.py:42
  87.4 7.0 %collective-permute-start.35 = (f32[512,128]{1,0:T(8,128)S(1)}, f32[512,128]{1,0:T(8,128)S(1)}, u32[]{:S(2)}, u32[]{:S(2)}) collective-permute-start(f32[512,128]{1,0:T(8,128)S(1)} %get-tuple-element.133), channel_id=1, source_target_pairs={{0,32},{32,0},{64,96},{96,64},{1,33},{33,1},{65,97},{97,65},{2,34}... | collective-permute-start | bytes 786440 | tf_op jit(solution)/shard_map/ppermute | solution.py:42
  87.4 7.0 %collective-permute-start.33 = (f32[288,128]{1,0:T(8,128)S(1)}, f32[288,128]{1,0:T(8,128)S(1)}, u32[]{:S(2)}, u32[]{:S(2)}) collective-permute-start(f32[288,128]{1,0:T(8,128)S(1)} %get-tuple-element.131.rest_15_), channel_id=1, source_target_pairs={{1,2},{2,1},{3,4},{4,3},{5,6},{6,5},{7,0},{0,7},{9,10},{10,9},{11,... | collective-permute-start | bytes 442376 | tf_op jit(solution)/shard_map/ppermute | solution.py:42
  89.8 4.7 %collective-permute-start.34 = (f32[288,128]{1,0:T(8,128)S(1)}, f32[288,128]{1,0:T(8,128)S(1)}, u32[]{:S(2)}, u32[]{:S(2)}) collective-permute-start(f32[288,128]{1,0:T(8,128)S(1)} %get-tuple-element.132.rest_16_), channel_id=1, source_target_pairs={{0,1},{1,0},{2,3},{3,2},{4,5},{5,4},{6,7},{7,6},{8,9},{9,8},{10,11... | collective-permute-start | bytes 442376 | tf_op jit(solution)/shard_map/ppermute | solution.py:42

commit v4 on v3

--- a/solution.py
+++ b/solution.py
@@ -80,14 +80,6 @@
 def cross_base(depth):
     up = side(*CROSS)
     return pl.multiple_of(up * ((NX - depth) * PLANE) + (1 - up) * ((depth - 1) * PLANE), PLANE)
-
-
-def loop(n, body, unroll=4):
-    def step(i, c):
-        body(i)
-        return c
-
-    lax.fori_loop(0, n, step, 0, unroll=unroll)
 
 
 def copy_plane(src, base, dst):
@@ -199,21 +191,12 @@
     plane((NX - 1) * PLANE, True, False)
 
 
-def ghost_pass(half, g, inner, inner_base, a2, prior, out):
+def ghost_pass(half, g, inner, inner_base, outer, a2, prior, out):
     def emit(r, n):
-        v = a2[rows8(0, r), :] * (n + inner[rows8(inner_base, r), :])
+        v = a2[rows8(0, r), :] * (n + inner[rows8(inner_base, r), :] + outer[rows8(0, r), :])
         out[rows8(0, r), :] = 0.5 * v if half else v - prior[rows8(0, r), :]
 
     yz_sums(g, 0, emit)
-
-
-def ghost_add(half, g, a2, outer, out):
-    def body(i):
-        rows = pl.ds(pl.multiple_of(i * 64, 64), 64)
-        r = a2[rows, :] * outer[rows, :]
-        out[rows, :] = g[rows, :] + (0.5 * r if half else r)
-
-    loop(PLANE // 64, body)
 
 
 def spread(tile, emit):
@@ -274,7 +257,7 @@
             send[pl.ds(x * LINE[axis], LINE[axis]), :] = jnp.where(side(axis, kind) == 1, high, low)
 
 
-def aux_kernel(sv, fv, weights, w0, a2, w4, *faces):
+def aux_kernel(sv, fv, w0, a2, *faces):
     for x in range(NX):
 
         def emit(j, b, x=x):
@@ -283,7 +266,20 @@
             a2[rows, :] = -2.0 * (b * b)
 
         spread(sv[x], emit)
-    for (axis, kind), face in zip(LOCALS, faces):
+    for (axis, kind), face in zip(LOCALS[2:4], faces):
+        emit_face(a2, axis, kind, face)
+
+
+def ghost_aux_kernel(d, a2g):
+    def emit(j, b):
+        a2g[pl.ds(j * NZ, NZ), :] = -2.0 * (b * b)
+
+    spread(d[PLANE:, :], emit)
+
+
+def ghost1_kernel(d, a2, weights, a2g, w4, *faces):
+    ghost_aux_kernel(d, a2g)
+    for (axis, kind), face in zip(LOCALS[:2], faces):
         emit_face(a2, axis, kind, face)
     for layer in range(2):
         w = weights[layer]
@@ -294,26 +290,19 @@
         w4[layer, C:, :] = both
 
 
-def ghost_aux_kernel(d, a2g):
-    def emit(j, b):
-        a2g[pl.ds(j * NZ, NZ), :] = -2.0 * (b * b)
-
-    spread(d[PLANE:, :], emit)
-
-
 def local1_kernel(w0, a2, w1):
     local_pass(True, w0, a2, None, w1)
 
 
-def local2_kernel(w1, a2, w0, d1, a2g1, w2, p1):
+def local2_kernel(w1, a2, w0, d1, d2, a2g1, w2, p1):
     local_pass(False, w1, a2, w0, w2)
-    ghost_pass(True, d1, w0, cross_base(1), a2g1, None, p1)
-
-
-def local3_kernel(w2, a2, w1, d1, d2, w1g1, a2g1, a2g2, w3, p2, q1):
+    ghost_pass(True, d1, w0, cross_base(1), d2, a2g1, None, p1)
+
+
+def local3_kernel(w2, a2, w1, d1, d2, d3, w1g1, a2g1, a2g2, w3, q1, p2):
     local_pass(False, w2, a2, w1, w3)
-    ghost_pass(True, d2, d1, 0, a2g2, None, p2)
-    ghost_pass(False, w1g1, w1, cross_base(1), a2g1, d1, q1)
+    ghost_pass(True, d2, d1, 0, d3, a2g2, None, p2)
+    ghost_pass(False, w1g1, w1, cross_base(1), p2, a2g1, d1, q1)
 
 
 def fix1_kernel(w_in, a2, z1, z0, d1, *rest):
@@ -324,17 +313,17 @@
 
 def fix2_kernel(w_in, a2, z1, z0, d2, p1, a2g1, *rest):
     halos, w, w1g1, sends = rest[:5], rest[5], rest[6], rest[7:]
-    ghost_add(True, p1, a2g1, d2, w1g1)
     fix_lines(True, w1g1, a2g1, halos, 0)
     fix_faces(False, w, a2, (z1, z0), halos, w1g1, sends)
     emit_ghost_lines((w1g1, d2), sends)
 
 
-def fix3(w, a2, zfaces, d3, p2, q1, a2g1, a2g2, halos, g2, g1, faces):
-    ghost_add(True, p2, a2g2, d3, g2)
-    fix_lines(True, g2, a2g2, halos, 1)
-    ghost_add(False, q1, a2g1, g2, g1)
-    fix_lines(False, g1, a2g1, halos, 0)
+def fix3(w, a2, zfaces, q1, a2g1, a2g2, halos, g1, faces):
+    copy_plane(q1, 0, g1)
+    for (axis, kind), halo in zip(LOCALS[:-1], halos):
+        at = plane_line(axis, kind)
+        beyond = 0.5 * (a2g2[at, :] * halo[line_rows(axis, 1), :]) + halo[line_rows(axis, 0), :]
+        g1[at, :] = g1[at, :] + a2g1[at, :] * beyond
     fix_faces(False, w, a2, zfaces, halos, g1, (*faces, None))
 
 
@@ -360,9 +349,9 @@
         dst[pl.ds(at + i * 256, 256), :] = mixed(layer, ws, a2, thetas, w4, rows, scaled)
 
 
-def cross_mix_kernel(layer, w3_in, a2, z1, z0, d3, p2, q1, a2g1, a2g2, w0, w1, w2, thetas, w4, *rest):
-    halos, w3, d1, faces, (g2, g1) = rest[:5], rest[5], rest[6], rest[7:11], rest[11:]
-    fix3(w3, a2, (z1, z0), d3, p2, q1, a2g1, a2g2, halos, g2, g1, faces)
+def cross_mix_kernel(layer, w3_in, a2, z1, z0, q1, a2g1, a2g2, w0, w1, w2, thetas, w4, *rest):
+    halos, w3, d1, faces, g1 = rest[:5], rest[5], rest[6], rest[7:11], rest[11]
+    fix3(w3, a2, (z1, z0), q1, a2g1, a2g2, halos, g1, faces)
     mix_planes(layer, (w0, w1, w2, w3), a2, thetas, w4, CROSS, d1, True)
 
 
@@ -416,10 +405,10 @@
     copy_plane(out, cross_base(3), d3)
 
 
-def last_kernel(layer, w3_in, a2, z1, z0, d3, p2, q1, a2g1, a2g2, w0, w1, w2, thetas, w4, inner, *rest):
+def last_kernel(layer, w3_in, a2, z1, z0, q1, a2g1, a2g2, w0, w1, w2, thetas, w4, inner, *rest):
     halos, known = rest[:5], rest[5:21]
-    (w3, hidden, out), (g2, g1), faces, done, sems = rest[21:24], rest[24:26], rest[26:30], rest[30:34], rest[34]
-    fix3(w3, a2, (z1, z0), d3, p2, q1, a2g1, a2g2, halos, g2, g1, faces)
+    (w3, hidden, out), g1, faces, done, sems = rest[21:24], rest[24], rest[25:29], rest[29:33], rest[33]
+    fix3(w3, a2, (z1, z0), q1, a2g1, a2g2, halos, g1, faces)
 
     def copy(i):
         rows = pl.ds(i * PLANE, PLANE)
@@ -455,7 +444,7 @@
     feat = pltpu.with_memory_space_constraint(fv, pltpu.HBM)
     block, plane = arr(ROWS), arr(PLANE)
     scales = pltpu.with_memory_space_constraint(scales, pltpu.HBM)
-    ghosts = [pltpu.VMEM((PLANE, C), F32)] * 2
+    ghosts = [pltpu.VMEM((PLANE, C), F32)]
     (s1,) = call(
         first_kernel,
         [arr(PLANE + SCALES)],
@@ -476,26 +465,27 @@
         known = [sends[:4]]
         (d1,), halos, (d2,) = exchange(sends, cross=s1, late=s2)
         if not last:
-            w4 = jax.ShapeDtypeStruct((2, 2 * C, 2 * C), jnp.bfloat16)
-            w0, a2, w4, *af = call(aux_kernel, [block, block, w4] + locals_out(0)[:4], (sv, fv, weights))
-            main = (a2, af[2], af[3])
+            w0, a2, *az = call(aux_kernel, [block, block] + locals_out(0)[2:4], (sv, fv))
+            main = (a2, *az)
         (w1,) = call(local1_kernel, [block], (w0, a2))
         w1, *sends = call(fix1_kernel, [block] + locals_out(1), (w1, *main, d1, *halos), aliases={0: 0})
         known.append(sends[:4])
         _, halos, (d3,) = exchange(sends, late=s3)
         if not last:
-            (a2g1,) = call(ghost_aux_kernel, [plane], (d1,))
-        w2, p1 = call(local2_kernel, [block, plane], (w1, a2, w0, d1, a2g1))
+            w4 = jax.ShapeDtypeStruct((2, 2 * C, 2 * C), jnp.bfloat16)
+            a2g1, w4, *ay = call(ghost1_kernel, [plane, w4] + locals_out(0)[:2], (d1, a2, weights))
+            af = (*ay, *az)
+        w2, p1 = call(local2_kernel, [block, plane], (w1, a2, w0, d1, d2, a2g1))
         w2, w1g1, *sends = call(
-            fix2_kernel, [block, plane] + locals_out(2), (w2, *main, d2, p1, a2g1, *halos), aliases={0: 0}
+            fix2_kernel, [block, plane] + locals_out(2), (w2, *main, d2, p1, a2g1, *halos), aliases={0: 0, 5: 1}
         )
         known.append(sends[:4])
         _, halos, _ = exchange(sends)
         if not last:
             (a2g2,) = call(ghost_aux_kernel, [plane], (d2,))
-        w3, p2, q1 = call(local3_kernel, [block, plane, plane], (w2, a2, w1, d1, d2, w1g1, a2g1, a2g2))
+        w3, q1 = call(local3_kernel, [block, plane], (w2, a2, w1, d1, d2, d3, w1g1, a2g1, a2g2), scratch=ghosts)
         (inner,) = call(functools.partial(inner_mix_kernel, layer, not last), [block], (w0, w1, w2, w3, a2, thetas, w4))
-        tail = (w3, *main, d3, p2, q1, a2g1, a2g2, w0, w1, w2, thetas, w4)
+        tail = (w3, *main, q1, a2g1, a2g2, w0, w1, w2, thetas, w4)
         if not last:
             w3, s1, *faces = call(
                 functools.partial(cross_mix_kernel, layer),

time: 100 us -> 100 us (level)
  no operation moved by 1% of the time
where the time goes in v4:
time: 100 us; the launch traced here: 99.8 us
  starting transfers between devices  43.6 us (44%)
  Pallas kernels  26.5 us (26%)
  waiting for transfers between devices  26.1 us (26%)
  local copies, waits for them, and re-layouts  3.11 us (3%)
    ppermute x36, starting transfers between devices, swap(): return lax.ppermute(x, axis, pairs)  43.6 us
    pallas_call x21, Pallas kernels, call(): pl.pallas_call(kernel, out_shape=out_shape, in_specs=[HBM if i in in_hbm...  26.5 us
    ppermute x36, waiting for transfers between devices, swap(): return lax.ppermute(x, axis, pairs)  26.1 us
    unnamed x12, local copies, waits for them, and re-layouts  3.11 us
  transfers between devices with their start and end apart: 36, of which 12 were waited for; matrix products, arithmetic and copies ran while one was open for 0% of the time, Pallas kernels for 21%

profile of v4, /device:TPU:1, one launch (start us, length us, event | category | flops | bytes accessed | tf_op | source)
XLA Modules:
  0.0 99.8 jit_solution(985491071576907048)
XLA Ops:
  0.0 2.2 %copy-done = f32[16,16,32,128]{3,2,1,0:T(8,128)S(1)} copy-done((f32[16,16,32,128]{3,2,1,0:T(8,128)S(1)}, f32[16,16,32,128]{3,2,1,0:T(8,128)}, u32[]{:S(2)}) %copy-start) | copy-done | bytes 4194328
  2.2 0.9 copy-done.2
  3.8 5.7 %collective-permute-start.3 = (f32[256,128]{1,0:T(8,128)S(1)}, f32[256,128]{1,0:T(8,128)S(1)}, u32[]{:S(2)}, u32[]{:S(2)}) collective-permute-start(f32[256,128]{1,0:T(8,128)S(1)} %get-tuple-element.75.rest_2_), channel_id=1, source_target_pairs={{1,2},{2,1},{3,4},{4,3},{5,6},{6,5},{7,0},{0,7},{9,10},{10,9},{11,... | collective-permute-start | bytes 393224 | tf_op jit(solution)/shard_map/ppermute | solution.py:42
  9.4 1.2 %shard_map.48 = f32[528,128]{1,0:T(8,128)S(1)} custom-call(f32[8192,128]{1,0:T(8,128)} %bitcast.2, f32[16,16,32]{2,1,0:T(8,128)} %sv.3), custom_call_target="tpu_custom_call" | custom-call | tf_op jit(solution)/shard_map/pallas_call | solution.py:430
  10.7 3.5 %collective-permute-start = (f32[528,128]{1,0:T(8,128)S(1)}, f32[528,128]{1,0:T(8,128)S(1)}, u32[]{:S(2)}, u32[]{:S(2)}) collective-permute-start(f32[528,128]{1,0:T(8,128)S(1)} %shard_map.48), channel_id=1, source_target_pairs={{32,64},{64,32},{96,0},{0,96},{33,65},{65,33},{97,1},{1,97},{34,66... | collective-permute-start | bytes 811016 | tf_op jit(solution)/shard_map/ppermute | solution.py:42
  14.2 1.2 %collective-permute-start.1 = (f32[512,128]{1,0:T(8,128)S(1)}, f32[512,128]{1,0:T(8,128)S(1)}, u32[]{:S(2)}, u32[]{:S(2)}) collective-permute-start(f32[512,128]{1,0:T(8,128)S(1)} %get-tuple-element.73.rest_0_), channel_id=1, source_target_pairs={{0,8},{8,0},{16,24},{24,16},{1,9},{9,1},{17,25},{25,17},{2,10},{10... | collective-permute-start | bytes 786440 | tf_op jit(solution)/shard_map/ppermute | solution.py:42
  15.4 1.8 %collective-permute-start.2 = (f32[512,128]{1,0:T(8,128)S(1)}, f32[512,128]{1,0:T(8,128)S(1)}, u32[]{:S(2)}, u32[]{:S(2)}) collective-permute-start(f32[512,128]{1,0:T(8,128)S(1)} %get-tuple-element.74.rest_1_), channel_id=1, source_target_pairs={{8,16},{16,8},{24,0},{0,24},{9,17},{17,9},{25,1},{1,25},{10,18},{1... | collective-permute-start | bytes 786440 | tf_op jit(solution)/shard_map/ppermute | solution.py:42
  17.3 4.1 %collective-permute-done.4.rest_3_ = f32[256,128]{1,0:T(8,128)S(1)} collective-permute-done((f32[256,128]{1,0:T(8,128)S(1)}, f32[256,128]{1,0:T(8,128)S(1)}, u32[]{:S(2)}, u32[]{:S(2)}) %collective-permute-start.4) | collective-permute-done | bytes 131104 | tf_op jit(solution)/shard_map/ppermute | solution.py:42
  21.4 2.2 %collective-permute-start.6 = (f32[528,128]{1,0:T(8,128)S(1)}, f32[528,128]{1,0:T(8,128)S(1)}, u32[]{:S(2)}, u32[]{:S(2)}) collective-permute-start(f32[528,128]{1,0:T(8,128)S(1)} %get-tuple-element.79), channel_id=1, source_target_pairs={{32,64},{64,32},{96,0},{0,96},{33,65},{65,33},{97,1},{1,97},{34,66... | collective-permute-start | bytes 811016 | tf_op jit(solution)/shard_map/ppermute | solution.py:42
  23.5 2.0 %shard_map.46 = (f32[8192,128]{1,0:T(8,128)S(1)}, f32[8192,128]{1,0:T(8,128)S(1)}, f32[256,128]{1,0:T(8,128)S(1)}, f32[256,128]{1,0:T(8,128)S(1)}) custom-call(f32[16,16,32]{2,1,0:T(8,128)S(1)} %copy-done.3, f32[8192,128]{1,0:T(8,128)S(1)} %bitcast.4), custom_call_target="tpu_custom_call" | custom-call | tf_op jit(solution)/shard_map/pallas_call | solution.py:430
  25.5 1.5 %shard_map.47.w_in = f32[8192,128]{1,0:T(8,128)S(1)} custom-call(f32[8192,128]{1,0:T(8,128)S(1)} %get-tuple-element.69.w0, f32[8192,128]{1,0:T(8,128)S(1)} %get-tuple-element.70.a2), custom_call_target="tpu_custom_call" | custom-call | tf_op jit(solution)/shard_map/pallas_call | solution.py:430
  28.9 3.0 %collective-permute-start.9 = (f32[272,128]{1,0:T(8,128)S(1)}, f32[272,128]{1,0:T(8,128)S(1)}, u32[]{:S(2)}, u32[]{:S(2)}) collective-permute-start(f32[272,128]{1,0:T(8,128)S(1)} %get-tuple-element.85.rest_6_), channel_id=1, source_target_pairs={{1,2},{2,1},{3,4},{4,3},{5,6},{6,5},{7,0},{0,7},{9,10},{10,9},{11,... | collective-permute-start | bytes 417800 | tf_op jit(solution)/shard_map/ppermute | solution.py:42
  32.0 4.0 %collective-permute-done.9.rest_2_ = f32[272,128]{1,0:T(8,128)S(1)} collective-permute-done((f32[272,128]{1,0:T(8,128)S(1)}, f32[272,128]{1,0:T(8,128)S(1)}, u32[]{:S(2)}, u32[]{:S(2)}) %collective-permute-start.9) | collective-permute-done | bytes 139296 | tf_op jit(solution)/shard_map/ppermute | solution.py:42
  35.9 3.5 %collective-permute-start.12 = (f32[512,128]{1,0:T(8,128)S(1)}, f32[512,128]{1,0:T(8,128)S(1)}, u32[]{:S(2)}, u32[]{:S(2)}) collective-permute-start(f32[512,128]{1,0:T(8,128)S(1)} %get-tuple-element.89), channel_id=1, source_target_pairs={{32,64},{64,32},{96,0},{0,96},{33,65},{65,33},{97,1},{1,97},{34,66... | collective-permute-start | bytes 786440 | tf_op jit(solution)/shard_map/ppermute | solution.py:42
  39.7 1.6 %shard_map.52 = (f32[8192,128]{1,0:T(8,128)S(1)}, f32[512,128]{1,0:T(8,128)S(1)}) custom-call(f32[8192,128]{1,0:T(8,128)S(1)} %get-tuple-element.78.w1, f32[8192,128]{1,0:T(8,128)S(1)} %get-tuple-element.70.a2, f32[8192,128]{1,0:T(8,128)S(1)} %get-tuple-element.69.w0, f32[528,128]{1,0:T(8,128)S(1)} %collective-permute-done.d1.d, ...), custom_call_target="tpu_custom_call" | custom-call | tf_op jit(solution)/shard_map/pallas_call | solution.py:430
  41.4 0.7 shard_map.53
  42.1 0.8 collective-permute-start.13
  43.0 1.8 %collective-permute-start.14 = (f32[576,128]{1,0:T(8,128)S(1)}, f32[576,128]{1,0:T(8,128)S(1)}, u32[]{:S(2)}, u32[]{:S(2)}) collective-permute-start(f32[576,128]{1,0:T(8,128)S(1)} %get-tuple-element.95.rest_9_), channel_id=1, source_target_pairs={{8,16},{16,8},{24,0},{0,24},{9,17},{17,9},{25,1},{1,25},{10,18},{1... | collective-permute-start | bytes 884744 | tf_op jit(solution)/shard_map/ppermute | solution.py:42
  44.8 1.6 %collective-permute-done.12.d3 = f32[512,128]{1,0:T(8,128)S(1)} collective-permute-done((f32[512,128]{1,0:T(8,128)S(1)}, f32[512,128]{1,0:T(8,128)S(1)}, u32[]{:S(2)}, u32[]{:S(2)}) %collective-permute-start.12) | collective-permute-done | bytes 262176 | tf_op jit(solution)/shard_map/ppermute | solution.py:42
  46.7 1.7 %shard_map.55 = (f32[8192,128]{1,0:T(8,128)S(1)}, f32[512,128]{1,0:T(8,128)S(1)}) custom-call(f32[8192,128]{1,0:T(8,128)S(1)} %get-tuple-element.88.w2, f32[8192,128]{1,0:T(8,128)S(1)} %get-tuple-element.70.a2, f32[8192,128]{1,0:T(8,128)S(1)} %get-tuple-element.78.w1, f32[528,128]{1,0:T(8,128)S(1)} %collective-permute-done.d1.d, ...), custom_call_target="tpu_custom_call" | custom-call | tf_op jit(solution)/shard_map/pallas_call | solution.py:430
  48.4 1.6 %shard_map.56.inner = f32[8192,128]{1,0:T(8,128)S(1)} custom-call(f32[8192,128]{1,0:T(8,128)S(1)} %get-tuple-element.69.w0, f32[8192,128]{1,0:T(8,128)S(1)} %get-tuple-element.78.w1, f32[8192,128]{1,0:T(8,128)S(1)} %get-tuple-element.88.w2, f32[8192,128]{1,0:T(8,128)S(1)} %get-tuple-element.91.w3.w3_in, f32[8192,128]{1,0:T(8,128)S(1)} %get-tuple-element.70.a2, ...), custom_call_target="tpu_custom_call" | custom-call | tf_op jit(solution)/shard_map/pallas_call | solution.py:430
  50.1 1.8 %collective-permute-done.15.rest_2_ = f32[288,128]{1,0:T(8,128)S(1)} collective-permute-done((f32[288,128]{1,0:T(8,128)S(1)}, f32[288,128]{1,0:T(8,128)S(1)}, u32[]{:S(2)}, u32[]{:S(2)}) %collective-permute-start.15) | collective-permute-done | bytes 147488 | tf_op jit(solution)/shard_map/ppermute | solution.py:42
  51.8 1.2 %collective-permute-done.14.rest_1_ = f32[576,128]{1,0:T(8,128)S(1)} collective-permute-done((f32[576,128]{1,0:T(8,128)S(1)}, f32[576,128]{1,0:T(8,128)S(1)}, u32[]{:S(2)}, u32[]{:S(2)}) %collective-permute-start.14) | collective-permute-done | bytes 294944 | tf_op jit(solution)/shard_map/ppermute | solution.py:42
  53.0 1.0 %shard_map.57 = (f32[8192,128]{1,0:T(8,128)S(1)}, f32[512,128]{1,0:T(8,128)S(1)}, f32[512,128]{1,0:T(8,128)S(1)}, f32[512,128]{1,0:T(8,128)S(1)}, f32[256,128]{1,0:T(8,128)S(1)}, /*index=5*/f32[256,128]{1,0:T(8,128)S(1)}) custom-call(f32[8192,128]{1,0:T(8,128)S(1)} %get-tuple-element.91.w3.w3_in, ...), custom_call_target="tpu_custom_call", output_to_operand_aliasing={{0}: (0, {})} | custom-call | tf_op jit(solution)/shard_map/pallas_call | solution.py:430
  54.0 0.9 shard_map.58
  54.9 0.9 collective-permute-start.21
  55.9 1.2 %collective-permute-start.23 = (f32[512,128]{1,0:T(8,128)S(1)}, f32[512,128]{1,0:T(8,128)S(1)}, u32[]{:S(2)}, u32[]{:S(2)}) collective-permute-start(f32[512,128]{1,0:T(8,128)S(1)} %get-tuple-element.111.rest_4_), channel_id=1, source_target_pairs={{0,32},{32,0},{64,96},{96,64},{1,33},{33,1},{65,97},{97,65},{2,34}... | collective-permute-start | bytes 786440 | tf_op jit(solution)/shard_map/ppermute | solution.py:42
  58.0 3.0 %collective-permute-start.18 = (f32[512,128]{1,0:T(8,128)S(1)}, f32[512,128]{1,0:T(8,128)S(1)}, u32[]{:S(2)}, u32[]{:S(2)}) collective-permute-start(f32[512,128]{1,0:T(8,128)S(1)} %get-tuple-element.99.d1), channel_id=1, source_target_pairs={{32,64},{64,32},{96,0},{0,96},{33,65},{65,33},{97,1},{1,97},{34,66... | collective-permute-start | bytes 786440 | tf_op jit(solution)/shard_map/ppermute | solution.py:42
  61.1 0.7 collective-permute-done.21.rest_2_
  61.8 1.4 %shard_map.59 = (f32[8192,128]{1,0:T(8,128)S(1)}, f32[512,128]{1,0:T(8,128)S(1)}, f32[512,128]{1,0:T(8,128)S(1)}) custom-call(f32[8192,128]{1,0:T(8,128)S(1)} %shard_map.56.inner, f32[512,128]{1,0:T(8,128)S(1)} %get-tuple-element.99.d1, f32[8192,128]{1,0:T(8,128)S(1)} %get-tuple-element.69.w0, ...), custom_call_target="tpu_custom_call", output_to_operand_aliasing={{0}: (0, {})} | custom-call | tf_op jit(solution)/shard_map/pallas_call | solution.py:430
  63.2 2.7 %collective-permute-done.22.rest_3_ = f32[256,128]{1,0:T(8,128)S(1)} collective-permute-done((f32[256,128]{1,0:T(8,128)S(1)}, f32[256,128]{1,0:T(8,128)S(1)}, u32[]{:S(2)}, u32[]{:S(2)}) %collective-permute-start.22) | collective-permute-done | bytes 131104 | tf_op jit(solution)/shard_map/ppermute | solution.py:42
  65.9 2.7 %collective-permute-start.24 = (f32[512,128]{1,0:T(8,128)S(1)}, f32[512,128]{1,0:T(8,128)S(1)}, u32[]{:S(2)}, u32[]{:S(2)}) collective-permute-start(f32[512,128]{1,0:T(8,128)S(1)} %get-tuple-element.114), channel_id=1, source_target_pairs={{32,64},{64,32},{96,0},{0,96},{33,65},{65,33},{97,1},{1,97},{34,66... | collective-permute-start | bytes 786440 | tf_op jit(solution)/shard_map/ppermute | solution.py:42
  68.6 1.5 %shard_map.60.w_in = f32[8192,128]{1,0:T(8,128)S(1)} custom-call(f32[8192,128]{1,0:T(8,128)S(1)} %get-tuple-element.112.w0, f32[8192,128]{1,0:T(8,128)S(1)} %get-tuple-element.70.a2), custom_call_target="tpu_custom_call" | custom-call | tf_op jit(solution)/shard_map/pallas_call | solution.py:430
  71.2 1.8 %collective-permute-start.26 = (f32[544,128]{1,0:T(8,128)S(1)}, f32[544,128]{1,0:T(8,128)S(1)}, u32[]{:S(2)}, u32[]{:S(2)}) collective-permute-start(f32[544,128]{1,0:T(8,128)S(1)} %get-tuple-element.118.rest_10_), channel_id=1, source_target_pairs={{8,16},{16,8},{24,0},{0,24},{9,17},{17,9},{25,1},{1,25},{10,18},{1... | collective-permute-start | bytes 835592 | tf_op jit(solution)/shard_map/ppermute | solution.py:42
  73.0 1.5 %collective-permute-start.27 = (f32[272,128]{1,0:T(8,128)S(1)}, f32[272,128]{1,0:T(8,128)S(1)}, u32[]{:S(2)}, u32[]{:S(2)}) collective-permute-start(f32[272,128]{1,0:T(8,128)S(1)} %get-tuple-element.119.rest_11_), channel_id=1, source_target_pairs={{1,2},{2,1},{3,4},{4,3},{5,6},{6,5},{7,0},{0,7},{9,10},{10,9},{11,... | collective-permute-start | bytes 417800 | tf_op jit(solution)/shard_map/ppermute | solution.py:42
  75.1 4.7 %collective-permute-done.27.rest_2_ = f32[272,128]{1,0:T(8,128)S(1)} collective-permute-done((f32[272,128]{1,0:T(8,128)S(1)}, f32[272,128]{1,0:T(8,128)S(1)}, u32[]{:S(2)}, u32[]{:S(2)}) %collective-permute-start.27) | collective-permute-done | bytes 139296 | tf_op jit(solution)/shard_map/ppermute | solution.py:42
  79.9 3.2 %collective-permute-start.30 = (f32[512,128]{1,0:T(8,128)S(1)}, f32[512,128]{1,0:T(8,128)S(1)}, u32[]{:S(2)}, u32[]{:S(2)}) collective-permute-start(f32[512,128]{1,0:T(8,128)S(1)} %get-tuple-element.123), channel_id=1, source_target_pairs={{32,64},{64,32},{96,0},{0,96},{33,65},{65,33},{97,1},{1,97},{34,66... | collective-permute-start | bytes 786440 | tf_op jit(solution)/shard_map/ppermute | solution.py:42
  83.1 1.6 %shard_map.62 = (f32[8192,128]{1,0:T(8,128)S(1)}, f32[512,128]{1,0:T(8,128)S(1)}) custom-call(f32[8192,128]{1,0:T(8,128)S(1)} %get-tuple-element.113.w1, f32[8192,128]{1,0:T(8,128)S(1)} %get-tuple-element.70.a2, f32[8192,128]{1,0:T(8,128)S(1)} %get-tuple-element.112.w0, f32[512,128]{1,0:T(8,128)S(1)} %collective-permute-done.18.d1, ...), custom_call_target="tpu_custom_call" | custom-call | tf_op jit(solution)/shard_map/pallas_call | solution.py:430
  84.8 0.7 shard_map.63
  85.5 0.8 collective-permute-start.31
  86.3 0.9 collective-permute-start.32
  87.2 0.9 collective-permute-start.33
  88.1 1.5 %collective-permute-done.30.d3 = f32[512,128]{1,0:T(8,128)S(1)} collective-permute-done((f32[512,128]{1,0:T(8,128)S(1)}, f32[512,128]{1,0:T(8,128)S(1)}, u32[]{:S(2)}, u32[]{:S(2)}) %collective-permute-start.30) | collective-permute-done | bytes 262176 | tf_op jit(solution)/shard_map/ppermute | solution.py:42
  89.6 1.7 %shard_map.64 = (f32[8192,128]{1,0:T(8,128)S(1)}, f32[512,128]{1,0:T(8,128)S(1)}) custom-call(f32[8192,128]{1,0:T(8,128)S(1)} %get-tuple-element.122.w2, f32[8192,128]{1,0:T(8,128)S(1)} %get-tuple-element.70.a2, f32[8192,128]{1,0:T(8,128)S(1)} %get-tuple-element.113.w1, f32[512,128]{1,0:T(8,128)S(1)} %collective-permute-done.18.d1, ...), custom_call_target="tpu_custom_call" | custom-call | tf_op jit(solution)/shard_map/pallas_call | solution.py:430
  91.3 1.4 %shard_map.65.inner = f32[8192,128]{1,0:T(8,128)S(1)} custom-call(f32[8192,128]{1,0:T(8,128)S(1)} %get-tuple-element.112.w0, f32[8192,128]{1,0:T(8,128)S(1)} %get-tuple-element.113.w1, f32[8192,128]{1,0:T(8,128)S(1)} %get-tuple-element.122.w2, f32[8192,128]{1,0:T(8,128)S(1)} %get-tuple-element.125.w3.w3_in, f32[8192,128]{1,0:T(8,128)S(1)} %get-tuple-element.70.a2, ...), custom_call_target="tpu_custom_call" | custom-call | tf_op jit(solution)/shard_map/pallas_call | solution.py:430
  92.7 1.5 %collective-permute-done.33.rest_2_ = f32[288,128]{1,0:T(8,128)S(1)} collective-permute-done((f32[288,128]{1,0:T(8,128)S(1)}, f32[288,128]{1,0:T(8,128)S(1)}, u32[]{:S(2)}, u32[]{:S(2)}) %collective-permute-start.33) | collective-permute-done | bytes 147488 | tf_op jit(solution)/shard_map/ppermute | solution.py:42
  94.2 2.1 %collective-permute-done.32.rest_1_ = f32[576,128]{1,0:T(8,128)S(1)} collective-permute-done((f32[576,128]{1,0:T(8,128)S(1)}, f32[576,128]{1,0:T(8,128)S(1)}, u32[]{:S(2)}, u32[]{:S(2)}) %collective-permute-start.32) | collective-permute-done | bytes 294944 | tf_op jit(solution)/shard_map/ppermute | solution.py:42
  96.3 3.3 %shard_map.66 = (f32[8192,128]{1,0:T(8,128)S(1)}, f32[8192,128]{1,0:T(8,128)S(1)}, f32[8192,128]{1,0:T(8,128)}) custom-call(f32[8192,128]{1,0:T(8,128)S(1)} %get-tuple-element.125.w3.w3_in, f32[8192,128]{1,0:T(8,128)S(1)} %get-tuple-element.70.a2, ...), custom_call_target="tpu_custom_call", output_to_operand_aliasing={{0}: (0, {}), {1}: (12, {})} | custom-call | tf_op jit(solution)/shard_map/pallas_call | solution.py:430
  (57 shorter events, 5.7 us)
Async XLA Ops:
  0.0 2.2 %copy-start = (f32[16,16,32,128]{3,2,1,0:T(8,128)S(1)}, f32[16,16,32,128]{3,2,1,0:T(8,128)}, u32[]{:S(2)}) copy-start(f32[16,16,32,128]{3,2,1,0:T(8,128)} %param.4) | copy-start | bytes 12582916
  2.2 0.9 copy-start.2
  3.1 20.4 %copy-start.1 = (f32[16,16,32,128]{3,2,1,0:T(8,128)S(1)}, f32[16,16,32,128]{3,2,1,0:T(8,128)}, u32[]{:S(2)}) copy-start(f32[16,16,32,128]{3,2,1,0:T(8,128)} %param.4) | copy-start | bytes 12582916
  3.1 20.4 %copy-start.3 = (f32[16,16,32]{2,1,0:T(8,128)S(1)}, f32[16,16,32]{2,1,0:T(8,128)}, u32[]{:S(2)}) copy-start(f32[16,16,32]{2,1,0:T(8,128)} %sv.3) | copy-start | bytes 98308
  3.8 13.5 %collective-permute-start.3 = (f32[256,128]{1,0:T(8,128)S(1)}, f32[256,128]{1,0:T(8,128)S(1)}, u32[]{:S(2)}, u32[]{:S(2)}) collective-permute-start(f32[256,128]{1,0:T(8,128)S(1)} %get-tuple-element.75.rest_2_), channel_id=1, source_target_pairs={{1,2},{2,1},{3,4},{4,3},{5,6},{6,5},{7,0},{0,7},{9,10},{10,9},{11,... | collective-permute-start | bytes 393224 | tf_op jit(solution)/shard_map/ppermute | solution.py:42
  10.7 16.4 %collective-permute-start = (f32[528,128]{1,0:T(8,128)S(1)}, f32[528,128]{1,0:T(8,128)S(1)}, u32[]{:S(2)}, u32[]{:S(2)}) collective-permute-start(f32[528,128]{1,0:T(8,128)S(1)} %shard_map.48), channel_id=1, source_target_pairs={{32,64},{64,32},{96,0},{0,96},{33,65},{65,33},{97,1},{1,97},{34,66... | collective-permute-start | bytes 811016 | tf_op jit(solution)/shard_map/ppermute | solution.py:42
  14.2 12.8 %collective-permute-start.5 = (f32[512,128]{1,0:T(8,128)S(1)}, f32[512,128]{1,0:T(8,128)S(1)}, u32[]{:S(2)}, u32[]{:S(2)}) collective-permute-start(f32[512,128]{1,0:T(8,128)S(1)} %get-tuple-element.77), channel_id=1, source_target_pairs={{0,32},{32,0},{64,96},{96,64},{1,33},{33,1},{65,97},{97,65},{2,34}... | collective-permute-start | bytes 786440 | tf_op jit(solution)/shard_map/ppermute | solution.py:42
  14.2 12.8 %collective-permute-start.1 = (f32[512,128]{1,0:T(8,128)S(1)}, f32[512,128]{1,0:T(8,128)S(1)}, u32[]{:S(2)}, u32[]{:S(2)}) collective-permute-start(f32[512,128]{1,0:T(8,128)S(1)} %get-tuple-element.73.rest_0_), channel_id=1, source_target_pairs={{0,8},{8,0},{16,24},{24,16},{1,9},{9,1},{17,25},{25,17},{2,10},{10... | collective-permute-start | bytes 786440 | tf_op jit(solution)/shard_map/ppermute | solution.py:42
  15.4 11.6 %collective-permute-start.2 = (f32[512,128]{1,0:T(8,128)S(1)}, f32[512,128]{1,0:T(8,128)S(1)}, u32[]{:S(2)}, u32[]{:S(2)}) collective-permute-start(f32[512,128]{1,0:T(8,128)S(1)} %get-tuple-element.74.rest_1_), channel_id=1, source_target_pairs={{8,16},{16,8},{24,0},{0,24},{9,17},{17,9},{25,1},{1,25},{10,18},{1... | collective-permute-start | bytes 786440 | tf_op jit(solution)/shard_map/ppermute | solution.py:42
  17.3 4.1 %collective-permute-start.4 = (f32[256,128]{1,0:T(8,128)S(1)}, f32[256,128]{1,0:T(8,128)S(1)}, u32[]{:S(2)}, u32[]{:S(2)}) collective-permute-start(f32[256,128]{1,0:T(8,128)S(1)} %get-tuple-element.76.rest_3_), channel_id=1, source_target_pairs={{0,1},{1,0},{2,3},{3,2},{4,5},{5,4},{6,7},{7,6},{8,9},{9,8},{10,11... | collective-permute-start | bytes 393224 | tf_op jit(solution)/shard_map/ppermute | solution.py:42
  21.4 10.6 %collective-permute-start.6 = (f32[528,128]{1,0:T(8,128)S(1)}, f32[528,128]{1,0:T(8,128)S(1)}, u32[]{:S(2)}, u32[]{:S(2)}) collective-permute-start(f32[528,128]{1,0:T(8,128)S(1)} %get-tuple-element.79), channel_id=1, source_target_pairs={{32,64},{64,32},{96,0},{0,96},{33,65},{65,33},{97,1},{1,97},{34,66... | collective-permute-start | bytes 811016 | tf_op jit(solution)/shard_map/ppermute | solution.py:42
  27.1 12.4 %copy-start.5 = (f32[2,128,128]{2,1,0:T(8,128)S(1)}, f32[2,128,128]{2,1,0:T(8,128)}, u32[]{:S(2)}) copy-start(f32[2,128,128]{2,1,0:T(8,128)} %weights.1) | copy-start | bytes 393220
  27.7 13.7 %collective-permute-start.7 = (f32[544,128]{1,0:T(8,128)S(1)}, f32[544,128]{1,0:T(8,128)S(1)}, u32[]{:S(2)}, u32[]{:S(2)}) collective-permute-start(f32[544,128]{1,0:T(8,128)S(1)} %get-tuple-element.83.rest_4_), channel_id=1, source_target_pairs={{0,8},{8,0},{16,24},{24,16},{1,9},{9,1},{17,25},{25,17},{2,10},{10... | collective-permute-start | bytes 835592 | tf_op jit(solution)/shard_map/ppermute | solution.py:42
  28.1 13.3 %collective-permute-start.8 = (f32[544,128]{1,0:T(8,128)S(1)}, f32[544,128]{1,0:T(8,128)S(1)}, u32[]{:S(2)}, u32[]{:S(2)}) collective-permute-start(f32[544,128]{1,0:T(8,128)S(1)} %get-tuple-element.84.rest_5_), channel_id=1, source_target_pairs={{8,16},{16,8},{24,0},{0,24},{9,17},{17,9},{25,1},{1,25},{10,18},{1... | collective-permute-start | bytes 835592 | tf_op jit(solution)/shard_map/ppermute | solution.py:42
  28.8 12.6 %collective-permute-start.11 = (f32[512,128]{1,0:T(8,128)S(1)}, f32[512,128]{1,0:T(8,128)S(1)}, u32[]{:S(2)}, u32[]{:S(2)}) collective-permute-start(f32[512,128]{1,0:T(8,128)S(1)} %get-tuple-element.87), channel_id=1, source_target_pairs={{0,32},{32,0},{64,96},{96,64},{1,33},{33,1},{65,97},{97,65},{2,34}... | collective-permute-start | bytes 786440 | tf_op jit(solution)/shard_map/ppermute | solution.py:42
  28.9 7.0 %collective-permute-start.9 = (f32[272,128]{1,0:T(8,128)S(1)}, f32[272,128]{1,0:T(8,128)S(1)}, u32[]{:S(2)}, u32[]{:S(2)}) collective-permute-start(f32[272,128]{1,0:T(8,128)S(1)} %get-tuple-element.85.rest_6_), channel_id=1, source_target_pairs={{1,2},{2,1},{3,4},{4,3},{5,6},{6,5},{7,0},{0,7},{9,10},{10,9},{11,... | collective-permute-start | bytes 417800 | tf_op jit(solution)/shard_map/ppermute | solution.py:42
  32.0 9.4 %collective-permute-start.10 = (f32[272,128]{1,0:T(8,128)S(1)}, f32[272,128]{1,0:T(8,128)S(1)}, u32[]{:S(2)}, u32[]{:S(2)}) collective-permute-start(f32[272,128]{1,0:T(8,128)S(1)} %get-tuple-element.86.rest_7_), channel_id=1, source_target_pairs={{0,1},{1,0},{2,3},{3,2},{4,5},{5,4},{6,7},{7,6},{8,9},{9,8},{10,11... | collective-permute-start | bytes 417800 | tf_op jit(solution)/shard_map/ppermute | solution.py:42
  35.9 10.5 %collective-permute-start.12 = (f32[512,128]{1,0:T(8,128)S(1)}, f32[512,128]{1,0:T(8,128)S(1)}, u32[]{:S(2)}, u32[]{:S(2)}) collective-permute-start(f32[512,128]{1,0:T(8,128)S(1)} %get-tuple-element.89), channel_id=1, source_target_pairs={{32,64},{64,32},{96,0},{0,96},{33,65},{65,33},{97,1},{1,97},{34,66... | collective-permute-start | bytes 786440 | tf_op jit(solution)/shard_map/ppermute | solution.py:42
  42.1 9.7 %collective-permute-start.13 = (f32[576,128]{1,0:T(8,128)S(1)}, f32[576,128]{1,0:T(8,128)S(1)}, u32[]{:S(2)}, u32[]{:S(2)}) collective-permute-start(f32[576,128]{1,0:T(8,128)S(1)} %get-tuple-element.94.rest_8_), channel_id=1, source_target_pairs={{0,8},{8,0},{16,24},{24,16},{1,9},{9,1},{17,25},{25,17},{2,10},{10... | collective-permute-start | bytes 884744 | tf_op jit(solution)/shard_map/ppermute | solution.py:42
  43.0 10.0 %collective-permute-start.14 = (f32[576,128]{1,0:T(8,128)S(1)}, f32[576,128]{1,0:T(8,128)S(1)}, u32[]{:S(2)}, u32[]{:S(2)}) collective-permute-start(f32[576,128]{1,0:T(8,128)S(1)} %get-tuple-element.95.rest_9_), channel_id=1, source_target_pairs={{8,16},{16,8},{24,0},{0,24},{9,17},{17,9},{25,1},{1,25},{10,18},{1... | collective-permute-start | bytes 884744 | tf_op jit(solution)/shard_map/ppermute | solution.py:42
  44.8 7.0 %collective-permute-start.17 = (f32[512,128]{1,0:T(8,128)S(1)}, f32[512,128]{1,0:T(8,128)S(1)}, u32[]{:S(2)}, u32[]{:S(2)}) collective-permute-start(f32[512,128]{1,0:T(8,128)S(1)} %get-tuple-element.98), channel_id=1, source_target_pairs={{0,32},{32,0},{64,96},{96,64},{1,33},{33,1},{65,97},{97,65},{2,34}... | collective-permute-start | bytes 786440 | tf_op jit(solution)/shard_map/ppermute | solution.py:42
  44.8 7.0 %collective-permute-start.15 = (f32[288,128]{1,0:T(8,128)S(1)}, f32[288,128]{1,0:T(8,128)S(1)}, u32[]{:S(2)}, u32[]{:S(2)}) collective-permute-start(f32[288,128]{1,0:T(8,128)S(1)} %get-tuple-element.96.rest_10_), channel_id=1, source_target_pairs={{1,2},{2,1},{3,4},{4,3},{5,6},{6,5},{7,0},{0,7},{9,10},{10,9},{11,... | collective-permute-start | bytes 442376 | tf_op jit(solution)/shard_map/ppermute | solution.py:42
  46.4 5.4 %collective-permute-start.16 = (f32[288,128]{1,0:T(8,128)S(1)}, f32[288,128]{1,0:T(8,128)S(1)}, u32[]{:S(2)}, u32[]{:S(2)}) collective-permute-start(f32[288,128]{1,0:T(8,128)S(1)} %get-tuple-element.97.rest_11_), channel_id=1, source_target_pairs={{0,1},{1,0},{2,3},{3,2},{4,5},{5,4},{6,7},{7,6},{8,9},{9,8},{10,11... | collective-permute-start | bytes 442376 | tf_op jit(solution)/shard_map/ppermute | solution.py:42
  46.6 1.7 %copy-start.4 = (f32[2,4,128]{2,1,0:T(4,128)S(1)}, f32[2,4,128]{2,1,0:T(4,128)}, u32[]{:S(2)}) copy-start(f32[2,4,128]{2,1,0:T(4,128)} %thetas.11) | copy-start | bytes 12292
  54.9 6.8 %collective-permute-start.21 = (f32[256,128]{1,0:T(8,128)S(1)}, f32[256,128]{1,0:T(8,128)S(1)}, u32[]{:S(2)}, u32[]{:S(2)}) collective-permute-start(f32[256,128]{1,0:T(8,128)S(1)} %get-tuple-element.109.rest_2_.rest_7_), channel_id=1, source_target_pairs={{1,2},{2,1},{3,4},{4,3},{5,6},{6,5},{7,0},{0,7},{9,10},{10,9},{11,... | collective-permute-start | bytes 393224 | tf_op jit(solution)/shard_map/ppermute | solution.py:42
  55.9 14.2 %collective-permute-start.23 = (f32[512,128]{1,0:T(8,128)S(1)}, f32[512,128]{1,0:T(8,128)S(1)}, u32[]{:S(2)}, u32[]{:S(2)}) collective-permute-start(f32[512,128]{1,0:T(8,128)S(1)} %get-tuple-element.111.rest_4_), channel_id=1, source_target_pairs={{0,32},{32,0},{64,96},{96,64},{1,33},{33,1},{65,97},{97,65},{2,34}... | collective-permute-start | bytes 786440 | tf_op jit(solution)/shard_map/ppermute | solution.py:42
  57.1 13.0 %collective-permute-start.19 = (f32[512,128]{1,0:T(8,128)S(1)}, f32[512,128]{1,0:T(8,128)S(1)}, u32[]{:S(2)}, u32[]{:S(2)}) collective-permute-start(f32[512,128]{1,0:T(8,128)S(1)} %get-tuple-element.107.rest_0_.rest_5_), channel_id=1, source_target_pairs={{0,8},{8,0},{16,24},{24,16},{1,9},{9,1},{17,25},{25,17},{2,10},{10... | collective-permute-start | bytes 786440 | tf_op jit(solution)/shard_map/ppermute | solution.py:42
  57.4 12.7 %collective-permute-start.20 = (f32[512,128]{1,0:T(8,128)S(1)}, f32[512,128]{1,0:T(8,128)S(1)}, u32[]{:S(2)}, u32[]{:S(2)}) collective-permute-start(f32[512,128]{1,0:T(8,128)S(1)} %get-tuple-element.108.rest_1_.rest_6_), channel_id=1, source_target_pairs={{8,16},{16,8},{24,0},{0,24},{9,17},{17,9},{25,1},{1,25},{10,18},{1... | collective-permute-start | bytes 786440 | tf_op jit(solution)/shard_map/ppermute | solution.py:42
  58.0 12.1 %collective-permute-start.18 = (f32[512,128]{1,0:T(8,128)S(1)}, f32[512,128]{1,0:T(8,128)S(1)}, u32[]{:S(2)}, u32[]{:S(2)}) collective-permute-start(f32[512,128]{1,0:T(8,128)S(1)} %get-tuple-element.99.d1), channel_id=1, source_target_pairs={{32,64},{64,32},{96,0},{0,96},{33,65},{65,33},{97,1},{1,97},{34,66... | collective-permute-start | bytes 786440 | tf_op jit(solution)/shard_map/ppermute | solution.py:42
  61.8 4.1 %collective-permute-start.22 = (f32[256,128]{1,0:T(8,128)S(1)}, f32[256,128]{1,0:T(8,128)S(1)}, u32[]{:S(2)}, u32[]{:S(2)}) collective-permute-start(f32[256,128]{1,0:T(8,128)S(1)} %get-tuple-element.110.rest_3_.rest_8_), channel_id=1, source_target_pairs={{0,1},{1,0},{2,3},{3,2},{4,5},{5,4},{6,7},{7,6},{8,9},{9,8},{10,11... | collective-permute-start | bytes 393224 | tf_op jit(solution)/shard_map/ppermute | solution.py:42
  65.9 9.0 %collective-permute-start.24 = (f32[512,128]{1,0:T(8,128)S(1)}, f32[512,128]{1,0:T(8,128)S(1)}, u32[]{:S(2)}, u32[]{:S(2)}) collective-permute-start(f32[512,128]{1,0:T(8,128)S(1)} %get-tuple-element.114), channel_id=1, source_target_pairs={{32,64},{64,32},{96,0},{0,96},{33,65},{65,33},{97,1},{1,97},{34,66... | collective-permute-start | bytes 786440 | tf_op jit(solution)/shard_map/ppermute | solution.py:42
  70.8 14.0 %collective-permute-start.25 = (f32[544,128]{1,0:T(8,128)S(1)}, f32[544,128]{1,0:T(8,128)S(1)}, u32[]{:S(2)}, u32[]{:S(2)}) collective-permute-start(f32[544,128]{1,0:T(8,128)S(1)} %get-tuple-element.117.rest_9_), channel_id=1, source_target_pairs={{0,8},{8,0},{16,24},{24,16},{1,9},{9,1},{17,25},{25,17},{2,10},{10... | collective-permute-start | bytes 835592 | tf_op jit(solution)/shard_map/ppermute | solution.py:42
  71.2 13.6 %collective-permute-start.26 = (f32[544,128]{1,0:T(8,128)S(1)}, f32[544,128]{1,0:T(8,128)S(1)}, u32[]{:S(2)}, u32[]{:S(2)}) collective-permute-start(f32[544,128]{1,0:T(8,128)S(1)} %get-tuple-element.118.rest_10_), channel_id=1, source_target_pairs={{8,16},{16,8},{24,0},{0,24},{9,17},{17,9},{25,1},{1,25},{10,18},{1... | collective-permute-start | bytes 835592 | tf_op jit(solution)/shard_map/ppermute | solution.py:42
  73.0 11.7 %collective-permute-start.29 = (f32[512,128]{1,0:T(8,128)S(1)}, f32[512,128]{1,0:T(8,128)S(1)}, u32[]{:S(2)}, u32[]{:S(2)}) collective-permute-start(f32[512,128]{1,0:T(8,128)S(1)} %get-tuple-element.121), channel_id=1, source_target_pairs={{0,32},{32,0},{64,96},{96,64},{1,33},{33,1},{65,97},{97,65},{2,34}... | collective-permute-start | bytes 786440 | tf_op jit(solution)/shard_map/ppermute | solution.py:42
  73.0 6.8 %collective-permute-start.27 = (f32[272,128]{1,0:T(8,128)S(1)}, f32[272,128]{1,0:T(8,128)S(1)}, u32[]{:S(2)}, u32[]{:S(2)}) collective-permute-start(f32[272,128]{1,0:T(8,128)S(1)} %get-tuple-element.119.rest_11_), channel_id=1, source_target_pairs={{1,2},{2,1},{3,4},{4,3},{5,6},{6,5},{7,0},{0,7},{9,10},{10,9},{11,... | collective-permute-start | bytes 417800 | tf_op jit(solution)/shard_map/ppermute | solution.py:42
  74.9 9.9 %collective-permute-start.28 = (f32[272,128]{1,0:T(8,128)S(1)}, f32[272,128]{1,0:T(8,128)S(1)}, u32[]{:S(2)}, u32[]{:S(2)}) collective-permute-start(f32[272,128]{1,0:T(8,128)S(1)} %get-tuple-element.120.rest_12_), channel_id=1, source_target_pairs={{0,1},{1,0},{2,3},{3,2},{4,5},{5,4},{6,7},{7,6},{8,9},{9,8},{10,11... | collective-permute-start | bytes 417800 | tf_op jit(solution)/shard_map/ppermute | solution.py:42
  79.9 9.7 %collective-permute-start.30 = (f32[512,128]{1,0:T(8,128)S(1)}, f32[512,128]{1,0:T(8,128)S(1)}, u32[]{:S(2)}, u32[]{:S(2)}) collective-permute-start(f32[512,128]{1,0:T(8,128)S(1)} %get-tuple-element.123), channel_id=1, source_target_pairs={{32,64},{64,32},{96,0},{0,96},{33,65},{65,33},{97,1},{1,97},{34,66... | collective-permute-start | bytes 786440 | tf_op jit(solution)/shard_map/ppermute | solution.py:42
  85.5 8.7 %collective-permute-start.31 = (f32[576,128]{1,0:T(8,128)S(1)}, f32[576,128]{1,0:T(8,128)S(1)}, u32[]{:S(2)}, u32[]{:S(2)}) collective-permute-start(f32[576,128]{1,0:T(8,128)S(1)} %get-tuple-element.127.rest_13_), channel_id=1, source_target_pairs={{0,8},{8,0},{16,24},{24,16},{1,9},{9,1},{17,25},{25,17},{2,10},{10... | collective-permute-start | bytes 884744 | tf_op jit(solution)/shard_map/ppermute | solution.py:42
  86.3 10.0 %collective-permute-start.32 = (f32[576,128]{1,0:T(8,128)S(1)}, f32[576,128]{1,0:T(8,128)S(1)}, u32[]{:S(2)}, u32[]{:S(2)}) collective-permute-start(f32[576,128]{1,0:T(8,128)S(1)} %get-tuple-element.128.rest_14_), channel_id=1, source_target_pairs={{8,16},{16,8},{24,0},{0,24},{9,17},{17,9},{25,1},{1,25},{10,18},{1... | collective-permute-start | bytes 884744 | tf_op jit(solution)/shard_map/ppermute | solution.py:42
  87.2 7.0 %collective-permute-start.35 = (f32[512,128]{1,0:T(8,128)S(1)}, f32[512,128]{1,0:T(8,128)S(1)}, u32[]{:S(2)}, u32[]{:S(2)}) collective-permute-start(f32[512,128]{1,0:T(8,128)S(1)} %get-tuple-element.131), channel_id=1, source_target_pairs={{0,32},{32,0},{64,96},{96,64},{1,33},{33,1},{65,97},{97,65},{2,34}... | collective-permute-start | bytes 786440 | tf_op jit(solution)/shard_map/ppermute | solution.py:42
  87.2 7.0 %collective-permute-start.33 = (f32[288,128]{1,0:T(8,128)S(1)}, f32[288,128]{1,0:T(8,128)S(1)}, u32[]{:S(2)}, u32[]{:S(2)}) collective-permute-start(f32[288,128]{1,0:T(8,128)S(1)} %get-tuple-element.129.rest_15_), channel_id=1, source_target_pairs={{1,2},{2,1},{3,4},{4,3},{5,6},{6,5},{7,0},{0,7},{9,10},{10,9},{11,... | collective-permute-start | bytes 442376 | tf_op jit(solution)/shard_map/ppermute | solution.py:42
  89.6 4.6 %collective-permute-start.34 = (f32[288,128]{1,0:T(8,128)S(1)}, f32[288,128]{1,0:T(8,128)S(1)}, u32[]{:S(2)}, u32[]{:S(2)}) collective-permute-start(f32[288,128]{1,0:T(8,128)S(1)} %get-tuple-element.130.rest_16_), channel_id=1, source_target_pairs={{0,1},{1,0},{2,3},{3,2},{4,5},{5,4},{6,7},{7,6},{8,9},{9,8},{10,11... | collective-permute-start | bytes 442376 | tf_op jit(solution)/shard_map/ppermute | solution.py:42

commit v5 on v4

--- a/solution.py
+++ b/solution.py
@@ -16,7 +16,7 @@
 LINE = {"gy": NZ, "gz": NY}
 CROSS = ("gx", 1)
 LOCALS = (("gy", 0), ("gy", 1), ("gz", 1), ("gz", 0), ("gx", 0))
-EARLY = (1, 9)
+EARLY = ((1, 7), (1, 9))
 SCALES = 16
 
 F32 = jnp.float32
@@ -380,7 +380,7 @@
 
 
 def inner_mix_kernel(layer, scaled, w0, w1, w2, w3, a2, thetas, w4, out):
-    mix_range(layer, scaled, (w0, w1, w2, w3), a2, thetas, w4, out, EARLY)
+    mix_range(layer, scaled, (w0, w1, w2, w3), a2, thetas, w4, out, EARLY[layer])
 
 
 def put_faces(out, faces, planes):
@@ -395,12 +395,12 @@
 
 def merge_kernel(layer, inner, d1, w0, w1, w2, w3, a2, thetas, w4, *rest):
     sends, out, d2, d3 = rest[:5], *rest[5:]
-    put_faces(out, sends[:-1], EARLY)
+    put_faces(out, sends[:-1], EARLY[layer])
     for key, face in ((CROSS, d1), (LOCALS[-1], sends[-1])):
         base = side(*key) * ((NX - 1) * PLANE)
         for i in range(PLANE // 128):
             out[pl.ds(pl.multiple_of(base + i * 128, 128), 128), :] = face[pl.ds(i * 128, 128), :]
-    mix_range(layer, True, (w0, w1, w2, w3), a2, thetas, w4, out, (EARLY[1], NX - 1))
+    mix_range(layer, True, (w0, w1, w2, w3), a2, thetas, w4, out, (EARLY[layer][1], NX - 1))
     copy_plane(out, cross_base(2), d2)
     copy_plane(out, cross_base(3), d3)
 
@@ -415,12 +415,13 @@
         return pltpu.make_async_copy(hidden.at[rows, :], out.at[rows, :], sems.at[i])
 
     f = [(*known[i:12:4], faces[i], known[12 + i]) for i in range(4)]
-    mix_faces(layer, f, thetas, w4, done, False, EARLY)
-    put_faces(hidden, done, EARLY)
-    for i in range(*EARLY):
+    early = EARLY[layer]
+    mix_faces(layer, f, thetas, w4, done, False, early)
+    put_faces(hidden, done, early)
+    for i in range(*early):
         copy(i).start()
     ws = (w0, w1, w2, w3)
-    for planes in ((0, EARLY[0]), (EARLY[1], NX)):
+    for planes in ((0, early[0]), (early[1], NX)):
         mix_range(layer, False, ws, a2, thetas, w4, hidden, planes, lambda x: copy(x).start())
     for i in range(NX):
         copy(i).wait()

time: 100 us -> 100 us (level)
  no operation moved by 1% of the time
where the time goes in v5:
time: 100 us; the launch traced here: 99.8 us
  starting transfers between devices  43.6 us (44%)
  Pallas kernels  26.5 us (26%)
  waiting for transfers between devices  26.1 us (26%)
  local copies, waits for them, and re-layouts  3.11 us (3%)
    ppermute x36, starting transfers between devices, swap(): return lax.ppermute(x, axis, pairs)  43.6 us
    pallas_call x21, Pallas kernels, call(): pl.pallas_call(kernel, out_shape=out_shape, in_specs=[HBM if i in in_hbm...  26.5 us
    ppermute x36, waiting for transfers between devices, swap(): return lax.ppermute(x, axis, pairs)  26.1 us
    unnamed x12, local copies, waits for them, and re-layouts  3.11 us
  transfers between devices with their start and end apart: 36, of which 12 were waited for; matrix products, arithmetic and copies ran while one was open for 0% of the time, Pallas kernels for 21%

profile of v5, /device:TPU:1, one launch (start us, length us, event | category | flops | bytes accessed | tf_op | source)
XLA Modules:
  0.0 99.8 jit_solution(1125023748613567212)
XLA Ops:
  0.0 2.2 %copy-done = f32[16,16,32,128]{3,2,1,0:T(8,128)S(1)} copy-done((f32[16,16,32,128]{3,2,1,0:T(8,128)S(1)}, f32[16,16,32,128]{3,2,1,0:T(8,128)}, u32[]{:S(2)}) %copy-start) | copy-done | bytes 4194328
  2.2 0.9 copy-done.2
  3.8 5.7 %collective-permute-start.3 = (f32[256,128]{1,0:T(8,128)S(1)}, f32[256,128]{1,0:T(8,128)S(1)}, u32[]{:S(2)}, u32[]{:S(2)}) collective-permute-start(f32[256,128]{1,0:T(8,128)S(1)} %get-tuple-element.75.rest_2_), channel_id=1, source_target_pairs={{1,2},{2,1},{3,4},{4,3},{5,6},{6,5},{7,0},{0,7},{9,10},{10,9},{11,... | collective-permute-start | bytes 393224 | tf_op jit(solution)/shard_map/ppermute | solution.py:42
  9.4 1.2 %shard_map.48 = f32[528,128]{1,0:T(8,128)S(1)} custom-call(f32[8192,128]{1,0:T(8,128)} %bitcast.2, f32[16,16,32]{2,1,0:T(8,128)} %sv.3), custom_call_target="tpu_custom_call" | custom-call | tf_op jit(solution)/shard_map/pallas_call | solution.py:431
  10.7 3.5 %collective-permute-start = (f32[528,128]{1,0:T(8,128)S(1)}, f32[528,128]{1,0:T(8,128)S(1)}, u32[]{:S(2)}, u32[]{:S(2)}) collective-permute-start(f32[528,128]{1,0:T(8,128)S(1)} %shard_map.48), channel_id=1, source_target_pairs={{32,64},{64,32},{96,0},{0,96},{33,65},{65,33},{97,1},{1,97},{34,66... | collective-permute-start | bytes 811016 | tf_op jit(solution)/shard_map/ppermute | solution.py:42
  14.2 1.2 %collective-permute-start.1 = (f32[512,128]{1,0:T(8,128)S(1)}, f32[512,128]{1,0:T(8,128)S(1)}, u32[]{:S(2)}, u32[]{:S(2)}) collective-permute-start(f32[512,128]{1,0:T(8,128)S(1)} %get-tuple-element.73.rest_0_), channel_id=1, source_target_pairs={{0,8},{8,0},{16,24},{24,16},{1,9},{9,1},{17,25},{25,17},{2,10},{10... | collective-permute-start | bytes 786440 | tf_op jit(solution)/shard_map/ppermute | solution.py:42
  15.4 1.8 %collective-permute-start.2 = (f32[512,128]{1,0:T(8,128)S(1)}, f32[512,128]{1,0:T(8,128)S(1)}, u32[]{:S(2)}, u32[]{:S(2)}) collective-permute-start(f32[512,128]{1,0:T(8,128)S(1)} %get-tuple-element.74.rest_1_), channel_id=1, source_target_pairs={{8,16},{16,8},{24,0},{0,24},{9,17},{17,9},{25,1},{1,25},{10,18},{1... | collective-permute-start | bytes 786440 | tf_op jit(solution)/shard_map/ppermute | solution.py:42
  17.3 4.1 %collective-permute-done.4.rest_3_ = f32[256,128]{1,0:T(8,128)S(1)} collective-permute-done((f32[256,128]{1,0:T(8,128)S(1)}, f32[256,128]{1,0:T(8,128)S(1)}, u32[]{:S(2)}, u32[]{:S(2)}) %collective-permute-start.4) | collective-permute-done | bytes 131104 | tf_op jit(solution)/shard_map/ppermute | solution.py:42
  21.4 2.2 %collective-permute-start.6 = (f32[528,128]{1,0:T(8,128)S(1)}, f32[528,128]{1,0:T(8,128)S(1)}, u32[]{:S(2)}, u32[]{:S(2)}) collective-permute-start(f32[528,128]{1,0:T(8,128)S(1)} %get-tuple-element.79), channel_id=1, source_target_pairs={{32,64},{64,32},{96,0},{0,96},{33,65},{65,33},{97,1},{1,97},{34,66... | collective-permute-start | bytes 811016 | tf_op jit(solution)/shard_map/ppermute | solution.py:42
  23.5 2.0 %shard_map.46 = (f32[8192,128]{1,0:T(8,128)S(1)}, f32[8192,128]{1,0:T(8,128)S(1)}, f32[256,128]{1,0:T(8,128)S(1)}, f32[256,128]{1,0:T(8,128)S(1)}) custom-call(f32[16,16,32]{2,1,0:T(8,128)S(1)} %copy-done.3, f32[8192,128]{1,0:T(8,128)S(1)} %bitcast.4), custom_call_target="tpu_custom_call" | custom-call | tf_op jit(solution)/shard_map/pallas_call | solution.py:431
  25.5 1.5 %shard_map.47.w_in = f32[8192,128]{1,0:T(8,128)S(1)} custom-call(f32[8192,128]{1,0:T(8,128)S(1)} %get-tuple-element.69.w0, f32[8192,128]{1,0:T(8,128)S(1)} %get-tuple-element.70.a2), custom_call_target="tpu_custom_call" | custom-call | tf_op jit(solution)/shard_map/pallas_call | solution.py:431
  28.9 3.0 %collective-permute-start.9 = (f32[272,128]{1,0:T(8,128)S(1)}, f32[272,128]{1,0:T(8,128)S(1)}, u32[]{:S(2)}, u32[]{:S(2)}) collective-permute-start(f32[272,128]{1,0:T(8,128)S(1)} %get-tuple-element.85.rest_6_), channel_id=1, source_target_pairs={{1,2},{2,1},{3,4},{4,3},{5,6},{6,5},{7,0},{0,7},{9,10},{10,9},{11,... | collective-permute-start | bytes 417800 | tf_op jit(solution)/shard_map/ppermute | solution.py:42
  32.0 4.0 %collective-permute-done.9.rest_2_ = f32[272,128]{1,0:T(8,128)S(1)} collective-permute-done((f32[272,128]{1,0:T(8,128)S(1)}, f32[272,128]{1,0:T(8,128)S(1)}, u32[]{:S(2)}, u32[]{:S(2)}) %collective-permute-start.9) | collective-permute-done | bytes 139296 | tf_op jit(solution)/shard_map/ppermute | solution.py:42
  35.9 3.5 %collective-permute-start.12 = (f32[512,128]{1,0:T(8,128)S(1)}, f32[512,128]{1,0:T(8,128)S(1)}, u32[]{:S(2)}, u32[]{:S(2)}) collective-permute-start(f32[512,128]{1,0:T(8,128)S(1)} %get-tuple-element.89), channel_id=1, source_target_pairs={{32,64},{64,32},{96,0},{0,96},{33,65},{65,33},{97,1},{1,97},{34,66... | collective-permute-start | bytes 786440 | tf_op jit(solution)/shard_map/ppermute | solution.py:42
  39.7 1.6 %shard_map.52 = (f32[8192,128]{1,0:T(8,128)S(1)}, f32[512,128]{1,0:T(8,128)S(1)}) custom-call(f32[8192,128]{1,0:T(8,128)S(1)} %get-tuple-element.78.w1, f32[8192,128]{1,0:T(8,128)S(1)} %get-tuple-element.70.a2, f32[8192,128]{1,0:T(8,128)S(1)} %get-tuple-element.69.w0, f32[528,128]{1,0:T(8,128)S(1)} %collective-permute-done.d1.d, ...), custom_call_target="tpu_custom_call" | custom-call | tf_op jit(solution)/shard_map/pallas_call | solution.py:431
  41.4 0.7 shard_map.53
  42.1 0.8 collective-permute-start.13
  43.0 1.8 %collective-permute-start.14 = (f32[576,128]{1,0:T(8,128)S(1)}, f32[576,128]{1,0:T(8,128)S(1)}, u32[]{:S(2)}, u32[]{:S(2)}) collective-permute-start(f32[576,128]{1,0:T(8,128)S(1)} %get-tuple-element.95.rest_9_), channel_id=1, source_target_pairs={{8,16},{16,8},{24,0},{0,24},{9,17},{17,9},{25,1},{1,25},{10,18},{1... | collective-permute-start | bytes 884744 | tf_op jit(solution)/shard_map/ppermute | solution.py:42
  44.8 1.6 %collective-permute-done.12.d3 = f32[512,128]{1,0:T(8,128)S(1)} collective-permute-done((f32[512,128]{1,0:T(8,128)S(1)}, f32[512,128]{1,0:T(8,128)S(1)}, u32[]{:S(2)}, u32[]{:S(2)}) %collective-permute-start.12) | collective-permute-done | bytes 262176 | tf_op jit(solution)/shard_map/ppermute | solution.py:42
  46.7 1.7 %shard_map.55 = (f32[8192,128]{1,0:T(8,128)S(1)}, f32[512,128]{1,0:T(8,128)S(1)}) custom-call(f32[8192,128]{1,0:T(8,128)S(1)} %get-tuple-element.88.w2, f32[8192,128]{1,0:T(8,128)S(1)} %get-tuple-element.70.a2, f32[8192,128]{1,0:T(8,128)S(1)} %get-tuple-element.78.w1, f32[528,128]{1,0:T(8,128)S(1)} %collective-permute-done.d1.d, ...), custom_call_target="tpu_custom_call" | custom-call | tf_op jit(solution)/shard_map/pallas_call | solution.py:431
  48.4 1.2 %shard_map.56.inner = f32[8192,128]{1,0:T(8,128)S(1)} custom-call(f32[8192,128]{1,0:T(8,128)S(1)} %get-tuple-element.69.w0, f32[8192,128]{1,0:T(8,128)S(1)} %get-tuple-element.78.w1, f32[8192,128]{1,0:T(8,128)S(1)} %get-tuple-element.88.w2, f32[8192,128]{1,0:T(8,128)S(1)} %get-tuple-element.91.w3.w3_in, f32[8192,128]{1,0:T(8,128)S(1)} %get-tuple-element.70.a2, ...), custom_call_target="tpu_custom_call" | custom-call | tf_op jit(solution)/shard_map/pallas_call | solution.py:431
  49.7 2.2 %collective-permute-done.15.rest_2_ = f32[288,128]{1,0:T(8,128)S(1)} collective-permute-done((f32[288,128]{1,0:T(8,128)S(1)}, f32[288,128]{1,0:T(8,128)S(1)}, u32[]{:S(2)}, u32[]{:S(2)}) %collective-permute-start.15) | collective-permute-done | bytes 147488 | tf_op jit(solution)/shard_map/ppermute | solution.py:42
  51.8 1.2 %collective-permute-done.14.rest_1_ = f32[576,128]{1,0:T(8,128)S(1)} collective-permute-done((f32[576,128]{1,0:T(8,128)S(1)}, f32[576,128]{1,0:T(8,128)S(1)}, u32[]{:S(2)}, u32[]{:S(2)}) %collective-permute-start.14) | collective-permute-done | bytes 294944 | tf_op jit(solution)/shard_map/ppermute | solution.py:42
  53.0 1.0 %shard_map.57 = (f32[8192,128]{1,0:T(8,128)S(1)}, f32[512,128]{1,0:T(8,128)S(1)}, f32[512,128]{1,0:T(8,128)S(1)}, f32[512,128]{1,0:T(8,128)S(1)}, f32[256,128]{1,0:T(8,128)S(1)}, /*index=5*/f32[256,128]{1,0:T(8,128)S(1)}) custom-call(f32[8192,128]{1,0:T(8,128)S(1)} %get-tuple-element.91.w3.w3_in, ...), custom_call_target="tpu_custom_call", output_to_operand_aliasing={{0}: (0, {})} | custom-call | tf_op jit(solution)/shard_map/pallas_call | solution.py:431
  54.0 0.9 shard_map.58
  54.9 0.9 collective-permute-start.21
  55.9 1.2 %collective-permute-start.23 = (f32[512,128]{1,0:T(8,128)S(1)}, f32[512,128]{1,0:T(8,128)S(1)}, u32[]{:S(2)}, u32[]{:S(2)}) collective-permute-start(f32[512,128]{1,0:T(8,128)S(1)} %get-tuple-element.111.rest_4_), channel_id=1, source_target_pairs={{0,32},{32,0},{64,96},{96,64},{1,33},{33,1},{65,97},{97,65},{2,34}... | collective-permute-start | bytes 786440 | tf_op jit(solution)/shard_map/ppermute | solution.py:42
  58.0 3.0 %collective-permute-start.18 = (f32[512,128]{1,0:T(8,128)S(1)}, f32[512,128]{1,0:T(8,128)S(1)}, u32[]{:S(2)}, u32[]{:S(2)}) collective-permute-start(f32[512,128]{1,0:T(8,128)S(1)} %get-tuple-element.99.d1), channel_id=1, source_target_pairs={{32,64},{64,32},{96,0},{0,96},{33,65},{65,33},{97,1},{1,97},{34,66... | collective-permute-start | bytes 786440 | tf_op jit(solution)/shard_map/ppermute | solution.py:42
  61.1 0.7 collective-permute-done.21.rest_2_
  61.8 1.8 %shard_map.59 = (f32[8192,128]{1,0:T(8,128)S(1)}, f32[512,128]{1,0:T(8,128)S(1)}, f32[512,128]{1,0:T(8,128)S(1)}) custom-call(f32[8192,128]{1,0:T(8,128)S(1)} %shard_map.56.inner, f32[512,128]{1,0:T(8,128)S(1)} %get-tuple-element.99.d1, f32[8192,128]{1,0:T(8,128)S(1)} %get-tuple-element.69.w0, ...), custom_call_target="tpu_custom_call", output_to_operand_aliasing={{0}: (0, {})} | custom-call | tf_op jit(solution)/shard_map/pallas_call | solution.py:431
  63.6 2.3 %collective-permute-done.22.rest_3_ = f32[256,128]{1,0:T(8,128)S(1)} collective-permute-done((f32[256,128]{1,0:T(8,128)S(1)}, f32[256,128]{1,0:T(8,128)S(1)}, u32[]{:S(2)}, u32[]{:S(2)}) %collective-permute-start.22) | collective-permute-done | bytes 131104 | tf_op jit(solution)/shard_map/ppermute | solution.py:42
  65.9 2.7 %collective-permute-start.24 = (f32[512,128]{1,0:T(8,128)S(1)}, f32[512,128]{1,0:T(8,128)S(1)}, u32[]{:S(2)}, u32[]{:S(2)}) collective-permute-start(f32[512,128]{1,0:T(8,128)S(1)} %get-tuple-element.114), channel_id=1, source_target_pairs={{32,64},{64,32},{96,0},{0,96},{33,65},{65,33},{97,1},{1,97},{34,66... | collective-permute-start | bytes 786440 | tf_op jit(solution)/shard_map/ppermute | solution.py:42
  68.6 1.5 %shard_map.60.w_in = f32[8192,128]{1,0:T(8,128)S(1)} custom-call(f32[8192,128]{1,0:T(8,128)S(1)} %get-tuple-element.112.w0, f32[8192,128]{1,0:T(8,128)S(1)} %get-tuple-element.70.a2), custom_call_target="tpu_custom_call" | custom-call | tf_op jit(solution)/shard_map/pallas_call | solution.py:431
  71.2 1.8 %collective-permute-start.26 = (f32[544,128]{1,0:T(8,128)S(1)}, f32[544,128]{1,0:T(8,128)S(1)}, u32[]{:S(2)}, u32[]{:S(2)}) collective-permute-start(f32[544,128]{1,0:T(8,128)S(1)} %get-tuple-element.118.rest_10_), channel_id=1, source_target_pairs={{8,16},{16,8},{24,0},{0,24},{9,17},{17,9},{25,1},{1,25},{10,18},{1... | collective-permute-start | bytes 835592 | tf_op jit(solution)/shard_map/ppermute | solution.py:42
  73.0 1.5 %collective-permute-start.27 = (f32[272,128]{1,0:T(8,128)S(1)}, f32[272,128]{1,0:T(8,128)S(1)}, u32[]{:S(2)}, u32[]{:S(2)}) collective-permute-start(f32[272,128]{1,0:T(8,128)S(1)} %get-tuple-element.119.rest_11_), channel_id=1, source_target_pairs={{1,2},{2,1},{3,4},{4,3},{5,6},{6,5},{7,0},{0,7},{9,10},{10,9},{11,... | collective-permute-start | bytes 417800 | tf_op jit(solution)/shard_map/ppermute | solution.py:42
  75.1 4.7 %collective-permute-done.27.rest_2_ = f32[272,128]{1,0:T(8,128)S(1)} collective-permute-done((f32[272,128]{1,0:T(8,128)S(1)}, f32[272,128]{1,0:T(8,128)S(1)}, u32[]{:S(2)}, u32[]{:S(2)}) %collective-permute-start.27) | collective-permute-done | bytes 139296 | tf_op jit(solution)/shard_map/ppermute | solution.py:42
  79.9 3.2 %collective-permute-start.30 = (f32[512,128]{1,0:T(8,128)S(1)}, f32[512,128]{1,0:T(8,128)S(1)}, u32[]{:S(2)}, u32[]{:S(2)}) collective-permute-start(f32[512,128]{1,0:T(8,128)S(1)} %get-tuple-element.123), channel_id=1, source_target_pairs={{32,64},{64,32},{96,0},{0,96},{33,65},{65,33},{97,1},{1,97},{34,66... | collective-permute-start | bytes 786440 | tf_op jit(solution)/shard_map/ppermute | solution.py:42
  83.1 1.6 %shard_map.62 = (f32[8192,128]{1,0:T(8,128)S(1)}, f32[512,128]{1,0:T(8,128)S(1)}) custom-call(f32[8192,128]{1,0:T(8,128)S(1)} %get-tuple-element.113.w1, f32[8192,128]{1,0:T(8,128)S(1)} %get-tuple-element.70.a2, f32[8192,128]{1,0:T(8,128)S(1)} %get-tuple-element.112.w0, f32[512,128]{1,0:T(8,128)S(1)} %collective-permute-done.18.d1, ...), custom_call_target="tpu_custom_call" | custom-call | tf_op jit(solution)/shard_map/pallas_call | solution.py:431
  84.8 0.7 shard_map.63
  85.5 0.8 collective-permute-start.31
  86.3 0.9 collective-permute-start.32
  87.2 0.9 collective-permute-start.33
  88.1 1.5 %collective-permute-done.30.d3 = f32[512,128]{1,0:T(8,128)S(1)} collective-permute-done((f32[512,128]{1,0:T(8,128)S(1)}, f32[512,128]{1,0:T(8,128)S(1)}, u32[]{:S(2)}, u32[]{:S(2)}) %collective-permute-start.30) | collective-permute-done | bytes 262176 | tf_op jit(solution)/shard_map/ppermute | solution.py:42
  89.6 1.7 %shard_map.64 = (f32[8192,128]{1,0:T(8,128)S(1)}, f32[512,128]{1,0:T(8,128)S(1)}) custom-call(f32[8192,128]{1,0:T(8,128)S(1)} %get-tuple-element.122.w2, f32[8192,128]{1,0:T(8,128)S(1)} %get-tuple-element.70.a2, f32[8192,128]{1,0:T(8,128)S(1)} %get-tuple-element.113.w1, f32[512,128]{1,0:T(8,128)S(1)} %collective-permute-done.18.d1, ...), custom_call_target="tpu_custom_call" | custom-call | tf_op jit(solution)/shard_map/pallas_call | solution.py:431
  91.3 1.4 %shard_map.65.inner = f32[8192,128]{1,0:T(8,128)S(1)} custom-call(f32[8192,128]{1,0:T(8,128)S(1)} %get-tuple-element.112.w0, f32[8192,128]{1,0:T(8,128)S(1)} %get-tuple-element.113.w1, f32[8192,128]{1,0:T(8,128)S(1)} %get-tuple-element.122.w2, f32[8192,128]{1,0:T(8,128)S(1)} %get-tuple-element.125.w3.w3_in, f32[8192,128]{1,0:T(8,128)S(1)} %get-tuple-element.70.a2, ...), custom_call_target="tpu_custom_call" | custom-call | tf_op jit(solution)/shard_map/pallas_call | solution.py:431
  92.7 1.5 %collective-permute-done.33.rest_2_ = f32[288,128]{1,0:T(8,128)S(1)} collective-permute-done((f32[288,128]{1,0:T(8,128)S(1)}, f32[288,128]{1,0:T(8,128)S(1)}, u32[]{:S(2)}, u32[]{:S(2)}) %collective-permute-start.33) | collective-permute-done | bytes 147488 | tf_op jit(solution)/shard_map/ppermute | solution.py:42
  94.2 2.1 %collective-permute-done.32.rest_1_ = f32[576,128]{1,0:T(8,128)S(1)} collective-permute-done((f32[576,128]{1,0:T(8,128)S(1)}, f32[576,128]{1,0:T(8,128)S(1)}, u32[]{:S(2)}, u32[]{:S(2)}) %collective-permute-start.32) | collective-permute-done | bytes 294944 | tf_op jit(solution)/shard_map/ppermute | solution.py:42
  96.3 3.3 %shard_map.66 = (f32[8192,128]{1,0:T(8,128)S(1)}, f32[8192,128]{1,0:T(8,128)S(1)}, f32[8192,128]{1,0:T(8,128)}) custom-call(f32[8192,128]{1,0:T(8,128)S(1)} %get-tuple-element.125.w3.w3_in, f32[8192,128]{1,0:T(8,128)S(1)} %get-tuple-element.70.a2, ...), custom_call_target="tpu_custom_call", output_to_operand_aliasing={{0}: (0, {}), {1}: (12, {})} | custom-call | tf_op jit(solution)/shard_map/pallas_call | solution.py:431
  (57 shorter events, 5.7 us)
Async XLA Ops:
  0.0 2.2 %copy-start = (f32[16,16,32,128]{3,2,1,0:T(8,128)S(1)}, f32[16,16,32,128]{3,2,1,0:T(8,128)}, u32[]{:S(2)}) copy-start(f32[16,16,32,128]{3,2,1,0:T(8,128)} %param.4) | copy-start | bytes 12582916
  2.2 0.9 copy-start.2
  3.1 20.4 %copy-start.1 = (f32[16,16,32,128]{3,2,1,0:T(8,128)S(1)}, f32[16,16,32,128]{3,2,1,0:T(8,128)}, u32[]{:S(2)}) copy-start(f32[16,16,32,128]{3,2,1,0:T(8,128)} %param.4) | copy-start | bytes 12582916
  3.1 20.4 %copy-start.3 = (f32[16,16,32]{2,1,0:T(8,128)S(1)}, f32[16,16,32]{2,1,0:T(8,128)}, u32[]{:S(2)}) copy-start(f32[16,16,32]{2,1,0:T(8,128)} %sv.3) | copy-start | bytes 98308
  3.8 13.5 %collective-permute-start.3 = (f32[256,128]{1,0:T(8,128)S(1)}, f32[256,128]{1,0:T(8,128)S(1)}, u32[]{:S(2)}, u32[]{:S(2)}) collective-permute-start(f32[256,128]{1,0:T(8,128)S(1)} %get-tuple-element.75.rest_2_), channel_id=1, source_target_pairs={{1,2},{2,1},{3,4},{4,3},{5,6},{6,5},{7,0},{0,7},{9,10},{10,9},{11,... | collective-permute-start | bytes 393224 | tf_op jit(solution)/shard_map/ppermute | solution.py:42
  10.7 16.4 %collective-permute-start = (f32[528,128]{1,0:T(8,128)S(1)}, f32[528,128]{1,0:T(8,128)S(1)}, u32[]{:S(2)}, u32[]{:S(2)}) collective-permute-start(f32[528,128]{1,0:T(8,128)S(1)} %shard_map.48), channel_id=1, source_target_pairs={{32,64},{64,32},{96,0},{0,96},{33,65},{65,33},{97,1},{1,97},{34,66... | collective-permute-start | bytes 811016 | tf_op jit(solution)/shard_map/ppermute | solution.py:42
  14.2 12.8 %collective-permute-start.5 = (f32[512,128]{1,0:T(8,128)S(1)}, f32[512,128]{1,0:T(8,128)S(1)}, u32[]{:S(2)}, u32[]{:S(2)}) collective-permute-start(f32[512,128]{1,0:T(8,128)S(1)} %get-tuple-element.77), channel_id=1, source_target_pairs={{0,32},{32,0},{64,96},{96,64},{1,33},{33,1},{65,97},{97,65},{2,34}... | collective-permute-start | bytes 786440 | tf_op jit(solution)/shard_map/ppermute | solution.py:42
  14.2 12.8 %collective-permute-start.1 = (f32[512,128]{1,0:T(8,128)S(1)}, f32[512,128]{1,0:T(8,128)S(1)}, u32[]{:S(2)}, u32[]{:S(2)}) collective-permute-start(f32[512,128]{1,0:T(8,128)S(1)} %get-tuple-element.73.rest_0_), channel_id=1, source_target_pairs={{0,8},{8,0},{16,24},{24,16},{1,9},{9,1},{17,25},{25,17},{2,10},{10... | collective-permute-start | bytes 786440 | tf_op jit(solution)/shard_map/ppermute | solution.py:42
  15.4 11.6 %collective-permute-start.2 = (f32[512,128]{1,0:T(8,128)S(1)}, f32[512,128]{1,0:T(8,128)S(1)}, u32[]{:S(2)}, u32[]{:S(2)}) collective-permute-start(f32[512,128]{1,0:T(8,128)S(1)} %get-tuple-element.74.rest_1_), channel_id=1, source_target_pairs={{8,16},{16,8},{24,0},{0,24},{9,17},{17,9},{25,1},{1,25},{10,18},{1... | collective-permute-start | bytes 786440 | tf_op jit(solution)/shard_map/ppermute | solution.py:42
  17.3 4.1 %collective-permute-start.4 = (f32[256,128]{1,0:T(8,128)S(1)}, f32[256,128]{1,0:T(8,128)S(1)}, u32[]{:S(2)}, u32[]{:S(2)}) collective-permute-start(f32[256,128]{1,0:T(8,128)S(1)} %get-tuple-element.76.rest_3_), channel_id=1, source_target_pairs={{0,1},{1,0},{2,3},{3,2},{4,5},{5,4},{6,7},{7,6},{8,9},{9,8},{10,11... | collective-permute-start | bytes 393224 | tf_op jit(solution)/shard_map/ppermute | solution.py:42
  21.4 10.6 %collective-permute-start.6 = (f32[528,128]{1,0:T(8,128)S(1)}, f32[528,128]{1,0:T(8,128)S(1)}, u32[]{:S(2)}, u32[]{:S(2)}) collective-permute-start(f32[528,128]{1,0:T(8,128)S(1)} %get-tuple-element.79), channel_id=1, source_target_pairs={{32,64},{64,32},{96,0},{0,96},{33,65},{65,33},{97,1},{1,97},{34,66... | collective-permute-start | bytes 811016 | tf_op jit(solution)/shard_map/ppermute | solution.py:42
  27.1 12.4 %copy-start.5 = (f32[2,128,128]{2,1,0:T(8,128)S(1)}, f32[2,128,128]{2,1,0:T(8,128)}, u32[]{:S(2)}) copy-start(f32[2,128,128]{2,1,0:T(8,128)} %weights.1) | copy-start | bytes 393220
  27.7 13.7 %collective-permute-start.7 = (f32[544,128]{1,0:T(8,128)S(1)}, f32[544,128]{1,0:T(8,128)S(1)}, u32[]{:S(2)}, u32[]{:S(2)}) collective-permute-start(f32[544,128]{1,0:T(8,128)S(1)} %get-tuple-element.83.rest_4_), channel_id=1, source_target_pairs={{0,8},{8,0},{16,24},{24,16},{1,9},{9,1},{17,25},{25,17},{2,10},{10... | collective-permute-start | bytes 835592 | tf_op jit(solution)/shard_map/ppermute | solution.py:42
  28.1 13.3 %collective-permute-start.8 = (f32[544,128]{1,0:T(8,128)S(1)}, f32[544,128]{1,0:T(8,128)S(1)}, u32[]{:S(2)}, u32[]{:S(2)}) collective-permute-start(f32[544,128]{1,0:T(8,128)S(1)} %get-tuple-element.84.rest_5_), channel_id=1, source_target_pairs={{8,16},{16,8},{24,0},{0,24},{9,17},{17,9},{25,1},{1,25},{10,18},{1... | collective-permute-start | bytes 835592 | tf_op jit(solution)/shard_map/ppermute | solution.py:42
  28.8 12.6 %collective-permute-start.11 = (f32[512,128]{1,0:T(8,128)S(1)}, f32[512,128]{1,0:T(8,128)S(1)}, u32[]{:S(2)}, u32[]{:S(2)}) collective-permute-start(f32[512,128]{1,0:T(8,128)S(1)} %get-tuple-element.87), channel_id=1, source_target_pairs={{0,32},{32,0},{64,96},{96,64},{1,33},{33,1},{65,97},{97,65},{2,34}... | collective-permute-start | bytes 786440 | tf_op jit(solution)/shard_map/ppermute | solution.py:42
  28.9 7.0 %collective-permute-start.9 = (f32[272,128]{1,0:T(8,128)S(1)}, f32[272,128]{1,0:T(8,128)S(1)}, u32[]{:S(2)}, u32[]{:S(2)}) collective-permute-start(f32[272,128]{1,0:T(8,128)S(1)} %get-tuple-element.85.rest_6_), channel_id=1, source_target_pairs={{1,2},{2,1},{3,4},{4,3},{5,6},{6,5},{7,0},{0,7},{9,10},{10,9},{11,... | collective-permute-start | bytes 417800 | tf_op jit(solution)/shard_map/ppermute | solution.py:42
  32.0 9.4 %collective-permute-start.10 = (f32[272,128]{1,0:T(8,128)S(1)}, f32[272,128]{1,0:T(8,128)S(1)}, u32[]{:S(2)}, u32[]{:S(2)}) collective-permute-start(f32[272,128]{1,0:T(8,128)S(1)} %get-tuple-element.86.rest_7_), channel_id=1, source_target_pairs={{0,1},{1,0},{2,3},{3,2},{4,5},{5,4},{6,7},{7,6},{8,9},{9,8},{10,11... | collective-permute-start | bytes 417800 | tf_op jit(solution)/shard_map/ppermute | solution.py:42
  35.9 10.5 %collective-permute-start.12 = (f32[512,128]{1,0:T(8,128)S(1)}, f32[512,128]{1,0:T(8,128)S(1)}, u32[]{:S(2)}, u32[]{:S(2)}) collective-permute-start(f32[512,128]{1,0:T(8,128)S(1)} %get-tuple-element.89), channel_id=1, source_target_pairs={{32,64},{64,32},{96,0},{0,96},{33,65},{65,33},{97,1},{1,97},{34,66... | collective-permute-start | bytes 786440 | tf_op jit(solution)/shard_map/ppermute | solution.py:42
  42.1 9.7 %collective-permute-start.13 = (f32[576,128]{1,0:T(8,128)S(1)}, f32[576,128]{1,0:T(8,128)S(1)}, u32[]{:S(2)}, u32[]{:S(2)}) collective-permute-start(f32[576,128]{1,0:T(8,128)S(1)} %get-tuple-element.94.rest_8_), channel_id=1, source_target_pairs={{0,8},{8,0},{16,24},{24,16},{1,9},{9,1},{17,25},{25,17},{2,10},{10... | collective-permute-start | bytes 884744 | tf_op jit(solution)/shard_map/ppermute | solution.py:42
  43.0 10.0 %collective-permute-start.14 = (f32[576,128]{1,0:T(8,128)S(1)}, f32[576,128]{1,0:T(8,128)S(1)}, u32[]{:S(2)}, u32[]{:S(2)}) collective-permute-start(f32[576,128]{1,0:T(8,128)S(1)} %get-tuple-element.95.rest_9_), channel_id=1, source_target_pairs={{8,16},{16,8},{24,0},{0,24},{9,17},{17,9},{25,1},{1,25},{10,18},{1... | collective-permute-start | bytes 884744 | tf_op jit(solution)/shard_map/ppermute | solution.py:42
  44.8 7.0 %collective-permute-start.17 = (f32[512,128]{1,0:T(8,128)S(1)}, f32[512,128]{1,0:T(8,128)S(1)}, u32[]{:S(2)}, u32[]{:S(2)}) collective-permute-start(f32[512,128]{1,0:T(8,128)S(1)} %get-tuple-element.98), channel_id=1, source_target_pairs={{0,32},{32,0},{64,96},{96,64},{1,33},{33,1},{65,97},{97,65},{2,34}... | collective-permute-start | bytes 786440 | tf_op jit(solution)/shard_map/ppermute | solution.py:42
  44.8 7.0 %collective-permute-start.15 = (f32[288,128]{1,0:T(8,128)S(1)}, f32[288,128]{1,0:T(8,128)S(1)}, u32[]{:S(2)}, u32[]{:S(2)}) collective-permute-start(f32[288,128]{1,0:T(8,128)S(1)} %get-tuple-element.96.rest_10_), channel_id=1, source_target_pairs={{1,2},{2,1},{3,4},{4,3},{5,6},{6,5},{7,0},{0,7},{9,10},{10,9},{11,... | collective-permute-start | bytes 442376 | tf_op jit(solution)/shard_map/ppermute | solution.py:42
  46.4 5.4 %collective-permute-start.16 = (f32[288,128]{1,0:T(8,128)S(1)}, f32[288,128]{1,0:T(8,128)S(1)}, u32[]{:S(2)}, u32[]{:S(2)}) collective-permute-start(f32[288,128]{1,0:T(8,128)S(1)} %get-tuple-element.97.rest_11_), channel_id=1, source_target_pairs={{0,1},{1,0},{2,3},{3,2},{4,5},{5,4},{6,7},{7,6},{8,9},{9,8},{10,11... | collective-permute-start | bytes 442376 | tf_op jit(solution)/shard_map/ppermute | solution.py:42
  46.6 1.7 %copy-start.4 = (f32[2,4,128]{2,1,0:T(4,128)S(1)}, f32[2,4,128]{2,1,0:T(4,128)}, u32[]{:S(2)}) copy-start(f32[2,4,128]{2,1,0:T(4,128)} %thetas.11) | copy-start | bytes 12292
  54.9 6.8 %collective-permute-start.21 = (f32[256,128]{1,0:T(8,128)S(1)}, f32[256,128]{1,0:T(8,128)S(1)}, u32[]{:S(2)}, u32[]{:S(2)}) collective-permute-start(f32[256,128]{1,0:T(8,128)S(1)} %get-tuple-element.109.rest_2_.rest_7_), channel_id=1, source_target_pairs={{1,2},{2,1},{3,4},{4,3},{5,6},{6,5},{7,0},{0,7},{9,10},{10,9},{11,... | collective-permute-start | bytes 393224 | tf_op jit(solution)/shard_map/ppermute | solution.py:42
  55.9 14.2 %collective-permute-start.23 = (f32[512,128]{1,0:T(8,128)S(1)}, f32[512,128]{1,0:T(8,128)S(1)}, u32[]{:S(2)}, u32[]{:S(2)}) collective-permute-start(f32[512,128]{1,0:T(8,128)S(1)} %get-tuple-element.111.rest_4_), channel_id=1, source_target_pairs={{0,32},{32,0},{64,96},{96,64},{1,33},{33,1},{65,97},{97,65},{2,34}... | collective-permute-start | bytes 786440 | tf_op jit(solution)/shard_map/ppermute | solution.py:42
  57.1 13.0 %collective-permute-start.19 = (f32[512,128]{1,0:T(8,128)S(1)}, f32[512,128]{1,0:T(8,128)S(1)}, u32[]{:S(2)}, u32[]{:S(2)}) collective-permute-start(f32[512,128]{1,0:T(8,128)S(1)} %get-tuple-element.107.rest_0_.rest_5_), channel_id=1, source_target_pairs={{0,8},{8,0},{16,24},{24,16},{1,9},{9,1},{17,25},{25,17},{2,10},{10... | collective-permute-start | bytes 786440 | tf_op jit(solution)/shard_map/ppermute | solution.py:42
  57.4 12.7 %collective-permute-start.20 = (f32[512,128]{1,0:T(8,128)S(1)}, f32[512,128]{1,0:T(8,128)S(1)}, u32[]{:S(2)}, u32[]{:S(2)}) collective-permute-start(f32[512,128]{1,0:T(8,128)S(1)} %get-tuple-element.108.rest_1_.rest_6_), channel_id=1, source_target_pairs={{8,16},{16,8},{24,0},{0,24},{9,17},{17,9},{25,1},{1,25},{10,18},{1... | collective-permute-start | bytes 786440 | tf_op jit(solution)/shard_map/ppermute | solution.py:42
  58.0 12.1 %collective-permute-start.18 = (f32[512,128]{1,0:T(8,128)S(1)}, f32[512,128]{1,0:T(8,128)S(1)}, u32[]{:S(2)}, u32[]{:S(2)}) collective-permute-start(f32[512,128]{1,0:T(8,128)S(1)} %get-tuple-element.99.d1), channel_id=1, source_target_pairs={{32,64},{64,32},{96,0},{0,96},{33,65},{65,33},{97,1},{1,97},{34,66... | collective-permute-start | bytes 786440 | tf_op jit(solution)/shard_map/ppermute | solution.py:42
  61.8 4.1 %collective-permute-start.22 = (f32[256,128]{1,0:T(8,128)S(1)}, f32[256,128]{1,0:T(8,128)S(1)}, u32[]{:S(2)}, u32[]{:S(2)}) collective-permute-start(f32[256,128]{1,0:T(8,128)S(1)} %get-tuple-element.110.rest_3_.rest_8_), channel_id=1, source_target_pairs={{0,1},{1,0},{2,3},{3,2},{4,5},{5,4},{6,7},{7,6},{8,9},{9,8},{10,11... | collective-permute-start | bytes 393224 | tf_op jit(solution)/shard_map/ppermute | solution.py:42
  65.9 9.0 %collective-permute-start.24 = (f32[512,128]{1,0:T(8,128)S(1)}, f32[512,128]{1,0:T(8,128)S(1)}, u32[]{:S(2)}, u32[]{:S(2)}) collective-permute-start(f32[512,128]{1,0:T(8,128)S(1)} %get-tuple-element.114), channel_id=1, source_target_pairs={{32,64},{64,32},{96,0},{0,96},{33,65},{65,33},{97,1},{1,97},{34,66... | collective-permute-start | bytes 786440 | tf_op jit(solution)/shard_map/ppermute | solution.py:42
  70.8 14.0 %collective-permute-start.25 = (f32[544,128]{1,0:T(8,128)S(1)}, f32[544,128]{1,0:T(8,128)S(1)}, u32[]{:S(2)}, u32[]{:S(2)}) collective-permute-start(f32[544,128]{1,0:T(8,128)S(1)} %get-tuple-element.117.rest_9_), channel_id=1, source_target_pairs={{0,8},{8,0},{16,24},{24,16},{1,9},{9,1},{17,25},{25,17},{2,10},{10... | collective-permute-start | bytes 835592 | tf_op jit(solution)/shard_map/ppermute | solution.py:42
  71.2 13.6 %collective-permute-start.26 = (f32[544,128]{1,0:T(8,128)S(1)}, f32[544,128]{1,0:T(8,128)S(1)}, u32[]{:S(2)}, u32[]{:S(2)}) collective-permute-start(f32[544,128]{1,0:T(8,128)S(1)} %get-tuple-element.118.rest_10_), channel_id=1, source_target_pairs={{8,16},{16,8},{24,0},{0,24},{9,17},{17,9},{25,1},{1,25},{10,18},{1... | collective-permute-start | bytes 835592 | tf_op jit(solution)/shard_map/ppermute | solution.py:42
  73.0 11.7 %collective-permute-start.29 = (f32[512,128]{1,0:T(8,128)S(1)}, f32[512,128]{1,0:T(8,128)S(1)}, u32[]{:S(2)}, u32[]{:S(2)}) collective-permute-start(f32[512,128]{1,0:T(8,128)S(1)} %get-tuple-element.121), channel_id=1, source_target_pairs={{0,32},{32,0},{64,96},{96,64},{1,33},{33,1},{65,97},{97,65},{2,34}... | collective-permute-start | bytes 786440 | tf_op jit(solution)/shard_map/ppermute | solution.py:42
  73.0 6.8 %collective-permute-start.27 = (f32[272,128]{1,0:T(8,128)S(1)}, f32[272,128]{1,0:T(8,128)S(1)}, u32[]{:S(2)}, u32[]{:S(2)}) collective-permute-start(f32[272,128]{1,0:T(8,128)S(1)} %get-tuple-element.119.rest_11_), channel_id=1, source_target_pairs={{1,2},{2,1},{3,4},{4,3},{5,6},{6,5},{7,0},{0,7},{9,10},{10,9},{11,... | collective-permute-start | bytes 417800 | tf_op jit(solution)/shard_map/ppermute | solution.py:42
  74.9 9.9 %collective-permute-start.28 = (f32[272,128]{1,0:T(8,128)S(1)}, f32[272,128]{1,0:T(8,128)S(1)}, u32[]{:S(2)}, u32[]{:S(2)}) collective-permute-start(f32[272,128]{1,0:T(8,128)S(1)} %get-tuple-element.120.rest_12_), channel_id=1, source_target_pairs={{0,1},{1,0},{2,3},{3,2},{4,5},{5,4},{6,7},{7,6},{8,9},{9,8},{10,11... | collective-permute-start | bytes 417800 | tf_op jit(solution)/shard_map/ppermute | solution.py:42
  79.9 9.7 %collective-permute-start.30 = (f32[512,128]{1,0:T(8,128)S(1)}, f32[512,128]{1,0:T(8,128)S(1)}, u32[]{:S(2)}, u32[]{:S(2)}) collective-permute-start(f32[512,128]{1,0:T(8,128)S(1)} %get-tuple-element.123), channel_id=1, source_target_pairs={{32,64},{64,32},{96,0},{0,96},{33,65},{65,33},{97,1},{1,97},{34,66... | collective-permute-start | bytes 786440 | tf_op jit(solution)/shard_map/ppermute | solution.py:42
  85.5 8.7 %collective-permute-start.31 = (f32[576,128]{1,0:T(8,128)S(1)}, f32[576,128]{1,0:T(8,128)S(1)}, u32[]{:S(2)}, u32[]{:S(2)}) collective-permute-start(f32[576,128]{1,0:T(8,128)S(1)} %get-tuple-element.127.rest_13_), channel_id=1, source_target_pairs={{0,8},{8,0},{16,24},{24,16},{1,9},{9,1},{17,25},{25,17},{2,10},{10... | collective-permute-start | bytes 884744 | tf_op jit(solution)/shard_map/ppermute | solution.py:42
  86.3 10.0 %collective-permute-start.32 = (f32[576,128]{1,0:T(8,128)S(1)}, f32[576,128]{1,0:T(8,128)S(1)}, u32[]{:S(2)}, u32[]{:S(2)}) collective-permute-start(f32[576,128]{1,0:T(8,128)S(1)} %get-tuple-element.128.rest_14_), channel_id=1, source_target_pairs={{8,16},{16,8},{24,0},{0,24},{9,17},{17,9},{25,1},{1,25},{10,18},{1... | collective-permute-start | bytes 884744 | tf_op jit(solution)/shard_map/ppermute | solution.py:42
  87.2 7.0 %collective-permute-start.35 = (f32[512,128]{1,0:T(8,128)S(1)}, f32[512,128]{1,0:T(8,128)S(1)}, u32[]{:S(2)}, u32[]{:S(2)}) collective-permute-start(f32[512,128]{1,0:T(8,128)S(1)} %get-tuple-element.131), channel_id=1, source_target_pairs={{0,32},{32,0},{64,96},{96,64},{1,33},{33,1},{65,97},{97,65},{2,34}... | collective-permute-start | bytes 786440 | tf_op jit(solution)/shard_map/ppermute | solution.py:42
  87.2 7.0 %collective-permute-start.33 = (f32[288,128]{1,0:T(8,128)S(1)}, f32[288,128]{1,0:T(8,128)S(1)}, u32[]{:S(2)}, u32[]{:S(2)}) collective-permute-start(f32[288,128]{1,0:T(8,128)S(1)} %get-tuple-element.129.rest_15_), channel_id=1, source_target_pairs={{1,2},{2,1},{3,4},{4,3},{5,6},{6,5},{7,0},{0,7},{9,10},{10,9},{11,... | collective-permute-start | bytes 442376 | tf_op jit(solution)/shard_map/ppermute | solution.py:42
  89.6 4.6 %collective-permute-start.34 = (f32[288,128]{1,0:T(8,128)S(1)}, f32[288,128]{1,0:T(8,128)S(1)}, u32[]{:S(2)}, u32[]{:S(2)}) collective-permute-start(f32[288,128]{1,0:T(8,128)S(1)} %get-tuple-element.130.rest_16_), channel_id=1, source_target_pairs={{0,1},{1,0},{2,3},{3,2},{4,5},{5,4},{6,7},{7,6},{8,9},{9,8},{10,11... | collective-permute-start | bytes 442376 | tf_op jit(solution)/shard_map/ppermute | solution.py:42
